TPU v7x, 32 devices: a whole 2x2x4 slice. The times are simulated.
32 devices in a mesh: fsdp: 2 (over core), ctx: 4 (over y, x), tp: 4 (over z).
Axes of the slice: x: 2, y: 2, z: 4, core: 2. Of those that a mesh axis runs over, the one named last changes fastest.
Arguments:
- tokens_in: bfloat16 [4, 2048, 768], P(None, ('fsdp', 'ctx', 'tp')), may hold values from -6 to 6
- cotangent: bfloat16 [4, 2048, 768], P(None, ('fsdp', 'ctx', 'tp')), may hold values from -6 to 6
- seq_lengths: int32 [4, 2, 3], P(None, 'fsdp'), may hold values from 1 to 512, 1024 in all within a row
- row_order: int32 [4, 2, 1024], P(None, 'fsdp'), may hold values from 0 to 1023, each once within a row
- w_query: bfloat16 [768, 768], P(('fsdp', 'ctx'), 'tp'), may hold values from -0.3125 to 0.3125
- b_query: bfloat16 [12, 64], P('tp', ('fsdp', 'ctx')), may hold values from -3 to 3
- w_key: bfloat16 [768, 768], P(('fsdp', 'ctx'), 'tp'), may hold values from -0.3125 to 0.3125
- w_value: bfloat16 [768, 768], P(('fsdp', 'ctx'), 'tp'), may hold values from -0.21875 to 0.21875
- b_value: bfloat16 [12, 64], P('tp', ('fsdp', 'ctx')), may hold values from -3 to 3
- w_out: bfloat16 [768, 768], P(('fsdp', 'ctx'), 'tp'), may hold values from -1 to 1
- b_out: bfloat16 [768], P(('fsdp', 'ctx')), may hold values from -3 to 3
- mid_gain: bfloat16 [768], P(('fsdp', 'ctx')), may hold values from 0.099609375 to 1.8984375
- mid_shift: bfloat16 [768], P(('fsdp', 'ctx')), may hold values from -3 to 3
- w_up: bfloat16 [768, 3072], P(('fsdp', 'ctx'), 'tp'), may hold values from -0.21875 to 0.21875
- b_up: bfloat16 [12, 256], P('tp', ('fsdp', 'ctx')), may hold values from -3 to 3
- w_down: bfloat16 [768, 3072], P(('fsdp', 'ctx'), 'tp'), may hold values from -0.15625 to 0.15625
- b_down: bfloat16 [768], P(('fsdp', 'ctx')), may hold values from -3 to 3
- end_gain: bfloat16 [768], P(('fsdp', 'ctx')), may hold values from 0.099609375 to 1.8984375
- end_shift: bfloat16 [768], P(('fsdp', 'ctx')), may hold values from -3 to 3
Outputs:
- layer_out: bfloat16 [4, 2048, 768], P(None, ('fsdp', 'ctx', 'tp'))
- input_grad: bfloat16 [4, 2048, 768], P(None, ('fsdp', 'ctx', 'tp'))
- grad_w_query: float32 [768, 768], P(('fsdp', 'ctx'), 'tp')
- grad_b_query: float32 [12, 64], P('tp', ('fsdp', 'ctx'))
- grad_w_key: float32 [768, 768], P(('fsdp', 'ctx'), 'tp')
- grad_w_value: float32 [768, 768], P(('fsdp', 'ctx'), 'tp')
- grad_b_value: float32 [12, 64], P('tp', ('fsdp', 'ctx'))
- grad_w_out: float32 [768, 768], P(('fsdp', 'ctx'), 'tp')
- grad_b_out: float32 [768], P(('fsdp', 'ctx'))
- grad_mid_gain: float32 [768], P(('fsdp', 'ctx'))
- grad_mid_shift: float32 [768], P(('fsdp', 'ctx'))
- grad_w_up: float32 [768, 3072], P(('fsdp', 'ctx'), 'tp')
- grad_b_up: float32 [12, 256], P('tp', ('fsdp', 'ctx'))
- grad_w_down: float32 [768, 3072], P(('fsdp', 'ctx'), 'tp')
- grad_b_down: float32 [768], P(('fsdp', 'ctx'))
- grad_end_gain: float32 [768], P(('fsdp', 'ctx'))
- grad_end_shift: float32 [768], P(('fsdp', 'ctx'))
Inputs may be any that keep to these rules, and one draw needn't show every extreme that they name: `seq_lengths`: each row of 3 lengths sums to 1024, and its largest is exactly 512. `row_order`: each row holds every number of 0 to 1023 once.
All inputs are finite; a program needn't handle non-finite values.
Results may differ from a plain program's by a relative error of at most 0.02.
Values may be sent and summed in bfloat16 or wider, within the bound.
A program may use at most 128 MiB of HBM per device.

v0:
```python
import jax
import jax.numpy as jnp
from jax import lax
from jax.sharding import PartitionSpec as P

epsilon = 1e-06
masked_score = -1e30


def layer_norm(values, gain_vec, shift_vec):
    centre = values - jnp.mean(values, axis=-1, keepdims=True)
    spread = jnp.mean(centre * centre, axis=-1, keepdims=True)
    return centre * lax.rsqrt(spread + epsilon) * gain_vec + shift_vec


def gelu_exact(values):
    return jax.nn.gelu(values, approximate=False)


def dot_plain(former, latter):
    return jnp.dot(former, latter, preferred_element_type=jnp.float32)


def dot_right_t(former, latter):
    return lax.dot_general(
        former, latter, (((1,), (1,)), ((), ())), preferred_element_type=jnp.float32
    )


def dot_left_t(former, latter):
    return lax.dot_general(
        former, latter, (((0,), (0,)), ((), ())), preferred_element_type=jnp.float32
    )


def segment_ids(lengths, row_count):
    run_ends = jnp.cumsum(lengths)
    places = lax.iota(jnp.int32, row_count)
    return jnp.sum((run_ends[None, :] <= places[:, None]).astype(jnp.int32), axis=1)


def head_forward(queries, key_rows, value_rows, query_seg, key_seg, block_rows):
    total_rows, head_size = queries.shape
    blocks = total_rows // block_rows

    def one_block(pieces):
        query_block, seg_block = pieces
        scores = dot_right_t(query_block, key_rows) * 0.125
        scores = jnp.where(seg_block[:, None] == key_seg[None, :], scores, masked_score)
        top_score = jnp.max(scores, axis=1, keepdims=True)
        totals = jnp.sum(jnp.exp(scores - top_score), axis=1, keepdims=True)
        log_totals = top_score + jnp.log(totals)
        weights = jnp.exp(scores - log_totals).astype(jnp.bfloat16)
        return (dot_plain(weights, value_rows), log_totals[:, 0])

    attended, log_totals = lax.map(
        one_block,
        (queries.reshape(blocks, block_rows, head_size), query_seg.reshape(blocks, block_rows)),
    )
    return (attended.reshape(total_rows, head_size), log_totals.reshape(total_rows))


def head_backward(
    queries, key_rows, value_rows, grad_rows, log_totals, query_seg, key_seg, block_rows
):
    total_rows, head_size = queries.shape
    blocks = total_rows // block_rows

    def one_block(running, pieces):
        key_grad, value_grad = running
        query_block, grad_block, total_block, seg_block = pieces
        scores = dot_right_t(query_block, key_rows) * 0.125
        scores = jnp.where(seg_block[:, None] == key_seg[None, :], scores, masked_score)
        weights = jnp.exp(scores - total_block[:, None])
        weight_grad = dot_right_t(grad_block, value_rows)
        row_inner = jnp.sum(weights * weight_grad, axis=1, keepdims=True)
        score_grad = (weights * (weight_grad - row_inner)).astype(jnp.bfloat16)
        query_grad = dot_plain(score_grad, key_rows) * 0.125
        key_grad = key_grad + dot_left_t(score_grad, query_block) * 0.125
        value_grad = value_grad + dot_left_t(weights.astype(jnp.bfloat16), grad_block)
        return ((key_grad, value_grad), query_grad)

    initial = (jnp.zeros(key_rows.shape, jnp.float32), jnp.zeros(key_rows.shape, jnp.float32))
    pieces = (
        queries.reshape(blocks, block_rows, head_size),
        grad_rows.reshape(blocks, block_rows, head_size),
        log_totals.reshape(blocks, block_rows),
        query_seg.reshape(blocks, block_rows),
    )
    (key_grad, value_grad), query_grad = lax.scan(one_block, initial, pieces)
    return (query_grad.reshape(total_rows, head_size), key_grad, value_grad)


def unpack(gathered):
    return {
        "query_w": gathered[0],
        "query_b": gathered[1].astype(jnp.float32).reshape(-1),
        "key_w": gathered[2],
        "value_w": gathered[3],
        "value_b": gathered[4].astype(jnp.float32).reshape(-1),
        "out_w": gathered[5],
        "out_b": gathered[6].astype(jnp.float32),
        "gain_mid": gathered[7].astype(jnp.float32),
        "shift_mid": gathered[8].astype(jnp.float32),
        "up_w": gathered[9],
        "up_b": gathered[10].astype(jnp.float32).reshape(-1),
        "down_w": gathered[11],
        "down_b": gathered[12].astype(jnp.float32),
        "gain_end": gathered[13].astype(jnp.float32),
        "shift_end": gathered[14].astype(jnp.float32),
        "head_size": gathered[1].shape[1],
        "bias_rows": gathered[1].shape[0],
        "up_shape": gathered[10].shape,
    }


def reduce_grads(local):
    summed = lax.psum((local[6], local[7], local[8], local[12], local[13], local[14]), "tp")
    return (
        lax.psum_scatter(local[0], ("fsdp", "ctx"), scatter_dimension=0, tiled=True),
        lax.psum_scatter(local[1], ("fsdp", "ctx"), scatter_dimension=1, tiled=True),
        lax.psum_scatter(local[2], ("fsdp", "ctx"), scatter_dimension=0, tiled=True),
        lax.psum_scatter(local[3], ("fsdp", "ctx"), scatter_dimension=0, tiled=True),
        lax.psum_scatter(local[4], ("fsdp", "ctx"), scatter_dimension=1, tiled=True),
        lax.psum_scatter(local[5], ("fsdp", "ctx"), scatter_dimension=0, tiled=True),
        lax.psum_scatter(summed[0], ("fsdp", "ctx"), scatter_dimension=0, tiled=True),
        lax.psum_scatter(summed[1], ("fsdp", "ctx"), scatter_dimension=0, tiled=True),
        lax.psum_scatter(summed[2], ("fsdp", "ctx"), scatter_dimension=0, tiled=True),
        lax.psum_scatter(local[9], ("fsdp", "ctx"), scatter_dimension=0, tiled=True),
        lax.psum_scatter(local[10], ("fsdp", "ctx"), scatter_dimension=1, tiled=True),
        lax.psum_scatter(local[11], ("fsdp", "ctx"), scatter_dimension=0, tiled=True),
        lax.psum_scatter(summed[3], ("fsdp", "ctx"), scatter_dimension=0, tiled=True),
        lax.psum_scatter(summed[4], ("fsdp", "ctx"), scatter_dimension=0, tiled=True),
        lax.psum_scatter(summed[5], ("fsdp", "ctx"), scatter_dimension=0, tiled=True),
    )


def add_tuples(former, latter):
    if former is None:
        return latter
    return tuple((first_term + second_term for first_term, second_term in zip(former, latter)))


def body(
    tokens_in,
    cotangent,
    seq_lengths,
    row_order,
    w_query,
    b_query,
    w_key,
    w_value,
    b_value,
    w_out,
    b_out,
    mid_gain,
    mid_shift,
    w_up,
    b_up,
    w_down,
    b_down,
    end_gain,
    end_shift,
):
    ctx_count = lax.axis_size("ctx")
    tp_count = lax.axis_size("tp")
    ctx_index = lax.axis_index("ctx")
    tp_index = lax.axis_index("tp")
    micro_count, own_rows, model_width = tokens_in.shape
    tok_rows = own_rows * tp_count
    group_rows = tok_rows * ctx_count
    block_rows = min(512, tok_rows)
    natural_rows = (ctx_index * tp_count + tp_index) * own_rows + lax.iota(jnp.int32, own_rows)
    query_start = ctx_index * tok_rows
    owned_sum = None
    layer_rows = []
    input_rows = []
    for batch_index in range(micro_count):
        row_perm = row_order[batch_index, 0]
        seg_natural = segment_ids(seq_lengths[batch_index, 0], group_rows)
        seg_perm = jnp.take(seg_natural, row_perm)
        query_seg = lax.dynamic_slice_in_dim(seg_perm, query_start, tok_rows, 0)
        inverse = (
            jnp.zeros((group_rows,), jnp.int32).at[row_perm].set(lax.iota(jnp.int32, group_rows))
        )
        x_group = lax.all_gather(tokens_in[batch_index], ("ctx", "tp"), axis=0, tiled=True)
        x_perm = jnp.take(x_group, row_perm, axis=0)
        x_query = lax.dynamic_slice_in_dim(x_perm, query_start, tok_rows, 0)
        x_own = lax.dynamic_slice_in_dim(x_query, tp_index * own_rows, own_rows, 0).astype(
            jnp.float32
        )
        fwd = unpack(
            (
                lax.all_gather(w_query, ("fsdp", "ctx"), axis=0, tiled=True),
                lax.all_gather(b_query, ("fsdp", "ctx"), axis=1, tiled=True),
                lax.all_gather(w_key, ("fsdp", "ctx"), axis=0, tiled=True),
                lax.all_gather(w_value, ("fsdp", "ctx"), axis=0, tiled=True),
                lax.all_gather(b_value, ("fsdp", "ctx"), axis=1, tiled=True),
                lax.all_gather(w_out, ("fsdp", "ctx"), axis=0, tiled=True),
                lax.all_gather(b_out, ("fsdp", "ctx"), axis=0, tiled=True),
                lax.all_gather(mid_gain, ("fsdp", "ctx"), axis=0, tiled=True),
                lax.all_gather(mid_shift, ("fsdp", "ctx"), axis=0, tiled=True),
                lax.all_gather(w_up, ("fsdp", "ctx"), axis=0, tiled=True),
                lax.all_gather(b_up, ("fsdp", "ctx"), axis=1, tiled=True),
                lax.all_gather(w_down, ("fsdp", "ctx"), axis=0, tiled=True),
                lax.all_gather(b_down, ("fsdp", "ctx"), axis=0, tiled=True),
                lax.all_gather(end_gain, ("fsdp", "ctx"), axis=0, tiled=True),
                lax.all_gather(end_shift, ("fsdp", "ctx"), axis=0, tiled=True),
            )
        )
        head_size = fwd["head_size"]
        local_heads = fwd["query_w"].shape[1] // head_size
        queries = (dot_plain(x_query, fwd["query_w"]) + fwd["query_b"]).astype(jnp.bfloat16)
        key_rows = dot_plain(x_perm, fwd["key_w"]).astype(jnp.bfloat16)
        value_rows = (dot_plain(x_perm, fwd["value_w"]) + fwd["value_b"]).astype(jnp.bfloat16)
        head_outs = []
        head_totals = []
        for head_index in range(local_heads):
            cols = slice(head_index * head_size, (head_index + 1) * head_size)
            head_out, head_total = head_forward(
                queries[:, cols],
                key_rows[:, cols],
                value_rows[:, cols],
                query_seg,
                seg_perm,
                block_rows,
            )
            head_outs.append(head_out)
            head_totals.append(head_total)
        attended = jnp.concatenate(head_outs, axis=1).astype(jnp.bfloat16)
        attn_own = lax.psum_scatter(
            dot_right_t(attended, fwd["out_w"]), "tp", scatter_dimension=0, tiled=True
        )
        mid_in = x_own + attn_own + fwd["out_b"]
        middle, mid_back = jax.vjp(layer_norm, mid_in, fwd["gain_mid"], fwd["shift_mid"])
        mid_full = lax.all_gather(middle.astype(jnp.bfloat16), "tp", axis=0, tiled=True)
        pre_act = dot_plain(mid_full, fwd["up_w"]) + fwd["up_b"]
        activated = gelu_exact(pre_act).astype(jnp.bfloat16)
        ffn_own = lax.psum_scatter(
            dot_right_t(activated, fwd["down_w"]).astype(jnp.bfloat16),
            "tp",
            scatter_dimension=0,
            tiled=True,
        ).astype(jnp.float32)
        end_in = middle + ffn_own + fwd["down_b"]
        out_value, end_back = jax.vjp(layer_norm, end_in, fwd["gain_end"], fwd["shift_end"])
        layer_rows.append(out_value.astype(jnp.bfloat16))
        bwd = unpack(
            (
                lax.all_gather(w_query, ("fsdp", "ctx"), axis=0, tiled=True),
                lax.all_gather(b_query, ("fsdp", "ctx"), axis=1, tiled=True),
                lax.all_gather(w_key, ("fsdp", "ctx"), axis=0, tiled=True),
                lax.all_gather(w_value, ("fsdp", "ctx"), axis=0, tiled=True),
                lax.all_gather(b_value, ("fsdp", "ctx"), axis=1, tiled=True),
                lax.all_gather(w_out, ("fsdp", "ctx"), axis=0, tiled=True),
                lax.all_gather(b_out, ("fsdp", "ctx"), axis=0, tiled=True),
                lax.all_gather(mid_gain, ("fsdp", "ctx"), axis=0, tiled=True),
                lax.all_gather(mid_shift, ("fsdp", "ctx"), axis=0, tiled=True),
                lax.all_gather(w_up, ("fsdp", "ctx"), axis=0, tiled=True),
                lax.all_gather(b_up, ("fsdp", "ctx"), axis=1, tiled=True),
                lax.all_gather(w_down, ("fsdp", "ctx"), axis=0, tiled=True),
                lax.all_gather(b_down, ("fsdp", "ctx"), axis=0, tiled=True),
                lax.all_gather(end_gain, ("fsdp", "ctx"), axis=0, tiled=True),
                lax.all_gather(end_shift, ("fsdp", "ctx"), axis=0, tiled=True),
            )
        )
        d_end, grad_gain_end, grad_shift_end = end_back(cotangent[batch_index].astype(jnp.float32))
        grad_down_b = jnp.sum(d_end, axis=0)
        d_f_full = lax.all_gather(d_end.astype(jnp.bfloat16), "tp", axis=0, tiled=True)
        d_act = dot_plain(d_f_full, bwd["down_w"])
        gelu_back = jax.vjp(gelu_exact, pre_act)[1]
        d_pre = gelu_back(d_act)[0].astype(jnp.bfloat16)
        grad_down_w = dot_left_t(d_f_full, activated)
        grad_up_w = dot_left_t(mid_full, d_pre)
        grad_up_b = jnp.sum(d_pre.astype(jnp.float32), axis=0).reshape(bwd["up_shape"])
        d_mid = d_end + lax.psum_scatter(
            dot_right_t(d_pre, bwd["up_w"]), "tp", scatter_dimension=0, tiled=True
        )
        d_mid_in, grad_gain_mid, grad_shift_mid = mid_back(d_mid)
        grad_out_b = jnp.sum(d_mid_in, axis=0)
        d_a_full = lax.all_gather(d_mid_in.astype(jnp.bfloat16), "tp", axis=0, tiled=True)
        d_attended = dot_plain(d_a_full, bwd["out_w"]).astype(jnp.bfloat16)
        grad_out_w = dot_left_t(d_a_full, attended)
        query_grads = []
        key_grads = []
        value_grads = []
        for head_index in range(local_heads):
            cols = slice(head_index * head_size, (head_index + 1) * head_size)
            query_grad, key_grad, value_grad = head_backward(
                queries[:, cols],
                key_rows[:, cols],
                value_rows[:, cols],
                d_attended[:, cols],
                head_totals[head_index],
                query_seg,
                seg_perm,
                block_rows,
            )
            query_grads.append(query_grad)
            key_grads.append(key_grad)
            value_grads.append(value_grad)
        d_query = jnp.concatenate(query_grads, axis=1).astype(jnp.bfloat16)
        key_part = jnp.concatenate(key_grads, axis=1)
        value_part = jnp.concatenate(value_grads, axis=1)
        key_sum, value_sum = (
            lax.psum_scatter(
                key_part.astype(jnp.bfloat16), "ctx", scatter_dimension=0, tiled=True
            ).astype(jnp.float32),
            lax.psum_scatter(
                value_part.astype(jnp.bfloat16), "ctx", scatter_dimension=0, tiled=True
            ).astype(jnp.float32),
        )
        d_keys = key_sum.astype(jnp.bfloat16)
        d_values = value_sum.astype(jnp.bfloat16)
        grad_query_w = dot_left_t(x_query, d_query)
        grad_query_b = jnp.sum(d_query.astype(jnp.float32), axis=0).reshape(
            bwd["bias_rows"], head_size
        )
        grad_key_w = dot_left_t(x_query, d_keys)
        grad_value_w = dot_left_t(x_query, d_values)
        grad_value_b = jnp.sum(d_values.astype(jnp.float32), axis=0).reshape(
            bwd["bias_rows"], head_size
        )
        d_x = (
            d_mid_in
            + lax.psum_scatter(
                (
                    dot_right_t(d_query, bwd["query_w"])
                    + dot_right_t(d_keys, bwd["key_w"])
                    + dot_right_t(d_values, bwd["value_w"])
                ).astype(jnp.bfloat16),
                "tp",
                scatter_dimension=0,
                tiled=True,
            ).astype(jnp.float32)
        ).astype(jnp.bfloat16)
        d_group = lax.all_gather(d_x, ("ctx", "tp"), axis=0, tiled=True)
        input_rows.append(jnp.take(d_group, jnp.take(inverse, natural_rows), axis=0))
        local_grads = (
            grad_query_w,
            grad_query_b,
            grad_key_w,
            grad_value_w,
            grad_value_b,
            grad_out_w,
            grad_out_b,
            grad_gain_mid,
            grad_shift_mid,
            grad_up_w,
            grad_up_b,
            grad_down_w,
            grad_down_b,
            grad_gain_end,
            grad_shift_end,
        )
        owned_sum = add_tuples(owned_sum, reduce_grads(local_grads))
    return (
        jnp.stack(layer_rows),
        jnp.stack(input_rows),
        owned_sum[0],
        owned_sum[1],
        owned_sum[2],
        owned_sum[3],
        owned_sum[4],
        owned_sum[5],
        owned_sum[6],
        owned_sum[7],
        owned_sum[8],
        owned_sum[9],
        owned_sum[10],
        owned_sum[11],
        owned_sum[12],
        owned_sum[13],
        owned_sum[14],
    )


def solution(mesh):
    return jax.shard_map(
        body,
        mesh=mesh,
        in_specs=(
            P(None, ("fsdp", "ctx", "tp"), None),
            P(None, ("fsdp", "ctx", "tp"), None),
            P(None, "fsdp", None),
            P(None, "fsdp", None),
            P(("fsdp", "ctx"), "tp"),
            P("tp", ("fsdp", "ctx")),
            P(("fsdp", "ctx"), "tp"),
            P(("fsdp", "ctx"), "tp"),
            P("tp", ("fsdp", "ctx")),
            P(("fsdp", "ctx"), "tp"),
            P(("fsdp", "ctx")),
            P(("fsdp", "ctx")),
            P(("fsdp", "ctx")),
            P(("fsdp", "ctx"), "tp"),
            P("tp", ("fsdp", "ctx")),
            P(("fsdp", "ctx"), "tp"),
            P(("fsdp", "ctx")),
            P(("fsdp", "ctx")),
            P(("fsdp", "ctx")),
        ),
        out_specs=(
            P(None, ("fsdp", "ctx", "tp"), None),
            P(None, ("fsdp", "ctx", "tp"), None),
            P(("fsdp", "ctx"), "tp"),
            P("tp", ("fsdp", "ctx")),
            P(("fsdp", "ctx"), "tp"),
            P(("fsdp", "ctx"), "tp"),
            P("tp", ("fsdp", "ctx")),
            P(("fsdp", "ctx"), "tp"),
            P(("fsdp", "ctx")),
            P(("fsdp", "ctx")),
            P(("fsdp", "ctx")),
            P(("fsdp", "ctx"), "tp"),
            P("tp", ("fsdp", "ctx")),
            P(("fsdp", "ctx"), "tp"),
            P(("fsdp", "ctx")),
            P(("fsdp", "ctx")),
            P(("fsdp", "ctx")),
        ),
        check_vma=False,
    )
```

profile of v0, /device:TPU:0, one launch (start us, length us, event | category | flops | bytes accessed | tf_op | source)
XLA Modules:
  0.0 1329.2 jit_solution(17265984445672718291)
XLA Ops:
  12.0 26.0 %all_gather.76 = bf16[768,192]{1,0:T(8,128)(2,1)S(1)} all-gather(bf16[96,192]{1,0:T(8,128)(2,1)} %param.36), channel_id=1, replica_groups=mesh['fsdp'=2,'ctx'=4,'tp'=4] {'fsdp','ctx'}, dimensions={0}, use_global_device_ids=true | all-gather | bytes 331776 | tf_op jit(solution)/shard_map/all_gather | solution.py:199
  43.2 25.4 %all_gather.74 = bf16[768,192]{1,0:T(8,128)(2,1)S(1)} all-gather(bf16[96,192]{1,0:T(8,128)(2,1)S(1)} %copy-done.211), channel_id=1, replica_groups=mesh['fsdp'=2,'ctx'=4,'tp'=4] {'fsdp','ctx'}, dimensions={0}, use_global_device_ids=true | all-gather | bytes 331776 | tf_op jit(solution)/shard_map/all_gather | solution.py:197
  68.7 14.4 %all-gather.5 = bf16[8,8,3]{1,2,0:T(4,128)(2,1)S(1)} all-gather(bf16[1,8,3]{1,2,0:T(4,128)(2,1)S(1)} %bitcast.295), channel_id=1, replica_groups=mesh['fsdp'=2,'ctx'=4,'tp'=4] {'fsdp','ctx'}, dimensions={0}, use_global_device_ids=true | all-gather | bytes 432 | tf_op jit(solution)/shard_map/all_gather | solution.py:198
  83.2 26.5 %all_gather.73 = bf16[768,192]{1,0:T(8,128)(2,1)S(1)} all-gather(bf16[96,192]{1,0:T(8,128)(2,1)S(1)} %copy-done.212), channel_id=1, replica_groups=mesh['fsdp'=2,'ctx'=4,'tp'=4] {'fsdp','ctx'}, dimensions={0}, use_global_device_ids=true | all-gather | bytes 331776 | tf_op jit(solution)/shard_map/all_gather | solution.py:196
  109.7 25.9 %all_gather.71 = bf16[768,192]{1,0:T(8,128)(2,1)S(1)} all-gather(bf16[96,192]{1,0:T(8,128)(2,1)S(1)} %copy-done.213), channel_id=1, replica_groups=mesh['fsdp'=2,'ctx'=4,'tp'=4] {'fsdp','ctx'}, dimensions={0}, use_global_device_ids=true | all-gather | bytes 331776 | tf_op jit(solution)/shard_map/all_gather | solution.py:194
  182.9 15.4 %all-gather.34.cloned.1.call-done = bf16[1,1024,768]{2,1,0:T(8,128)(2,1)} async-done(((bf16[1,64,768]{2,1,0:T(8,128)(2,1)}), bf16[1,1024,768]{2,1,0:T(8,128)(2,1)}) %all-gather.34.cloned.1.call-update) | async-done | bytes 1572880 | tf_op jit(solution)/shard_map/all_gather | solution.py:186
  219.8 38.4 %all-gather.36.cloned.1.call-done = bf16[1,1024,768]{2,1,0:T(8,128)(2,1)} async-done(((bf16[1,64,768]{2,1,0:T(8,128)(2,1)}), bf16[1,1024,768]{2,1,0:T(8,128)(2,1)}) %all-gather.36.cloned.1.call-update) | async-done | bytes 1572880 | tf_op jit(solution)/shard_map/all_gather | solution.py:186
  325.4 26.7 %all-reduce.16 = (bf16[768]{0:T(1024)(128)(2,1)S(1)}, bf16[768]{0:T(1024)(128)(2,1)S(1)}, bf16[768]{0:T(1024)(128)(2,1)S(1)}, bf16[768]{0:T(1024)(128)(2,1)}, bf...) all-reduce(bf16[768]{0:T(1024)(128)(2,1)S(1)} %dynamic-update-slice, ...), channel_id=1, replica_groups=mesh['fsdp'=2,'ctx'=4,'tp'=4] {'fsdp','ctx'}, use_global_device_ids=true, to_apply=%add | all-reduce | flops 4608 | bytes 18432
  352.2 19.1 %reduce-scatter.48.cloned.1.call-done = f32[64,768]{1,0:T(8,128)} async-done(((f32[256,768]{1,0:T(8,128)}), f32[64,768]{1,0:T(8,128)}) %reduce-scatter.48.cloned.1.call-update) | async-done | bytes 196624 | tf_op jit(solution)/shard_map/reduce_scatter | solution.py:231
  375.2 15.7 %all_gather.80 = bf16[256,768]{1,0:T(8,128)(2,1)} all-gather(bf16[64,768]{1,0:T(8,128)(2,1)S(1)} %get-tuple-element.828), channel_id=1, replica_groups=mesh['fsdp'=2,'ctx'=4,'tp'=4] {'tp'}, dimensions={0}, use_global_device_ids=true | all-gather | bytes 491520 | tf_op jit(solution)/shard_map/all_gather | solution.py:236
  398.3 17.0 %all_gather.88 = bf16[256,768]{1,0:T(8,128)(2,1)S(1)} all-gather(bf16[64,768]{1,0:T(8,128)(2,1)} %get-tuple-element.829), channel_id=1, replica_groups=mesh['fsdp'=2,'ctx'=4,'tp'=4] {'tp'}, dimensions={0}, use_global_device_ids=true | all-gather | bytes 491520 | tf_op jit(solution)/shard_map/all_gather | solution.py:236
  415.3 15.5 %all_gather.90 = bf16[256,768]{1,0:T(8,128)(2,1)} all-gather(bf16[64,768]{1,0:T(8,128)(2,1)S(1)} %get-tuple-element.830), channel_id=1, replica_groups=mesh['fsdp'=2,'ctx'=4,'tp'=4] {'tp'}, dimensions={0}, use_global_device_ids=true | all-gather | bytes 491520 | tf_op jit(solution)/shard_map/all_gather | solution.py:236
  458.1 21.4 %reduce-scatter.46.cloned.1.call-done = bf16[64,768]{1,0:T(8,128)(2,1)} async-done(((bf16[256,768]{1,0:T(8,128)(2,1)}), bf16[64,768]{1,0:T(8,128)(2,1)}) %reduce-scatter.46.cloned.1.call-update) | async-done | bytes 98320 | tf_op jit(solution)/shard_map/reduce_scatter | solution.py:239
  505.2 15.8 %reduce-scatter.50.cloned.1.call-done = bf16[64,768]{1,0:T(8,128)(2,1)} async-done(((bf16[256,768]{1,0:T(8,128)(2,1)}), bf16[64,768]{1,0:T(8,128)(2,1)}) %reduce-scatter.50.cloned.1.call-update) | async-done | bytes 98320 | tf_op jit(solution)/shard_map/reduce_scatter | solution.py:239
  547.2 16.9 %all_gather.102 = bf16[256,768]{1,0:T(8,128)(2,1)S(1)} all-gather(bf16[64,768]{1,0:T(8,128)(2,1)S(1)} %get-tuple-element.784), channel_id=1, replica_groups=mesh['fsdp'=2,'ctx'=4,'tp'=4] {'tp'}, dimensions={0}, use_global_device_ids=true | all-gather | bytes 491520 | tf_op jit(solution)/shard_map/all_gather | solution.py:269
  571.2 16.4 %all_gather.93 = bf16[256,768]{1,0:T(8,128)(2,1)S(1)} all-gather(bf16[64,768]{1,0:T(8,128)(2,1)S(1)} %get-tuple-element.780), channel_id=1, replica_groups=mesh['fsdp'=2,'ctx'=4,'tp'=4] {'tp'}, dimensions={0}, use_global_device_ids=true | all-gather | bytes 491520 | tf_op jit(solution)/shard_map/all_gather | solution.py:269
  624.4 24.9 %reduce-scatter.68.cloned.1.call-done = f32[64,768]{1,0:T(8,128)} async-done(((f32[256,768]{1,0:T(8,128)}), f32[64,768]{1,0:T(8,128)}) %reduce-scatter.68.cloned.1.call-update) | async-done | bytes 196624 | tf_op jit(solution)/shard_map/reduce_scatter | solution.py:276
  652.2 15.3 %all_gather.103 = bf16[256,768]{1,0:T(8,128)(2,1)S(1)} all-gather(bf16[64,768]{1,0:T(8,128)(2,1)S(1)} %get-tuple-element.803), channel_id=1, replica_groups=mesh['fsdp'=2,'ctx'=4,'tp'=4] {'tp'}, dimensions={0}, use_global_device_ids=true | all-gather | bytes 491520 | tf_op jit(solution)/shard_map/all_gather | solution.py:281
  680.4 14.4 %all_gather.100 = bf16[256,768]{1,0:T(8,128)(2,1)S(1)} all-gather(bf16[64,768]{1,0:T(8,128)(2,1)S(1)} %get-tuple-element.790), channel_id=1, replica_groups=mesh['fsdp'=2,'ctx'=4,'tp'=4] {'tp'}, dimensions={0}, use_global_device_ids=true | all-gather | bytes 491520 | tf_op jit(solution)/shard_map/all_gather | solution.py:281
  821.3 17.6 %reduce-scatter.72.cloned.1.call-done = bf16[256,192]{0,1:T(8,128)(2,1)} async-done(((bf16[1024,192]{0,1:T(8,128)(2,1)}), bf16[256,192]{0,1:T(8,128)(2,1)}) %reduce-scatter.72.cloned.1.call-update) | async-done | bytes 98320 | tf_op jit(solution)/shard_map/reduce_scatter | solution.py:309
  841.8 24.4 %reduce-scatter.62.cloned.1.call-done = bf16[256,192]{0,1:T(8,128)(2,1)} async-done(((bf16[1024,192]{0,1:T(8,128)(2,1)}), bf16[256,192]{0,1:T(8,128)(2,1)}) %reduce-scatter.62.cloned.1.call-update) | async-done | bytes 98320 | tf_op jit(solution)/shard_map/reduce_scatter | solution.py:306
  867.7 25.9 %reduce-scatter.64.cloned.1.call-done = bf16[256,192]{0,1:T(8,128)(2,1)} async-done(((bf16[1024,192]{0,1:T(8,128)(2,1)}), bf16[256,192]{0,1:T(8,128)(2,1)}) %reduce-scatter.64.cloned.1.call-update) | async-done | bytes 98320 | tf_op jit(solution)/shard_map/reduce_scatter | solution.py:309
  895.9 25.0 %reduce-scatter.54.cloned.1.call-done = bf16[256,192]{0,1:T(8,128)(2,1)} async-done(((bf16[1024,192]{0,1:T(8,128)(2,1)}), bf16[256,192]{0,1:T(8,128)(2,1)}) %reduce-scatter.54.cloned.1.call-update) | async-done | bytes 98320 | tf_op jit(solution)/shard_map/reduce_scatter | solution.py:306
  922.2 26.2 %reduce-scatter.56.cloned.1.call-done = bf16[256,192]{0,1:T(8,128)(2,1)} async-done(((bf16[1024,192]{0,1:T(8,128)(2,1)}), bf16[256,192]{0,1:T(8,128)(2,1)}) %reduce-scatter.56.cloned.1.call-update) | async-done | bytes 98320 | tf_op jit(solution)/shard_map/reduce_scatter | solution.py:309
  951.5 20.5 %reduce-scatter.82.cloned.1.call-done = bf16[64,768]{1,0:T(8,128)(2,1)} async-done(((bf16[256,768]{1,0:T(8,128)(2,1)}), bf16[64,768]{1,0:T(8,128)(2,1)}) %reduce-scatter.82.cloned.1.call-update) | async-done | bytes 98320 | tf_op jit(solution)/shard_map/reduce_scatter | solution.py:326
  973.6 19.7 %reduce-scatter.74.cloned.1.call-done = bf16[64,768]{1,0:T(8,128)(2,1)} async-done(((bf16[256,768]{1,0:T(8,128)(2,1)}), bf16[64,768]{1,0:T(8,128)(2,1)}) %reduce-scatter.74.cloned.1.call-update) | async-done | bytes 98320 | tf_op jit(solution)/shard_map/reduce_scatter | solution.py:326
  995.0 20.0 %reduce-scatter.66.cloned.1.call-done = bf16[64,768]{1,0:T(8,128)(2,1)} async-done(((bf16[256,768]{1,0:T(8,128)(2,1)}), bf16[64,768]{1,0:T(8,128)(2,1)}) %reduce-scatter.66.cloned.1.call-update) | async-done | bytes 98320 | tf_op jit(solution)/shard_map/reduce_scatter | solution.py:326
  1016.7 20.5 %reduce-scatter.58.cloned.1.call-done = bf16[64,768]{1,0:T(8,128)(2,1)} async-done(((bf16[256,768]{1,0:T(8,128)(2,1)}), bf16[64,768]{1,0:T(8,128)(2,1)}) %reduce-scatter.58.cloned.1.call-update) | async-done | bytes 98320 | tf_op jit(solution)/shard_map/reduce_scatter | solution.py:326
  1097.3 26.4 %all-reduce.14 = (f32[3,64]{1,0:T(4,128)S(1)}, f32[3,64]{1,0:T(4,128)S(1)}, f32[768]{0:T(1024)S(1)}, f32[768]{0:T(1024)S(1)}, f32[768]{0:T(1024)S(1)}, /*index=5...) all-reduce(f32[3,64]{1,0:T(4,128)S(1)} %reshape.1120, ...), channel_id=76, replica_groups=mesh['fsdp'=2,'ctx'=4,'tp'=4] {'fsdp','ctx'}, use_global_device_ids=true, to_apply=%region_109.114.clone | all-reduce | flops 4992 | bytes 39936
  1156.8 57.1 %all-gather.22.cloned.1.call-done = bf16[1024,768]{1,0:T(8,128)(2,1)} async-done(((bf16[64,768]{1,0:T(8,128)(2,1)}), bf16[1024,768]{1,0:T(8,128)(2,1)}) %all-gather.22.cloned.1.call-update) | async-done | bytes 1572880 | tf_op jit(solution)/shard_map/all_gather | solution.py:337
  1229.1 46.2 %reduce-scatter.92.cloned.1.call-done = f32[96,768]{1,0:T(8,128)} async-done(((f32[768,768]{1,0:T(8,128)}), f32[96,768]{1,0:T(8,128)}) %reduce-scatter.92.cloned.1.call-update) | async-done | bytes 294928 | tf_op jit(solution)/shard_map/reduce_scatter | solution.py:129
  1275.3 46.0 %reduce-scatter.94.cloned.1.call-done = f32[96,768]{1,0:T(8,128)} async-done(((f32[768,768]{1,0:T(8,128)}), f32[96,768]{1,0:T(8,128)}) %reduce-scatter.94.cloned.1.call-update) | async-done | bytes 294928 | tf_op jit(solution)/shard_map/reduce_scatter | solution.py:131
  (1071 shorter events, 540.3 us)
Async XLA Ops:
  8.0 154.9 %all-gather.30.cloned.1.call-start = ((), (), s32[]{:S(2)}) async-start(), calls=%async_computation.61 | async-start | bytes 1671168 | tf_op jit(solution)/shard_map/all_gather | solution.py:186
  9.9 160.3 %all-gather.32.cloned.1.call-start = ((), (), s32[]{:S(2)}) async-start(), calls=%async_computation.62 | async-start | bytes 1671168 | tf_op jit(solution)/shard_map/all_gather | solution.py:186
  10.6 187.6 %all-gather.34.cloned.1.call-start = ((), (), s32[]{:S(2)}) async-start(), calls=%async_computation.63 | async-start | bytes 1671168 | tf_op jit(solution)/shard_map/all_gather | solution.py:186
  11.4 246.9 %all-gather.36.cloned.1.call-start = ((), (), s32[]{:S(2)}) async-start(), calls=%async_computation.64 | async-start | bytes 1671168 | tf_op jit(solution)/shard_map/all_gather | solution.py:186
  12.0 340.2 %reduce-scatter.36.cloned.1.call-start = ((), (), s32[]{:S(2)}) async-start(), calls=%async_computation.31 | async-start | bytes 983040 | tf_op jit(solution)/shard_map/reduce_scatter | solution.py:231
  274.3 77.8 %reduce-scatter.40.cloned.1.call-start = ((), (), s32[]{:S(2)}) async-start(), calls=%async_computation.35 | async-start | bytes 983040 | tf_op jit(solution)/shard_map/reduce_scatter | solution.py:231
  307.4 83.5 %all-gather.18.cloned.1.call-start = ((), (), s32[]{:S(2)}) async-start(), calls=%async_computation.32 | async-start | bytes 1327104 | tf_op jit(solution)/shard_map/all_gather | solution.py:203
  308.0 87.6 %all-gather.20.cloned.1.call-start = ((), (), s32[]{:S(2)}) async-start(), calls=%async_computation.33 | async-start | bytes 1327104 | tf_op jit(solution)/shard_map/all_gather | solution.py:205
  308.6 135.8 %reduce-scatter.38.cloned.1.call-start = ((), (), s32[]{:S(2)}) async-start(), calls=%async_computation.34 | async-start | bytes 491520 | tf_op jit(solution)/shard_map/reduce_scatter | solution.py:239
  444.1 76.9 %reduce-scatter.50.cloned.1.call-start = ((), (), s32[]{:S(2)}) async-start(), calls=%async_computation.40 | async-start | bytes 491520 | tf_op jit(solution)/shard_map/reduce_scatter | solution.py:239
  501.3 113.0 %reduce-scatter.60.cloned.1.call-start = ((), (), s32[]{:S(2)}) async-start(), calls=%async_computation.46 | async-start | bytes 983040 | tf_op jit(solution)/shard_map/reduce_scatter | solution.py:276
  614.2 198.6 %reduce-scatter.78.cloned.1.call-start = ((), (), s32[]{:S(2)}) async-start(), calls=%async_computation.57 | async-start | bytes 491520 | tf_op jit(solution)/shard_map/reduce_scatter | solution.py:306
  726.0 89.1 %reduce-scatter.80.cloned.1.call-start = ((), (), s32[]{:S(2)}) async-start(), calls=%async_computation.58 | async-start | bytes 491520 | tf_op jit(solution)/shard_map/reduce_scatter | solution.py:309
  774.3 91.9 %reduce-scatter.62.cloned.1.call-start = ((), (), s32[]{:S(2)}) async-start(), calls=%async_computation.47 | async-start | bytes 491520 | tf_op jit(solution)/shard_map/reduce_scatter | solution.py:306
  786.8 106.8 %reduce-scatter.64.cloned.1.call-start = ((), (), s32[]{:S(2)}) async-start(), calls=%async_computation.48 | async-start | bytes 491520 | tf_op jit(solution)/shard_map/reduce_scatter | solution.py:309
  795.3 125.6 %reduce-scatter.54.cloned.1.call-start = ((), (), s32[]{:S(2)}) async-start(), calls=%async_computation.42 | async-start | bytes 491520 | tf_op jit(solution)/shard_map/reduce_scatter | solution.py:306
  802.6 145.8 %reduce-scatter.56.cloned.1.call-start = ((), (), s32[]{:S(2)}) async-start(), calls=%async_computation.43 | async-start | bytes 491520 | tf_op jit(solution)/shard_map/reduce_scatter | solution.py:309
  807.7 164.2 %reduce-scatter.82.cloned.1.call-start = ((), (), s32[]{:S(2)}) async-start(), calls=%async_computation.59 | async-start | bytes 491520 | tf_op jit(solution)/shard_map/reduce_scatter | solution.py:326
  817.5 175.8 %reduce-scatter.74.cloned.1.call-start = ((), (), s32[]{:S(2)}) async-start(), calls=%async_computation.54 | async-start | bytes 491520 | tf_op jit(solution)/shard_map/reduce_scatter | solution.py:326
  841.1 173.9 %reduce-scatter.66.cloned.1.call-start = ((), (), s32[]{:S(2)}) async-start(), calls=%async_computation.49 | async-start | bytes 491520 | tf_op jit(solution)/shard_map/reduce_scatter | solution.py:326
  895.5 141.7 %reduce-scatter.58.cloned.1.call-start = ((), (), s32[]{:S(2)}) async-start(), calls=%async_computation.44 | async-start | bytes 491520 | tf_op jit(solution)/shard_map/reduce_scatter | solution.py:326
  950.5 144.1 %reduce-scatter.96.cloned.1.call-start = ((), (), s32[]{:S(2)}) async-start(), calls=%async_computation.71 | async-start | bytes 147456
  951.4 185.7 %all-gather.28.cloned.1.call-start = ((), (), s32[]{:S(2)}) async-start(), calls=%async_computation.60 | async-start | bytes 1671168 | tf_op jit(solution)/shard_map/all_gather | solution.py:337
  973.6 165.9 %all-gather.26.cloned.1.call-start = ((), (), s32[]{:S(2)}) async-start(), calls=%async_computation.55 | async-start | bytes 1671168 | tf_op jit(solution)/shard_map/all_gather | solution.py:337
  994.9 159.5 %all-gather.24.cloned.1.call-start = ((), (), s32[]{:S(2)}) async-start(), calls=%async_computation.50 | async-start | bytes 1671168 | tf_op jit(solution)/shard_map/all_gather | solution.py:337
  1016.7 197.2 %all-gather.22.cloned.1.call-start = ((), (), s32[]{:S(2)}) async-start(), calls=%async_computation.45 | async-start | bytes 1671168 | tf_op jit(solution)/shard_map/all_gather | solution.py:337
  1038.9 178.5 %reduce-scatter.84.cloned.1.call-start = ((), (), s32[]{:S(2)}) async-start(), calls=%async_computation.65 | async-start | bytes 884736 | tf_op jit(solution)/shard_map/reduce_scatter | solution.py:120
  1046.4 171.0 %reduce-scatter.90.cloned.1.call-start = ((), (), s32[]{:S(2)}) async-start(), calls=%async_computation.68 | async-start | bytes 884736 | tf_op jit(solution)/shard_map/reduce_scatter | solution.py:125
  1049.2 168.2 %reduce-scatter.86.cloned.1.call-start = ((), (), s32[]{:S(2)}) async-start(), calls=%async_computation.66 | async-start | bytes 884736 | tf_op jit(solution)/shard_map/reduce_scatter | solution.py:122
  1054.6 174.4 %reduce-scatter.88.cloned.1.call-start = ((), (), s32[]{:S(2)}) async-start(), calls=%async_computation.67 | async-start | bytes 884736 | tf_op jit(solution)/shard_map/reduce_scatter | solution.py:123
  1060.1 215.2 %reduce-scatter.92.cloned.1.call-start = ((), (), s32[]{:S(2)}) async-start(), calls=%async_computation.69 | async-start | bytes 2654208 | tf_op jit(solution)/shard_map/reduce_scatter | solution.py:129
  1065.1 256.2 %reduce-scatter.94.cloned.1.call-start = ((), (), s32[]{:S(2)}) async-start(), calls=%async_computation.70 | async-start | bytes 2654208 | tf_op jit(solution)/shard_map/reduce_scatter | solution.py:131
  (300 other events, 5110.5 us)
Sparse Core Ops, SparseCore 0:
  12.3 61.7 all-gather.29
  77.5 60.1 all-gather.31
  141.1 57.1 all-gather.33
  201.5 56.6 all-gather.35
  274.5 21.8 reduce-scatter.35
  298.5 22.6 reduce-scatter.39
  323.5 22.6 reduce-scatter.43
  348.6 22.6 reduce-scatter.47
  398.4 21.3 reduce-scatter.37
  437.5 20.5 reduce-scatter.41
  460.3 19.0 reduce-scatter.45
  501.4 19.5 reduce-scatter.49
  545.4 25.3 reduce-scatter.59
  572.9 27.2 reduce-scatter.75
  602.3 22.0 reduce-scatter.51
  626.5 22.6 reduce-scatter.67
  973.7 60.1 all-gather.27
  1036.6 56.8 all-gather.25
  1096.3 58.0 all-gather.23
  1157.1 56.7 all-gather.21
Sparse Core Ops, SparseCore 1:
  309.8 22.6 all-gather.17
  334.1 23.9 all-gather.19
  726.1 24.4 reduce-scatter.77
  759.2 24.5 reduce-scatter.79
  786.6 24.7 reduce-scatter.69
  814.1 24.7 reduce-scatter.71
  841.5 24.6 reduce-scatter.61
  868.9 24.6 reduce-scatter.63
  896.2 24.6 reduce-scatter.53
  923.7 24.6 reduce-scatter.55
  951.2 20.7 reduce-scatter.81
  974.2 19.0 reduce-scatter.73
  995.4 19.5 reduce-scatter.65
  1017.3 19.8 reduce-scatter.57
  1040.3 33.7 reduce-scatter.95
  1077.7 35.0 reduce-scatter.83
  1116.5 35.3 reduce-scatter.89
  1155.6 34.9 reduce-scatter.85
  1194.2 34.9 reduce-scatter.87
  1233.0 42.2 reduce-scatter.91
  1279.1 42.2 reduce-scatter.93
where the time goes:
time: 1340 us; the launch traced here: 1330 us
  waiting for transfers between devices  533 us (40%)
  blocking collectives  391 us (29%)
  matrix products  188 us (14%)
  local copies, waits for them, and re-layouts  110 us (8%)
  other arithmetic  82.6 us (6%)
  between operations  22.3 us (2%)
    reduce_scatter x4, waiting for transfers between devices, body(): lax.psum_scatter((dot_right_t(d_query, bwd['query_w']) + dot_right_t(d_ke...  80.7 us
    dot_general x48, matrix products, dot_right_t(): lax.dot_general(former, latter, (((1,), (1,)), ((), ())), preferred_eleme...  71.5 us
    all_gather x4, waiting for transfers between devices, body(): d_group = lax.all_gather(d_x, ('ctx', 'tp'), axis=0, tiled=True)  69.7 us
    reduce_scatter x4, waiting for transfers between devices, body(): lax.psum_scatter(value_part.astype(jnp.bfloat16), 'ctx', scatter_dimensio...  69.6 us
    all_gather x4, blocking collectives, body(): lax.all_gather(middle.astype(jnp.bfloat16), 'tp', axis=0, tiled=True)  62.5 us
    all_gather x4, blocking collectives, body(): lax.all_gather(d_end.astype(jnp.bfloat16), 'tp', axis=0, tiled=True)  61.9 us
    dot_general x48, matrix products, dot_left_t(): lax.dot_general(former, latter, (((0,), (0,)), ((), ())), preferred_eleme...  59.4 us
    all_gather x4, blocking collectives, body(): lax.all_gather(d_mid_in.astype(jnp.bfloat16), 'tp', axis=0, tiled=True)  58.2 us
  transfers between devices with their start and end apart: 41, of which 22 were waited for; matrix products, arithmetic and copies ran while one was open for 22% of the time, Pallas kernels for 0%

commit v1 on v0

v1 whole, which is shorter than its diff:
```python
import jax
import jax.numpy as jnp
from jax import lax
from jax.sharding import PartitionSpec as P

EPS = 1e-06
MASKED = -1e30
ALL = ("fsdp", "ctx", "tp")
ROWS = ("fsdp", "ctx")
BF = jnp.bfloat16
F32 = jnp.float32


def mm(a, b):
    return jnp.dot(a, b, preferred_element_type=F32)


def mm_rt(a, b):
    return lax.dot_general(a, b, (((1,), (1,)), ((), ())), preferred_element_type=F32)


def mm_lt(a, b):
    return lax.dot_general(a, b, (((0,), (0,)), ((), ())), preferred_element_type=F32)


def norm(u):
    centre = u - jnp.mean(u, axis=-1, keepdims=True)
    inv = lax.rsqrt(jnp.mean(centre * centre, axis=-1, keepdims=True) + EPS)
    return centre * inv, inv


def norm_back(d, gain, n, inv):
    e = d * gain
    return (e - jnp.mean(e, axis=-1, keepdims=True) - n * jnp.mean(e * n, axis=-1, keepdims=True)) * inv


def phi_both(u):
    cdf = 0.5 * (1.0 + lax.erf(u * 0.7071067811865476))
    pdf = 0.3989422804014327 * jnp.exp(-0.5 * u * u)
    return cdf, pdf


def gather_group(block):
    width = block.shape[-1]
    mine = lax.all_to_all(block, "ctx", 0, 0, tiled=True)
    whole = lax.all_gather(mine, "tp", axis=1, tiled=False)
    return whole.reshape(-1, width)


def scatter_group(rows, own_rows):
    ctx_n, tp_n = lax.axis_size("ctx"), lax.axis_size("tp")
    width = rows.shape[-1]
    blocks = rows.reshape(ctx_n, tp_n * own_rows, width)
    mine = lax.psum_scatter(blocks, "tp", scatter_dimension=1, tiled=True)
    return lax.all_to_all(mine, "ctx", 0, 0, tiled=True)


def body(tokens_in, cotangent, seq_lengths, row_order, w_query, b_query, w_key, w_value, b_value,
         w_out, b_out, mid_gain, mid_shift, w_up, b_up, w_down, b_down, end_gain, end_shift):
    ctx_n, tp_n, fsdp_n = lax.axis_size("ctx"), lax.axis_size("tp"), lax.axis_size("fsdp")
    rows_n = ctx_n * fsdp_n
    c, t = lax.axis_index("ctx"), lax.axis_index("tp")
    micro, own_rows, width = tokens_in.shape
    group_rows = own_rows * ctx_n * tp_n
    half_rows = group_rows // 2
    parts = tp_n // 2
    my_rows = half_rows // parts
    half, quarter = t // parts, t % parts
    heads_l, head_l = b_query.shape
    heads, head = heads_l * tp_n, head_l * rows_n

    mats = (w_query, w_key, w_value, w_out, w_up, w_down)
    widths = [m.shape[1] for m in mats]
    packed = lax.all_gather(jnp.concatenate(mats, axis=1), ALL, axis=0, tiled=False)
    full, at = [], 0
    for wd in widths:
        piece = packed[:, :, at:at + wd].reshape(rows_n, tp_n, -1, wd)
        full.append(piece.transpose(0, 2, 1, 3).reshape(width, tp_n * wd))
        at += wd
    wq, wk, wv, wo, wu, wd_ = full
    vecs = (b_out, mid_gain, mid_shift, b_down, end_gain, end_shift)
    bias = (b_query, b_value, b_up)
    vec_all = lax.all_gather(jnp.stack(vecs), ROWS, axis=1, tiled=True).astype(F32)
    bias_all = lax.all_gather(jnp.concatenate(bias, axis=1), ALL, axis=0, tiled=False).astype(F32)

    def whole_bias(at, wd):
        piece = bias_all[:, :, at:at + wd].reshape(rows_n, tp_n, heads_l, wd)
        return piece.transpose(1, 2, 0, 3).reshape(-1)

    bq = whole_bias(0, head_l)
    bv = whole_bias(head_l, head_l)
    bu = whole_bias(2 * head_l, b_up.shape[1])
    bo, mg, ms, bd, eg, es = (vec_all[i] for i in range(6))

    lens = lax.dynamic_index_in_dim(seq_lengths[:, 0], c, 0, keepdims=False)
    order = lax.dynamic_index_in_dim(row_order[:, 0], c, 0, keepdims=False)
    places = lax.iota(jnp.int32, lens.shape[0])
    longest = jnp.argmax(lens)
    first = jnp.sum(jnp.where(places < longest, lens, 0))
    start = lax.rem(first + half * half_rows, group_rows)
    ends = jnp.cumsum(lens)
    nat = lax.rem(start + lax.iota(jnp.int32, half_rows), group_rows)
    seg = jnp.sum((ends[None, :] <= nat[:, None]).astype(jnp.int32), axis=1)
    q_at = quarter * my_rows
    nat_q = lax.dynamic_slice_in_dim(nat, q_at, my_rows)
    seg_q = lax.dynamic_slice_in_dim(seg, q_at, my_rows)

    x_group = gather_group(tokens_in)
    c_group = gather_group(cotangent)
    x_twice = jnp.concatenate([x_group, x_group[:half_rows]], axis=0)
    x_half = lax.dynamic_slice_in_dim(x_twice, start, half_rows, 0)
    x_mine = lax.dynamic_slice_in_dim(x_half, q_at, my_rows, 0)
    pick = (order[:, None] == nat_q[None, :]).astype(BF)
    pick_nat = (lax.iota(jnp.int32, group_rows)[:, None] == nat_q[None, :]).astype(BF)
    dy = mm_lt(pick, c_group)

    x = x_mine.astype(F32)
    q = (mm(x_mine, wq) + bq).astype(BF).reshape(my_rows, heads, head)
    k = mm(x_half, wk).astype(BF).reshape(half_rows, heads, head)
    v = (mm(x_half, wv) + bv).astype(BF).reshape(half_rows, heads, head)
    same = seg_q[:, None] == seg[None, :]
    s = jnp.einsum("qhd,khd->hqk", q, k, preferred_element_type=F32) * 0.125
    s = jnp.where(same[None], s, MASKED)
    p = jnp.exp(s - jnp.max(s, axis=-1, keepdims=True))
    p = p / jnp.sum(p, axis=-1, keepdims=True)
    pb = p.astype(BF)
    o = jnp.einsum("hqk,khd->qhd", pb, v, preferred_element_type=F32).astype(BF)
    o2 = o.reshape(my_rows, heads * head)
    r1 = x + mm_rt(o2, wo) + bo
    n1, inv1 = norm(r1)
    middle = n1 * mg + ms
    mid_b = middle.astype(BF)
    pre = mm(mid_b, wu) + bu
    cdf, pdf = phi_both(pre)
    act = (pre * cdf).astype(BF)
    r2 = middle + mm_rt(act, wd_) + bd
    n2, inv2 = norm(r2)
    y = n2 * eg + es

    d_r2 = norm_back(dy, eg, n2, inv2)
    df = d_r2.astype(BF)
    d_pre = (mm(df, wd_) * (cdf + pre * pdf)).astype(BF)
    g_down = mm_lt(df, act)
    g_up = mm_lt(mid_b, d_pre)
    d_mid = d_r2 + mm_rt(d_pre, wu)
    d_r1 = norm_back(d_mid, mg, n1, inv1)
    da = d_r1.astype(BF)
    g_out = mm_lt(da, o2)
    d_o = mm(da, wo).astype(BF).reshape(my_rows, heads, head)
    dp = jnp.einsum("qhd,khd->hqk", d_o, v, preferred_element_type=F32)
    ds = (p * (dp - jnp.sum(p * dp, axis=-1, keepdims=True))).astype(BF)
    d_q = (jnp.einsum("hqk,khd->qhd", ds, k, preferred_element_type=F32) * 0.125).astype(BF)
    d_k = jnp.einsum("hqk,qhd->khd", ds, q, preferred_element_type=F32) * 0.125
    d_v = jnp.einsum("hqk,qhd->khd", pb, d_o, preferred_element_type=F32)
    d_q = d_q.reshape(my_rows, heads * head)
    d_kv = jnp.concatenate([d_k.reshape(half_rows, -1), d_v.reshape(half_rows, -1)], axis=1).astype(BF)
    pairs = [[h * parts + j for j in range(parts)] for h in range(tp_n // parts)]
    d_kv = lax.psum_scatter(d_kv.astype(F32), "tp", scatter_dimension=0, tiled=True, axis_index_groups=pairs)
    d_k, d_v = jnp.split(d_kv.astype(BF), 2, axis=1)
    g_q = mm_lt(x_mine, d_q)
    g_k = mm_lt(x_mine, d_k)
    g_v = mm_lt(x_mine, d_v)
    d_x = (d_r1 + mm_rt(d_q, wq) + mm_rt(d_k, wk) + mm_rt(d_v, wv)).astype(BF)

    layer_out = scatter_group(mm(pick, y.astype(BF)).astype(BF), own_rows)
    input_grad = scatter_group(mm(pick_nat, d_x).astype(BF), own_rows)

    outs = []
    for g, wd in zip((g_q, g_k, g_v, g_out, g_up, g_down), widths):
        outs.append(g.astype(BF).reshape(rows_n, width // rows_n, tp_n, wd).transpose(0, 2, 1, 3))
    packed_g = jnp.concatenate(outs, axis=3)
    packed_g = packed_g.reshape(rows_n * tp_n, width // rows_n, -1)
    mine_g = lax.psum_scatter(packed_g, ALL, scatter_dimension=0, tiled=True)[0].astype(F32)
    gm, at = [], 0
    for wd in widths:
        gm.append(mine_g[:, at:at + wd])
        at += wd

    def total(a):
        return jnp.sum(a.astype(F32), axis=0)

    def split_bias(a, wd):
        return a.reshape(tp_n, heads_l, rows_n, wd).transpose(2, 0, 1, 3).reshape(rows_n * tp_n, heads_l, wd)

    small_b = jnp.concatenate([
        split_bias(total(d_q), head_l), split_bias(total(d_v), head_l), split_bias(total(d_pre), b_up.shape[1])],
        axis=2).reshape(rows_n * tp_n, -1)
    vec_g = jnp.stack([total(d_r1), total(d_mid * n1), total(d_mid), total(d_r2), total(dy * n2), total(dy)])
    small_v = vec_g.reshape(6, rows_n, 1, width // rows_n).transpose(1, 2, 0, 3)
    small_v = jnp.broadcast_to(small_v, (rows_n, tp_n, 6, width // rows_n)).reshape(rows_n * tp_n, -1)
    small = jnp.concatenate([small_b, small_v], axis=1)
    small = lax.psum_scatter(small, ALL, scatter_dimension=0, tiled=True)[0]
    nb = small_b.shape[1]
    sb = small[:nb].reshape(heads_l, -1)
    sv = small[nb:].reshape(6, -1)
    return (layer_out, input_grad, gm[0], sb[:, :head_l], gm[1], gm[2], sb[:, head_l:2 * head_l], gm[3],
            sv[0], sv[1], sv[2], gm[4], sb[:, 2 * head_l:], gm[5], sv[3], sv[4], sv[5])


def specs():
    tok = P(None, ALL, None)
    grp = P(None, "fsdp", None)
    mat = P(ROWS, "tp")
    bias = P("tp", ROWS)
    vec = P(ROWS)
    ins = (tok, tok, grp, grp, mat, bias, mat, mat, bias, mat, vec, vec, vec, mat, bias, mat, vec, vec, vec)
    return ins, (tok, tok) + ins[4:]


def solution(mesh):
    ins, outs = specs()
    return jax.shard_map(body, mesh=mesh, in_specs=ins, out_specs=outs, check_vma=False)
```

time: 1340 us -> 722 us (0.54)
  blocking collectives: 391 us -> 103 us
  waiting for transfers between devices: 533 us -> 299 us
  matrix products: 188 us -> 73.7 us
  local copies, waits for them, and re-layouts: 110 us -> 189 us
  other arithmetic: 82.6 us -> 15.8 us
    all_gather x19 -> x2, blocking collectives: 327 us -> 89.9 us  [the longest x1 68.8 us: body(): lax.all_gather(jnp.concatenate(bias, axis=1), ALL, axis=0, tiled=False)]
    reduce_scatter x30 -> x4, waiting for transfers between devices: 406 us -> 214 us  [the longest x1 158 us: body(): lax.psum_scatter(packed_g, ALL, scatter_dimension=0, tiled=True)[0]]
    dot_general x144 -> x25, matrix products: 188 us -> 67.5 us  [the longest x8 25.9 us: mm(): return jnp.dot(a, b, preferred_element_type=F32)]
    all_gather x10 -> x3, waiting for transfers between devices: 124 us -> 33.2 us  [the longest x1 33.1 us: body(): lax.all_gather(jnp.concatenate(mats, axis=1), ALL, axis=0, tiled=False)]
    gather x16 -> x0, local copies, waits for them, and re-layouts: 59.6 us -> none  [the longest x4 29 us: body(): x_perm = jnp.take(x_group, row_perm, axis=0)]
    reshape x0 -> x19, local copies, waits for them, and re-layouts: none -> 54.9 us  [the longest x6 37.8 us: body(): g.astype(BF).reshape(rows_n, width // rows_n, tp_n, wd)]
    concatenate x0 -> x4, local copies, waits for them, and re-layouts: none -> 54.7 us  [the longest x2 52.6 us: body(): packed_g = jnp.concatenate(outs, axis=3)]
    unnamed x2 -> x0, blocking collectives: 53.1 us -> none
  transfers between devices with their start and end apart: 41 -> 11, of which waited for: 22 -> 7; matrix products, arithmetic and copies ran while one was open for 22% -> 34% of each run, Pallas kernels for 0% -> 0%
where the time goes in v1:
time: 722 us; the launch traced here: 709 us
  waiting for transfers between devices  299 us (41%)
  local copies, waits for them, and re-layouts  189 us (26%)
  blocking collectives  103 us (14%)
  matrix products  73.7 us (10%)
  between operations  16.2 us (2%)
  other arithmetic  15.8 us (2%)
  starting transfers between devices  11.3 us (2%)
    reduce_scatter x1, waiting for transfers between devices, body(): lax.psum_scatter(packed_g, ALL, scatter_dimension=0, tiled=True)[0]  158 us
    all_gather x1, blocking collectives, body(): lax.all_gather(jnp.concatenate(bias, axis=1), ALL, axis=0, tiled=False)  68.8 us
    concatenate x2, local copies, waits for them, and re-layouts, body(): packed_g = jnp.concatenate(outs, axis=3)  52.6 us
    unnamed x9, waiting for transfers between devices  41 us
    reshape x6, local copies, waits for them, and re-layouts, body(): g.astype(BF).reshape(rows_n, width // rows_n, tp_n, wd)  37.8 us
    reduce_scatter x2, waiting for transfers between devices, scatter_group(): mine = lax.psum_scatter(blocks, 'tp', scatter_dimension=1, tiled=True)  37.3 us
    all_gather x1, waiting for transfers between devices, body(): lax.all_gather(jnp.concatenate(mats, axis=1), ALL, axis=0, tiled=False)  33.1 us
    transpose x6, local copies, waits for them, and re-layouts, body(): full.append(piece.transpose(0, 2, 1, 3).reshape(width, tp_n * wd))  27.6 us
  transfers between devices with their start and end apart: 11, of which 7 were waited for; matrix products, arithmetic and copies ran while one was open for 34% of the time, Pallas kernels for 0%

profile of v1, /device:TPU:0, one launch (start us, length us, event | category | flops | bytes accessed | tf_op | source)
XLA Modules:
  0.0 708.5 jit_solution(12837532554560193029)
XLA Ops:
  7.4 13.0 %all_to_all.20 = bf16[4,64,768]{2,1,0:T(8,128)(2,1)} all-to-all(bf16[4,64,768]{2,1,0:T(8,128)(2,1)} %param.19), channel_id=1, replica_groups=mesh['fsdp'=2,'ctx'=4,'tp'=4] {'ctx'}, dimensions={0} | all-to-all | bytes 786432 | tf_op jit(solution)/shard_map/all_to_all | solution.py:45
  29.6 21.1 %all-gather.5 = bf16[8,96,6]{1,2,0:T(8,128)(2,1)S(1)} all-gather(bf16[1,96,6]{1,2,0:T(8,128)(2,1)S(1)} %bitcast.231), channel_id=1, replica_groups=mesh['fsdp'=2,'ctx'=4,'tp'=4] {'fsdp','ctx'}, dimensions={0}, use_global_device_ids=true | all-gather | bytes 10368 | tf_op jit(solution)/shard_map/all_gather | solution.py:83
  50.9 68.8 %all-gather.4 = bf16[32,3,48]{2,1,0:T(4,128)(2,1)S(1)} all-gather(bf16[1,3,48]{2,1,0:T(4,128)(2,1)S(1)} %maximum_bitcast_fusion), channel_id=4, replica_groups=mesh['fsdp'=2,'ctx'=4,'tp'=4] {'fsdp','ctx','tp'}, dimensions={0}, use_global_device_ids=true | all-gather | bytes 9504 | tf_op jit(solution)/shard_map/all_gather | solution.py:84
  128.7 33.1 %all-gather.12.cloned.1.call-done = bf16[3072,2304]{1,0:T(8,128)(2,1)} async-done(((bf16[96,2304]{1,0:T(8,128)(2,1)}), bf16[3072,2304]{1,0:T(8,128)(2,1)}) %all-gather.12.cloned.1.call-update) | async-done | bytes 14155792 | tf_op jit(solution)/shard_map/all_gather | solution.py:74
  161.9 8.1 %fusion.61 = (bf16[32,96,768]{2,1,0:T(8,128)(2,1)}, bf16[32,96,768]{2,1,0:T(8,128)(2,1)}) fusion(bf16[32,96,2304]{2,1,0:T(8,128)(2,1)} %bitcast.177), kind=kLoop, calls=%fused_computation.141 | loop fusion | bytes 18874368 | tf_op jit(solution)/shard_map/slice | solution.py:77
  170.0 7.0 fusion.62
  179.8 3.8 reshape.317
  192.3 3.8 reshape.323
  216.3 6.1 fusion.67
  222.5 4.1 fusion.25
  234.0 14.7 %copy.123 = bf16[8,96,4,768]{3,2,1,0:T(4,128)(2,1)S(1)} copy(bf16[8,96,4,768]{3,1,2,0:T(8,128)(2,1)S(1)} %bitcast.173) | data formatting | bytes 9437184 | tf_op jit(solution)/shard_map/transpose | solution.py:78
  250.1 3.7 multiply_convert_fusion.1
  259.8 5.0 convert_reduce_fusion
  269.7 4.0 multiply_reduce_fusion
  306.3 19.4 %reduce-scatter.7.cloned.1.call-done = f32[256,1536]{0,1:T(8,128)} async-done(((f32[512,1536]{0,1:T(8,128)}), f32[256,1536]{0,1:T(8,128)}) %reduce-scatter.7.cloned.1.call-update) | async-done | bytes 1572880 | tf_op jit(solution)/shard_map/reduce_scatter | solution.py:158
  329.9 3.9 convolution_convert_fusion.2
  335.7 4.4 reshape.344
  341.8 4.4 reshape.347
  346.2 5.2 convolution_convert_fusion.1
  351.4 9.9 %reshape.348 = bf16[8,96,4,768]{3,2,1,0:T(4,128)(2,1)} reshape(bf16[768,3072]{1,0:T(8,128)(2,1)} %convolution_convert_fusion.1) | data formatting | bytes 9437184 | tf_op jit(solution)/shard_map/reshape | solution.py:170
  361.3 3.7 convolution_convert_fusion
  365.0 9.8 %reshape.349 = bf16[8,96,4,768]{3,2,1,0:T(4,128)(2,1)} reshape(bf16[768,3072]{1,0:T(8,128)(2,1)} %convolution_convert_fusion) | data formatting | bytes 9437184 | tf_op jit(solution)/shard_map/reshape | solution.py:170
  376.3 4.5 reshape.345
  382.4 4.8 reshape.346
  387.2 41.3 %concatenate.27 = bf16[8,4,96,2304]{3,1,2,0:T(4,128)(2,1)} concatenate(bf16[8,4,96,192]{3,1,2,0:T(4,128)(2,1)S(1)} %bitcast.179, bf16[8,4,96,192]{3,1,2,0:T(4,128)(2,1)} %bitcast.181, bf16[8,4,96,192]{3,1,2,0:T(4,128)(2,1)} %bitcast.182, bf16[8,4,96,192]{3,1,2,0:T(4,128)(2,1)S(1)} %bitcast.180, bf16[8,4,96,768]{3,1,2,0:T(4,128)(2,1)} %bitcast.167, bf16[8,4,96,768]{3,1,2,0:T(4,128)(2,1)} %bitcast.168), dimensions={3} | concatenate | bytes 28311552 | tf_op jit(solution)/shard_map/concatenate | solution.py:171
  428.5 11.3 %copy.125 = bf16[8,4,96,2304]{3,2,1,0:T(8,128)(2,1)} copy(bf16[8,4,96,2304]{3,1,2,0:T(4,128)(2,1)} %concatenate.27) | data formatting | bytes 28311552 | tf_op jit(solution)/shard_map/concatenate | solution.py:171
  443.5 6.5 all-to-all-done.1
  450.0 40.9 %all-reduce.3.cloned.1.call-done = f32[32,720]{1,0:T(8,128)} async-done(((f32[32,720]{1,0:T(8,128)}), f32[32,720]{1,0:T(8,128)}) %all-reduce.3.cloned.1.call-update) | async-done | bytes 92176
  492.3 37.2 %reduce-scatter.9.cloned.1.call-done = bf16[4,64,768]{2,1,0:T(8,128)(2,1)} async-done(((bf16[4,256,768]{2,1,0:T(8,128)(2,1)}), bf16[4,64,768]{2,1,0:T(8,128)(2,1)}) %reduce-scatter.9.cloned.1.call-update) | async-done | bytes 393232 | tf_op jit(solution)/shard_map/reduce_scatter | solution.py:54
  529.5 3.6 all-to-all-start.3
  535.3 4.1 all-to-all-done.3
  539.4 157.6 %reduce-scatter.11.cloned.1.call-done = bf16[1,96,2304]{2,1,0:T(8,128)(2,1)} async-done(((bf16[32,96,2304]{2,1,0:T(8,128)(2,1)}), bf16[1,96,2304]{2,1,0:T(8,128)(2,1)}) %reduce-scatter.11.cloned.1.call-update) | async-done | bytes 442384 | tf_op jit(solution)/shard_map/reduce_scatter | solution.py:173
  (258 shorter events, 123.2 us)
Async XLA Ops:
  7.2 115.8 %copy-start = (s32[4,1,1024]{2,1,0:T(1,128)S(1)}, s32[4,1,1024]{2,1,0:T(1,128)}, u32[]{:S(2)}) copy-start(s32[4,1,1024]{2,1,0:T(1,128)} %param.22) | copy-start | bytes 49156
  7.2 18.8 %copy-start.50 = (s32[4,1,3]{0,1,2:T(1,128)S(1)}, s32[4,1,3]{0,1,2:T(1,128)}, u32[]{:S(2)}) copy-start(s32[4,1,3]{0,1,2:T(1,128)} %param.21) | copy-start | bytes 148
  7.2 22.3 %copy-start.54 = (bf16[96]{0:T(256)(128)(2,1)S(1)}, bf16[96]{0:T(256)(128)(2,1)}, u32[]{:S(2)}) copy-start(bf16[96]{0:T(256)(128)(2,1)} %param.29) | copy-start | bytes 580
  7.2 22.3 %copy-start.55 = (bf16[96]{0:T(256)(128)(2,1)S(1)}, bf16[96]{0:T(256)(128)(2,1)}, u32[]{:S(2)}) copy-start(bf16[96]{0:T(256)(128)(2,1)} %param.30) | copy-start | bytes 580
  7.2 22.3 %copy-start.56 = (bf16[96]{0:T(256)(128)(2,1)S(1)}, bf16[96]{0:T(256)(128)(2,1)}, u32[]{:S(2)}) copy-start(bf16[96]{0:T(256)(128)(2,1)} %param.31) | copy-start | bytes 580
  7.3 22.3 %copy-start.57 = (bf16[96]{0:T(256)(128)(2,1)S(1)}, bf16[96]{0:T(256)(128)(2,1)}, u32[]{:S(2)}) copy-start(bf16[96]{0:T(256)(128)(2,1)} %param.35) | copy-start | bytes 580
  7.3 22.3 %copy-start.58 = (bf16[96]{0:T(256)(128)(2,1)S(1)}, bf16[96]{0:T(256)(128)(2,1)}, u32[]{:S(2)}) copy-start(bf16[96]{0:T(256)(128)(2,1)} %param.36) | copy-start | bytes 580
  7.3 22.3 %copy-start.59 = (bf16[96]{0:T(256)(128)(2,1)S(1)}, bf16[96]{0:T(256)(128)(2,1)}, u32[]{:S(2)}) copy-start(bf16[96]{0:T(256)(128)(2,1)} %param.37) | copy-start | bytes 580
  7.3 43.5 %copy-start.51 = (bf16[3,32]{1,0:T(4,128)(2,1)S(1)}, bf16[3,32]{1,0:T(4,128)(2,1)}, u32[]{:S(2)}) copy-start(bf16[3,32]{1,0:T(4,128)(2,1)} %param.33) | copy-start | bytes 580
  7.3 43.5 %copy-start.52 = (bf16[3,8]{1,0:T(4,128)(2,1)S(1)}, bf16[3,8]{1,0:T(4,128)(2,1)}, u32[]{:S(2)}) copy-start(bf16[3,8]{1,0:T(4,128)(2,1)} %param.27) | copy-start | bytes 148
  7.3 43.5 %copy-start.53 = (bf16[3,8]{1,0:T(4,128)(2,1)S(1)}, bf16[3,8]{1,0:T(4,128)(2,1)}, u32[]{:S(2)}) copy-start(bf16[3,8]{1,0:T(4,128)(2,1)} %param.24) | copy-start | bytes 148
  7.3 117.9 %all-gather.10.cloned.1.call-start = ((), (), s32[]{:S(2)}) async-start(), calls=%async_computation.12 | async-start | bytes 1966080 | tf_op jit(solution)/shard_map/all_gather | solution.py:46
  20.4 141.5 %all-gather.12.cloned.1.call-start = ((), (), s32[]{:S(2)}) async-start(), calls=%async_computation.13 | async-start | bytes 14598144 | tf_op jit(solution)/shard_map/all_gather | solution.py:74
  22.4 101.9 %all-to-all-start.2 = ((bf16[4,64,768]{2,1,0:T(8,128)(2,1)}), bf16[4,64,768]{2,1,0:T(8,128)(2,1)S(1)}, u32[]{:S(2)}, u32[]{:S(2)}) async-start(bf16[4,64,768]{2,1,0:T(8,128)(2,1)} %param.20), calls=%async_computation.3 | async-start | bytes 786432 | tf_op jit(solution)/shard_map/all_to_all | solution.py:45
  25.9 229.8 %all-gather.14.cloned.1.call-start = ((), (), s32[]{:S(2)}) async-start(), calls=%async_computation.14 | async-start | bytes 1966080 | tf_op jit(solution)/shard_map/all_gather | solution.py:46
  125.1 200.5 %reduce-scatter.7.cloned.1.call-start = ((), (), s32[]{:S(2)}) async-start(), calls=%async_computation.9 | async-start | bytes 4718592 | tf_op jit(solution)/shard_map/reduce_scatter | solution.py:158
  227.2 40.0 %copy-start.2 = (f32[256,768]{1,0:T(8,128)}, f32[256,768]{1,0:T(8,128)S(1)}, u32[]{:S(2)}) copy-start(f32[256,768]{1,0:T(8,128)S(1)} %get-tuple-element.62) | copy-start | bytes 2359300
  231.9 18.1 %copy-start.9 = (bf16[96,8,4,768]{3,1,2,0:T(8,128)(2,1)}, bf16[96,8,4,768]{3,1,2,0:T(8,128)(2,1)S(1)}, u32[]{:S(2)}) copy-start(bf16[96,8,4,768]{3,1,2,0:T(8,128)(2,1)S(1)} %copy.130) | copy-start | bytes 14155780
  249.8 17.3 %copy-start.33 = (f32[256]{0:T(256)}, f32[256]{0:T(256)S(1)}, u32[]{:S(2)}) copy-start(f32[256]{0:T(256)S(1)} %broadcast_multiply_fusion.5) | copy-start | bytes 3076
  250.1 17.1 %copy-start.41 = (f32[256]{0:T(256)}, f32[256]{0:T(256)S(1)}, u32[]{:S(2)}) copy-start(f32[256]{0:T(256)S(1)} %add_rsqrt_fusion.1) | copy-start | bytes 3076
  283.5 156.4 %reduce-scatter.5.cloned.1.call-start = ((), (), s32[]{:S(2)}) async-start(), calls=%async_computation.8 | async-start | bytes 1966080 | tf_op jit(solution)/shard_map/reduce_scatter | solution.py:54
  286.7 204.1 %all-reduce.3.cloned.1.call-start = ((), (), s32[]{:S(2)}) async-start(), calls=%async_computation.15 | async-start | bytes 196608
  303.9 23.6 %copy-start.29 = (f32[8,4,3,32]{3,1,0,2:T(4,128)S(1)}, f32[8,4,3,32]{3,1,0,2:T(4,128)}, u32[]{:S(2)}) copy-start(f32[8,4,3,32]{3,1,0,2:T(4,128)} %copy.128) | copy-start | bytes 36868
  304.0 23.7 %copy-start.28 = (f32[32,576]{1,0:T(8,128)S(1)}, f32[32,576]{1,0:T(8,128)}, u32[]{:S(2)}) copy-start(f32[32,576]{1,0:T(8,128)} %reshape.358) | copy-start | bytes 221188
  304.0 24.4 %copy-start.13 = (bf16[768,768]{0,1:T(8,128)(2,1)S(1)}, bf16[768,768]{0,1:T(8,128)(2,1)}, u32[]{:S(2)}) copy-start(bf16[768,768]{0,1:T(8,128)(2,1)} %copy-done.12) | copy-start | bytes 3538948
  306.2 23.7 %copy-start.45 = (s32[256]{0:T(256)S(1)}, s32[256]{0:T(256)}, u32[]{:S(2)}) copy-start(s32[256]{0:T(256)} %dynamic_slice.25) | copy-start | bytes 3076
  329.9 199.7 %reduce-scatter.9.cloned.1.call-start = ((), (), s32[]{:S(2)}) async-start(), calls=%async_computation.10 | async-start | bytes 1966080 | tf_op jit(solution)/shard_map/reduce_scatter | solution.py:54
  333.9 363.2 %reduce-scatter.11.cloned.1.call-start = ((), (), s32[]{:S(2)}) async-start(), calls=%async_computation.11 | async-start | bytes 14598144 | tf_op jit(solution)/shard_map/reduce_scatter | solution.py:173
  376.3 10.9 %copy-start.7 = (bf16[8,96,4,192]{3,2,1,0:T(4,128)(2,1)S(1)}, bf16[8,96,4,192]{3,2,1,0:T(4,128)(2,1)}, u32[]{:S(2)}) copy-start(bf16[8,96,4,192]{3,2,1,0:T(4,128)(2,1)} %reshape.344) | copy-start | bytes 3538948
  439.8 261.4 %copy-start.1 = (s32[4,1,1024]{2,1,0:T(1,128)S(1)}, s32[4,1,1024]{2,1,0:T(1,128)}, u32[]{:S(2)}) copy-start(s32[4,1,1024]{2,1,0:T(1,128)} %param.22) | copy-start | bytes 49156
  439.9 10.1 %all-to-all-start.1 = ((bf16[4,64,768]{2,1,0:T(8,128)(2,1)}), bf16[4,64,768]{2,1,0:T(8,128)(2,1)S(1)}, u32[]{:S(2)}, u32[]{:S(2)}) async-start(bf16[4,64,768]{2,1,0:T(8,128)(2,1)} %reduce-scatter.5.cloned.1.call-done), calls=%async_computation.2 | async-start | bytes 786432 | tf_op jit(solution)/shard_map/all_to_all | solution.py:55
  529.5 9.9 %all-to-all-start.3 = ((bf16[4,64,768]{2,1,0:T(8,128)(2,1)}), bf16[4,64,768]{2,1,0:T(8,128)(2,1)S(1)}, u32[]{:S(2)}, u32[]{:S(2)}) async-start(bf16[4,64,768]{2,1,0:T(8,128)(2,1)} %reduce-scatter.9.cloned.1.call-done), calls=%async_computation.6 | async-start | bytes 786432 | tf_op jit(solution)/shard_map/all_to_all | solution.py:55
  (45 other events, 187.0 us)
Sparse Core Ops, SparseCore 0:
  20.5 36.9 all-gather.9
  60.3 101.5 all-gather.11
  163.4 35.4 all-gather.13
  283.6 42.0 reduce-scatter.6
  327.8 35.3 reduce-scatter.4
  369.3 121.5 all-reduce.2
  493.1 36.3 reduce-scatter.8
  535.5 161.4 reduce-scatter.10

commit v2 on v1

--- a/solution.py
+++ b/solution.py
@@ -1,6 +1,10 @@
+import functools
+
 import jax
 import jax.numpy as jnp
 from jax import lax
+from jax.experimental import pallas as pl
+from jax.experimental.pallas import tpu as pltpu
 from jax.sharding import PartitionSpec as P
 
 EPS = 1e-06
@@ -11,6 +15,7 @@
 F32 = jnp.float32
 
 
+MESH = pl.DeviceIdType.MESH
 def mm(a, b):
     return jnp.dot(a, b, preferred_element_type=F32)
 
@@ -207,6 +212,753 @@
     return ins, (tok, tok) + ins[4:]
 
 
+CHUNK = 32
+VMEM_MAX = 62 * 1024 * 1024
+
+
+def block_mat(ref, t):
+    n, rows, width = ref.shape[1:]
+    return ref[t].reshape(n * rows, width)
+
+
+def row_facts(meta, group_n):
+    c, t = lax.axis_index("ctx"), lax.axis_index("tp")
+    lens = meta[4:5, :].astype(F32)
+    lane = lax.broadcasted_iota(jnp.int32, lens.shape, 1)
+
+    def one(k):
+        return jnp.sum(jnp.where(lane == 3 * c + k, lens, 0.0), axis=1, keepdims=True).astype(jnp.int32)
+
+    l0, l1 = one(0), one(1)
+    half = group_n // 2
+    first = jnp.where(l0 == half, 0, jnp.where(l1 == half, l0, l0 + l1))
+    return first + (t % 2) * half, l0, l0 + l1
+
+
+def wrap(v, group_n):
+    return jnp.where(v >= group_n, v - group_n, v)
+
+
+def pick_row(block, c):
+    row = lax.broadcasted_iota(jnp.int32, block.shape, 0)
+    return jnp.sum(jnp.where(row == c, block.astype(F32), 0.0), axis=0, keepdims=True).astype(jnp.int32)
+
+
+def chunks(total, fn, size=CHUNK):
+    def step(i, _):
+        fn(pl.ds(pl.multiple_of(i * size, size), size))
+        return 0
+    lax.fori_loop(0, total // size, step, 0)
+
+
+def each_t(fn):
+    def step(t, _):
+        fn(t)
+        return 0
+    lax.fori_loop(0, 4, step, 0)
+
+
+def k1_kernel(head, gath, meta_ref, group, gg, dq_out, dkv_out, xm_out, da_out, op_out, dr1_out, y_out, vec_out,
+              w_a, w_u, w_d, small, xh, dy, qkv, probs, sbuf, pb, pb2, acc, mid, midb, n1, inv1, gelu_d, act, n2, df, big, bias,
+              g_u, g_d, sem):
+    f, c, t_me = lax.axis_index("fsdp"), lax.axis_index("ctx"), lax.axis_index("tp")
+    width = xh.shape[1]
+    s_n, r_n, n_n = xh.shape[0], dy.shape[0], group.shape[1]
+    wl = w_a.shape[2]
+    hw = width // 4
+    per_t = hw // head
+
+    loads = [pltpu.make_async_copy(gath.at[:, :, pl.ds(wl * i, wl)], ref, sem.at[i])
+             for i, ref in enumerate((w_a, w_u, w_d))]
+    loads.append(pltpu.make_async_copy(gath.at[:, :, pl.ds(3 * wl, 16)], small, sem.at[3]))
+    for d in (loads[3], loads[0], loads[1], loads[2]):
+        d.start()
+
+    meta = meta_ref[t_me // 2]
+    start, e0, e1 = row_facts(meta, n_n)
+    order = pick_row(meta[0:4, :], c)
+
+    def half_rows(rows):
+        nat = wrap(start + rows.start + lax.broadcasted_iota(jnp.int32, (rows.size, 1), 0), n_n)
+        sel = (lax.broadcasted_iota(jnp.int32, (rows.size, n_n), 1) == nat).astype(F32).astype(BF)
+        xh[rows, :] = mm(sel, group[0]).astype(BF)
+    chunks(s_n, half_rows, 128)
+
+    def quarter_rows(rows):
+        nat = wrap(start + f * r_n + rows.start + lax.broadcasted_iota(jnp.int32, (rows.size, 1), 0), n_n)
+        sel = (order == nat).astype(F32).astype(BF)
+        dy[rows, :] = mm(sel, group[1])
+    chunks(r_n, quarter_rows, 128)
+
+    mine = pl.ds(pl.multiple_of(f * r_n, r_n), r_n)
+    loads[3].wait()
+    for t in range(4):
+        bias[t] = jnp.sum(small[t].astype(F32), axis=0)
+    vec = bias[0]
+    bo, mg, ms, bd, eg, es = (vec[i:i + 1, :] for i in range(6))
+    loads[0].wait()
+
+    nat_row = wrap(start + lax.broadcasted_iota(jnp.int32, (1, s_n), 1), n_n)
+    seg_row = (nat_row >= e0).astype(jnp.int32) + (nat_row >= e1).astype(jnp.int32)
+
+    def forward_t(t):
+        row6 = bias[t][6:7, :]
+        qkv[t] = (mm(xh[...], block_mat(w_a, t)) + row6).astype(BF)
+        q3 = qkv[t, mine, :]
+        kv = qkv[t]
+        outs = []
+        for h in range(per_t):
+            lo = hw + h * head
+            sbuf[...] = mm_rt(q3[:, lo:lo + head], kv[:, lo + hw:lo + hw + head])
+            at = t * per_t + h
+
+            def soft(rows):
+                nat = wrap(start + f * r_n + rows.start + lax.broadcasted_iota(jnp.int32, (rows.size, 1), 0), n_n)
+                seg = (nat >= e0).astype(jnp.int32) + (nat >= e1).astype(jnp.int32)
+                s = jnp.where(seg == seg_row, sbuf[rows, :] * 0.125, MASKED)
+                p = jnp.exp(s - jnp.max(s, axis=1, keepdims=True))
+                p = p / jnp.sum(p, axis=1, keepdims=True)
+                probs[at, rows, :] = p
+                pb[rows, :] = p.astype(BF)
+            chunks(r_n, soft)
+            outs.append(mm(pb[...], kv[:, lo + 2 * hw:lo + 2 * hw + head]).astype(BF))
+        outs.append(jnp.zeros((r_n, width - hw), BF))
+        op_out[t] = jnp.concatenate(outs, axis=1)
+    each_t(forward_t)
+
+    xm_out[...] = xh[mine, :]
+    acc[...] = xm_out[...].astype(F32) + bo
+
+    def out_t(t):
+        acc[...] += mm_rt(op_out[t], block_mat(w_a, t))
+    each_t(out_t)
+
+    def norm_rows(u):
+        centre = u - jnp.mean(u, axis=-1, keepdims=True)
+        inv = lax.rsqrt(jnp.mean(centre * centre, axis=-1, keepdims=True) + EPS)
+        return centre * inv, inv
+
+    def first_norm(rows):
+        n, inv = norm_rows(acc[rows, :])
+        n1[rows, :] = n
+        inv1[rows, :] = jnp.broadcast_to(inv, (rows.size, 128))
+        m = n * mg + ms
+        mid[rows, :] = m
+        midb[rows, :] = m.astype(BF)
+        acc[rows, :] = m + bd
+    chunks(r_n, first_norm)
+
+    loads[1].wait()
+    loads[2].wait()
+
+    def ffn_t(t):
+        row7 = bias[t][7:8, :]
+        big[...] = mm(midb[...], block_mat(w_u, t))
+
+        def gelu(rows):
+            u = big[rows, :] + row7
+            cdf = 0.5 * (1.0 + lax.erf(u * 0.7071067811865476))
+            pdf = 0.3989422804014327 * jnp.exp(-0.5 * u * u)
+            act[t, rows, :] = (u * cdf).astype(BF)
+            gelu_d[t, rows, :] = cdf + u * pdf
+        chunks(r_n, gelu, 16)
+        acc[...] += mm_rt(act[t], block_mat(w_d, t))
+    each_t(ffn_t)
+
+    vec_out[...] = jnp.zeros_like(vec_out)
+
+    def add_vec(i, v):
+        vec_out[i] += jnp.sum(v.reshape(-1, 8, v.shape[1]), axis=0)
+
+    def second_norm(rows):
+        n, inv = norm_rows(acc[rows, :])
+        y_out[rows, :] = (n * eg + es).astype(BF)
+        g = dy[rows, :]
+        e = g * eg
+        d = (e - jnp.mean(e, axis=-1, keepdims=True) - n * jnp.mean(e * n, axis=-1, keepdims=True)) * inv
+        add_vec(3, d)
+        add_vec(4, g * n)
+        add_vec(5, g)
+        df[rows, :] = d.astype(BF)
+        acc[rows, :] = d
+    chunks(r_n, second_norm)
+
+    def ffn_back_t(t):
+        big[...] = mm(df[...], block_mat(w_d, t))
+
+        def times(rows):
+            d = (big[rows, :] * gelu_d[t, rows, :]).astype(BF)
+            n2[rows, :] = d
+            add_vec(8 + t, d.astype(F32))
+        chunks(r_n, times)
+        acc[...] += mm_rt(n2[...], block_mat(w_u, t))
+        g_d[t] = mm_lt(df[...], act[t]).astype(BF).reshape(g_d.shape[1:])
+        g_u[t] = mm_lt(midb[...], n2[...]).astype(BF).reshape(g_u.shape[1:])
+    each_t(ffn_back_t)
+    stores = [pltpu.make_async_copy(g_u, gg.at[:, :, pl.ds(wl, wl)], sem.at[4]),
+              pltpu.make_async_copy(g_d, gg.at[:, :, pl.ds(2 * wl, wl)], sem.at[5])]
+    for d in stores:
+        d.start()
+
+    def first_norm_back(rows):
+        g, n = acc[rows, :], n1[rows, :]
+        e = g * mg
+        d = (e - jnp.mean(e, axis=-1, keepdims=True) - n * jnp.mean(e * n, axis=-1, keepdims=True)) * inv1[rows, :][:, 0:1]
+        add_vec(0, d)
+        add_vec(1, g * n)
+        add_vec(2, g)
+        dr1_out[rows, :] = d
+        da_out[rows, :] = d.astype(BF)
+    chunks(r_n, first_norm_back)
+
+    def attn_back_t(t):
+        do = mm(da_out[...], block_mat(w_a, t)).astype(BF)
+        q3 = qkv[t, mine, :]
+        kv = qkv[t]
+        dqs, dks, dvs = [], [], []
+        for h in range(per_t):
+            lo = hw + h * head
+            at = t * per_t + h
+            do_h = do[:, h * head:(h + 1) * head]
+            sbuf[...] = mm_rt(do_h, kv[:, lo + 2 * hw:lo + 2 * hw + head])
+
+            p, d = probs[at], sbuf[...]
+            pb[...] = (p * (d - jnp.sum(p * d, axis=1, keepdims=True))).astype(BF)
+            pb2[...] = p.astype(BF)
+            dvs.append(mm_lt(pb2[...], do_h))
+            dqs.append(mm(pb[...], kv[:, lo + hw:lo + hw + head]) * 0.125)
+            dks.append(mm_lt(pb[...], q3[:, lo:lo + head]) * 0.125)
+        dq_out[t] = jnp.concatenate([a.astype(BF) for a in dqs], axis=1)
+        dkv_out[t] = jnp.concatenate([a.astype(BF) for a in dks + dvs], axis=1)
+    each_t(attn_back_t)
+    for d in stores:
+        d.wait()
+
+
+def k1(gath, meta, group, head):
+    n_t, n_fc, rows, width = gath.shape
+    wl = (rows - 16) // 3
+    n_n = group.shape[1]
+    s_n, r_n = n_n // 2, n_n // 4
+    hw = width // 4
+    heads = width // head
+    v = pltpu.VMEM
+    sds = jax.ShapeDtypeStruct
+    vm = pl.BlockSpec(memory_space=pltpu.VMEM)
+    any_ = pl.BlockSpec(memory_space=pl.ANY)
+    wshape = (n_t, n_fc, wl, width)
+    return pl.pallas_call(
+        functools.partial(k1_kernel, head),
+        out_shape=(sds(gath.shape, BF), sds((n_t, r_n, hw), BF), sds((n_t, s_n, 2 * hw), BF), sds((r_n, width), BF),
+                   sds((r_n, width), BF), sds((n_t, r_n, width), BF), sds((r_n, width), F32), sds((r_n, width), BF),
+                   sds((16, 8, width), F32)),
+        in_specs=[any_, vm, vm],
+        out_specs=(any_,) + (vm,) * 8,
+        scratch_shapes=[
+            v(wshape, BF), v(wshape, BF), v(wshape, BF), v((n_t, n_fc, 16, width), BF),
+            v((s_n, width), BF), v((r_n, width), F32), v((n_t, s_n, width), BF), v((heads, r_n, s_n), F32),
+            v((r_n, s_n), F32), v((r_n, s_n), BF), v((r_n, s_n), BF), v((r_n, width), F32), v((r_n, width), F32), v((r_n, width), BF),
+            v((r_n, width), F32), v((r_n, 128), F32), v((n_t, r_n, width), F32), v((n_t, r_n, width), BF),
+            v((r_n, width), BF), v((r_n, width), BF), v((r_n, width), F32), v((n_t, 16, width), F32),
+            v(wshape, BF), v(wshape, BF), pltpu.SemaphoreType.DMA((6,))],
+        compiler_params=pltpu.CompilerParams(vmem_limit_bytes=VMEM_MAX),
+        name="layer_main",
+    )(gath, meta, group)
+
+
+def k2_kernel(gath, meta_ref, dq, dkv, dkv_in, xm, da, op, dr1, y, vec, gg_in, gg, place,
+              w_a, g_a, g_s, acc, dqkv, sem):
+    f, c, t_me = lax.axis_index("fsdp"), lax.axis_index("ctx"), lax.axis_index("tp")
+    r_n, width = xm.shape
+    n_n = place.shape[1]
+    wl = w_a.shape[2]
+    hw = width // 4
+    load = pltpu.make_async_copy(gath.at[:, :, pl.ds(0, wl)], w_a, sem.at[0])
+    load.start()
+    meta = meta_ref[t_me // 2]
+    start, _, _ = row_facts(meta, n_n)
+    order = pick_row(meta[8:12, :], c)
+    nat = wrap(start + f * r_n + lax.broadcasted_iota(jnp.int32, (r_n, 1), 0), n_n)
+    mine = pl.ds(pl.multiple_of(f * r_n, r_n), r_n)
+    acc[...] = dr1[...]
+    load.wait()
+    lane16 = lax.broadcasted_iota(jnp.int32, (16, width), 0)
+    sums = jnp.sum(vec[...], axis=1)
+
+    def grads_t(t):
+        both = (dkv[t, mine, :].astype(F32) + dkv_in[t].astype(F32)).astype(BF)
+        dqkv[...] = jnp.concatenate([jnp.zeros((r_n, hw), BF), dq[t], both], axis=1)
+        d = dqkv[...]
+        acc[...] += mm_rt(d, block_mat(w_a, t))
+        g_a[t] = (mm_lt(xm[...], d) + mm_lt(da[...], op[t])).astype(BF).reshape(g_a.shape[1:])
+        base = jnp.where(lane16 < 6, sums, 0.0)
+        base = base + jnp.where(lane16 == 6, jnp.sum(d.astype(F32), axis=0, keepdims=True), 0.0)
+        base = base + jnp.where(lane16 == 7, jnp.sum(vec[8 + t], axis=0, keepdims=True), 0.0)
+        g_s[t] = jnp.broadcast_to(base.astype(BF)[None], g_s.shape[1:])
+    each_t(grads_t)
+    stores = [pltpu.make_async_copy(g_a, gg.at[:, :, pl.ds(0, wl)], sem.at[1]),
+              pltpu.make_async_copy(g_s, gg.at[:, :, pl.ds(3 * wl, 16)], sem.at[2])]
+    for d in stores:
+        d.start()
+    pick = (order == nat).astype(F32).astype(BF)
+    place[0] = mm_lt(pick, y[...]).astype(BF)
+    lane = lax.broadcasted_iota(jnp.int32, (1, n_n), 1)
+    block = n_n // 16
+    at = ((lane // block) % 4) * (4 * block) + (lane // (4 * block)) * block + lane % block
+    pick2 = (at == nat).astype(F32).astype(BF)
+    place[1] = mm_lt(pick2, acc[...].astype(BF)).astype(BF)
+    for d in stores:
+        d.wait()
+
+
+def k2(gath, meta, dq, dkv, dkv_in, xm, da, op, dr1, y, vec, gg):
+    n_t, n_fc, rows, width = gath.shape
+    wl = (rows - 16) // 3
+    r_n = xm.shape[0]
+    n_n = 4 * r_n
+    v = pltpu.VMEM
+    vm = pl.BlockSpec(memory_space=pltpu.VMEM)
+    any_ = pl.BlockSpec(memory_space=pl.ANY)
+    wshape = (n_t, n_fc, wl, width)
+    return pl.pallas_call(
+        k2_kernel,
+        out_shape=(jax.ShapeDtypeStruct(gg.shape, BF), jax.ShapeDtypeStruct((2, n_n, width), BF)),
+        in_specs=[any_] + [vm] * 10 + [any_],
+        out_specs=(any_, vm),
+        input_output_aliases={11: 0},
+        scratch_shapes=[v(wshape, BF), v(wshape, BF), v((n_t, n_fc, 16, width), BF), v((r_n, width), F32),
+                        v((r_n, width), BF), pltpu.SemaphoreType.DMA((3,))],
+        compiler_params=pltpu.CompilerParams(vmem_limit_bytes=VMEM_MAX),
+        name="layer_tail",
+    )(gath, meta, dq, dkv, dkv_in, xm, da, op, dr1, y, vec, gg)
+
+
+def comm_in_kernel(cut, tok, cot, pack, meta, gath, group, meta_all, held, *sems):
+    (sem_l, s_e, r_e, s_xg, r_xg, s_xf, s_z, r_z, s_x0, r_x0, s_y0, r_y0, s_y1, r_y1, s_x1, r_x1,
+     s_c, r_c, s_c0, r_c0, s_c1, r_c1, s_m, r_m) = sems
+    f, c, t = lax.axis_index("fsdp"), lax.axis_index("ctx"), lax.axis_index("tp")
+    rows = pack.shape[0]
+    h0, h1 = pl.ds(0, cut), pl.ds(cut, rows - cut)
+    slot = f * 4 + c
+    partner = (1 - f, c, t)
+    cx = c + 1 - 2 * (c % 2)
+    cy = (c + 2) % 4
+    cd = (cx + 2) % 4
+    x_nb, y_nb = (f, cx, t), (f, cy, t)
+    near, far = 1 + f, 3 * f
+    is_near, is_far = t == near, t == far
+    receiver = (t // 2) == f
+
+    barrier = pltpu.get_barrier_semaphore()
+    peers = [partner] + [(f, (c + i) % 4, t) for i in (1, 2, 3)] + [(f, c, (t + i) % 4) for i in (1, 2, 3)]
+    for p in peers:
+        pl.semaphore_signal(barrier, inc=1, device_id=p, device_id_type=MESH)
+    pl.semaphore_wait(barrier, len(peers))
+
+    pending = []
+
+    def send(src, dst, ssem, rsem, dev, pred=None):
+        d = pltpu.make_async_remote_copy(src_ref=src, dst_ref=dst, send_sem=ssem, recv_sem=rsem,
+                                         device_id=dev, device_id_type=MESH)
+        if pred is None:
+            d.start()
+        else:
+            pl.when(pred)(d.start)
+        pending.append((pred, d))
+
+    def arrived(dst, rsem, pred=None):
+        d = pltpu.make_async_remote_copy(src_ref=dst, dst_ref=dst, send_sem=s_e.at[0, 0], recv_sem=rsem,
+                                         device_id=partner, device_id_type=MESH)
+        if pred is None:
+            d.wait_recv()
+        else:
+            pl.when(pred)(d.wait_recv)
+
+    def both(a, b):
+        return b if a is None else jnp.logical_and(a, b)
+
+    def first_sends(ten, ref):
+        for i in (1, 2, 3):
+            to = (c + i) % 4
+            send(ref.at[to], held.at[ten, c], s_e.at[ten, i], r_e.at[ten, c], (f, to, t))
+
+    first_sends(0, tok)
+    local = [pltpu.make_async_copy(tok.at[c], held.at[0, c], sem_l.at[0]),
+             pltpu.make_async_copy(cot.at[c], held.at[1, c], sem_l.at[1]),
+             pltpu.make_async_copy(pack, gath.at[t, slot], sem_l.at[2])]
+    for d in local:
+        d.start()
+    send(meta, meta_all.at[f], s_m.at[0], r_m.at[0], partner)
+    own_meta = pltpu.make_async_copy(meta, meta_all.at[f], sem_l.at[5])
+    own_meta.start()
+
+    def have_column(src, tt, pred=None):
+        send(src.at[h0], gath.at[tt, slot, h0], s_x0.at[tt], r_x0.at[tt], x_nb, pred)
+        send(src.at[h1], gath.at[tt, slot, h1], s_y1.at[tt], r_y1.at[tt], y_nb, pred)
+        send(src.at[h0], gath.at[tt, slot, h0], s_y0.at[0, tt], r_y0.at[0, tt], y_nb, pred)
+        send(src.at[h1], gath.at[tt, slot, h1], s_x1.at[0, tt], r_x1.at[0, tt], x_nb, pred)
+        send(src, gath.at[tt, slot], s_c.at[tt], r_c.at[tt], partner, pred)
+
+    send(pack, gath.at[t, slot], s_z.at[0, t], r_z.at[t], (f, c, (t + 1) % 4), t < 3)
+    send(pack, gath.at[t, slot], s_z.at[1, t], r_z.at[t], (f, c, (t + 3) % 4), t > 0)
+    have_column(pack, t)
+    first_sends(1, cot)
+
+    def second_sends(ten):
+        local[ten].wait()
+        for i in (1, 2, 3):
+            frm = (c + i) % 4
+            arrived(held.at[ten, frm], r_e.at[ten, frm])
+        blk = held.at[ten]
+        dst = group.at[ten, :, t]
+        to = jnp.where(is_near, far, near)
+        send(blk, dst, s_xg.at[ten, t], r_xg.at[ten, t], (f, c, to))
+        send(blk, dst, s_xf.at[ten, 0, t], r_xg.at[ten, t], partner, receiver)
+        keep = pltpu.make_async_copy(blk, dst, sem_l.at[3 + ten])
+        pl.when(receiver)(keep.start)
+        return keep
+
+    keeps = [second_sends(0)]
+
+    def z_step(d):
+        for sign in (-1, 1):
+            tt = t + sign * d
+            there = tt >= 0 if sign < 0 else tt <= 3
+            tt = (tt + 4) % 4
+            arrived(gath.at[tt, slot], r_z.at[tt], there)
+            on = t < 3 if sign < 0 else t > 0
+            nxt = (t + 1) % 4 if sign < 0 else (t + 3) % 4
+            if d < 3:
+                send(gath.at[tt, slot], gath.at[tt, slot], s_z.at[(1 - sign) // 2 * 0 + (0 if sign < 0 else 1), tt],
+                     r_z.at[tt], (f, c, nxt), both(there, on))
+            have_column(gath.at[tt, slot], tt, there)
+
+    def relay(ten):
+        for i in (1, 2, 3):
+            tt = (t + i) % 4
+            arrived(group.at[ten, :, tt], r_xg.at[ten, tt], receiver)
+            send(group.at[ten, :, tt], group.at[ten, :, tt], s_xg.at[ten, tt], r_xg.at[ten, tt], (f, c, far),
+                 jnp.logical_and(is_near, tt != far))
+            send(group.at[ten, :, tt], group.at[ten, :, tt], s_xf.at[ten, 0, tt], r_xg.at[ten, tt], partner, receiver)
+
+    z_step(1)
+    relay(0)
+    keeps.append(second_sends(1))
+    z_step(2)
+    z_step(3)
+    relay(1)
+
+    columns = [(t, None)]
+    for d in (1, 2, 3):
+        columns.append(((t - d + 4) % 4, t - d >= 0))
+        columns.append(((t + d) % 4, t + d <= 3))
+    for tt, pred in columns:
+        a = gath.at[tt, f * 4 + cx, h0]
+        arrived(a, r_x0.at[tt], pred)
+        send(a, a, s_y0.at[1, tt], r_y0.at[1, tt], y_nb, pred)
+        send(a, a, s_c0.at[0, tt], r_c0.at[0, tt], partner, pred)
+        b = gath.at[tt, f * 4 + cy, h1]
+        arrived(b, r_y1.at[tt], pred)
+        send(b, b, s_x1.at[1, tt], r_x1.at[1, tt], x_nb, pred)
+        send(b, b, s_c1.at[0, tt], r_c1.at[0, tt], partner, pred)
+    for step in (0, 1):
+        for tt, pred in columns:
+            a = gath.at[tt, f * 4 + (cy if step == 0 else cd), h0]
+            arrived(a, r_y0.at[step, tt], pred)
+            send(a, a, s_c0.at[1 + step, tt], r_c0.at[1 + step, tt], partner, pred)
+            b = gath.at[tt, f * 4 + (cx if step == 0 else cd), h1]
+            arrived(b, r_x1.at[step, tt], pred)
+            send(b, b, s_c1.at[1 + step, tt], r_c1.at[1 + step, tt], partner, pred)
+
+    other = (1 - f) * 4
+    for tt in range(4):
+        arrived(gath.at[tt, other + c], r_c.at[tt])
+        for j, cc in enumerate((cx, cy, cd)):
+            arrived(gath.at[tt, other + cc, h0], r_c0.at[j, tt])
+        for j, cc in enumerate((cy, cx, cd)):
+            arrived(gath.at[tt, other + cc, h1], r_c1.at[j, tt])
+    for ten in (0, 1):
+        for tt in range(4):
+            arrived(group.at[ten, :, tt], r_xg.at[ten, tt], jnp.logical_not(receiver))
+        pl.when(receiver)(keeps[ten].wait)
+    arrived(meta_all.at[1 - f], r_m.at[0])
+    own_meta.wait()
+    local[2].wait()
+    for pred, d in pending:
+        if pred is None:
+            d.wait_send()
+        else:
+            pl.when(pred)(d.wait_send)
+
+
+def comm_in(tok, cot, pack, meta, cut):
+    dma = pltpu.SemaphoreType.DMA
+    rows, width = pack.shape
+    own = tok.shape[1]
+    sems = [dma((6,)), dma((2, 4)), dma((2, 4)), dma((2, 4)), dma((2, 4)), dma((2, 1, 4)), dma((2, 4)), dma((4,)),
+            dma((4,)), dma((4,)), dma((2, 4)), dma((2, 4)), dma((4,)), dma((4,)), dma((2, 4)), dma((2, 4)),
+            dma((4,)), dma((4,)), dma((3, 4)), dma((3, 4)), dma((3, 4)), dma((3, 4)), dma((1,)), dma((1,))]
+    any_ = pl.BlockSpec(memory_space=pl.ANY)
+    return pl.pallas_call(
+        functools.partial(comm_in_kernel, cut),
+        out_shape=(jax.ShapeDtypeStruct((4, 8, rows, width), BF),
+                   jax.ShapeDtypeStruct((2, 4, 4, own, width), BF), jax.ShapeDtypeStruct((2,) + meta.shape, jnp.int32)),
+        in_specs=[any_, any_, pl.BlockSpec(memory_space=pltpu.VMEM), pl.BlockSpec(memory_space=pltpu.VMEM)],
+        out_specs=(any_, any_, any_),
+        scratch_shapes=[pltpu.VMEM((2, 4, own, width), BF)] + sems,
+        compiler_params=pltpu.CompilerParams(collective_id=0, has_side_effects=True),
+        name="comm_in",
+    )(tok, cot, pack, meta)
+
+
+def swap_kernel(dkv, got, ssem, rsem):
+    f, c, t = lax.axis_index("fsdp"), lax.axis_index("ctx"), lax.axis_index("tp")
+    partner = (1 - f, c, t)
+    barrier = pltpu.get_barrier_semaphore()
+    pl.semaphore_signal(barrier, inc=1, device_id=partner, device_id_type=MESH)
+    pl.semaphore_wait(barrier, 1)
+    n = got.shape[1]
+    d = pltpu.make_async_remote_copy(src_ref=dkv.at[:, pl.ds(pl.multiple_of((1 - f) * n, n), n)], dst_ref=got, send_sem=ssem, recv_sem=rsem,
+                                     device_id=partner, device_id_type=MESH)
+    d.start()
+    d.wait()
+
+
+def swap(dkv):
+    n_t, s_n, w = dkv.shape
+    vm = pl.BlockSpec(memory_space=pltpu.VMEM)
+    return pl.pallas_call(
+        swap_kernel, out_shape=jax.ShapeDtypeStruct((n_t, s_n // 2, w), BF), in_specs=[vm], out_specs=vm,
+        scratch_shapes=[pltpu.SemaphoreType.DMA, pltpu.SemaphoreType.DMA],
+        compiler_params=pltpu.CompilerParams(collective_id=1, has_side_effects=True), name="core_swap")(dkv)
+
+
+def comm_out_kernel(cut, gg, place, total, rows_out, own, got0, got1, got2, got3, pl1, pl2, final, *sems):
+    (sem_l, s0, r0, s1, r1, s2, r2, s3, r3, su, ru, s_o, r_o) = sems
+    f, c, t = lax.axis_index("fsdp"), lax.axis_index("ctx"), lax.axis_index("tp")
+    rows = got0.shape[2]
+    h0, h1 = pl.ds(0, cut), pl.ds(cut, rows - cut)
+    partner = (1 - f, c, t)
+    cx = c + 1 - 2 * (c % 2)
+    cy = (c + 2) % 4
+    cd = (cx + 2) % 4
+    x_nb, y_nb = (f, cx, t), (f, cy, t)
+    par = t % 2
+    z_nb = (f, c, t + 1 - 2 * par)
+    to_f, to_t = t // 2, 2 * f + par
+    stays = to_f == f
+
+    barrier = pltpu.get_barrier_semaphore()
+    peers = [partner] + [(f, (c + i) % 4, t) for i in (1, 2, 3)] + [(f, c, (t + i) % 4) for i in (1, 2, 3)]
+    for p in peers:
+        pl.semaphore_signal(barrier, inc=1, device_id=p, device_id_type=MESH)
+
+    @pl.when(jnp.logical_not(stays))
+    def _():
+        for i in range(4):
+            pl.semaphore_signal(barrier, inc=1, device_id=(to_f, (c + i) % 4, to_t), device_id_type=MESH)
+        pl.semaphore_wait(barrier, len(peers) + 4)
+
+    @pl.when(stays)
+    def _():
+        pl.semaphore_wait(barrier, len(peers))
+
+    pending = []
+
+    def send(src, dst, ssem, rsem, dev, pred=None):
+        d = pltpu.make_async_remote_copy(src_ref=src, dst_ref=dst, send_sem=ssem, recv_sem=rsem,
+                                         device_id=dev, device_id_type=MESH)
+        if pred is None:
+            d.start()
+        else:
+            pl.when(pred)(d.start)
+        pending.append((pred, d))
+
+    def arrived(dst, rsem):
+        pltpu.make_async_remote_copy(src_ref=dst, dst_ref=dst, send_sem=su.at[0], recv_sem=rsem,
+                                     device_id=partner, device_id_type=MESH).wait_recv()
+
+    turn = [(t + 2) % 4, (t + 1) % 4, (t + 3) % 4, t]
+    own_base = pl.ds(pl.multiple_of(f * 4, 4), 4)
+    loads = []
+    for i, tt in enumerate(turn):
+        d = pltpu.make_async_copy(gg.at[tt, own_base], own.at[tt], sem_l.at[i])
+        d.start()
+        loads.append(d)
+    lo = pl.multiple_of(2 * f, 2)
+    hi = pl.multiple_of(2 - 2 * f, 2)
+    send(place.at[:, pl.ds(hi, 2)], pl1, su.at[0], ru.at[0], partner)
+    for tt in turn:
+        for i in (1, 2, 3, 0):
+            cc = (c + i) % 4
+            send(gg.at[tt, 4 * (1 - f) + cc], got0.at[tt, cc], s0.at[tt, cc], r0.at[tt, cc], partner)
+
+    def add_into(dst, src, total_rows, step=16):
+        def go(i, _):
+            r = pl.ds(pl.multiple_of(i * step, step), step)
+            dst[r, :] = dst[r, :] + src[r, :]
+            return 0
+        lax.fori_loop(0, total_rows // step, go, 0, unroll=2 if (total_rows // step) % 2 == 0 else 1)
+
+    blocks = pl1.shape[2]
+    arrived(pl1, ru.at[0])
+    for ten in range(2):
+        for k in (0, 1):
+            for j in range(4):
+                add_into(pl1.at[ten, k, j], place.at[ten, lo + k, j], pl1.shape[3])
+    send(pl1.at[:, 1 - par], pl2, su.at[1], ru.at[1], z_nb)
+
+    for i, tt in enumerate(turn):
+        loads[i].wait()
+        for k in (1, 2, 3, 0):
+            cc = (c + k) % 4
+            arrived(got0.at[tt, cc], r0.at[tt, cc])
+            add_into(own.at[tt, cc], got0.at[tt, cc], rows)
+        for k, cc in enumerate((cy, cd)):
+            send(own.at[tt, cc, h0], got1.at[tt, k, h0], s1.at[0, k, tt], r1.at[0, k, tt], y_nb)
+        for k, cc in enumerate((cx, cd)):
+            send(own.at[tt, cc, h1], got1.at[tt, k, h1], s1.at[1, k, tt], r1.at[1, k, tt], x_nb)
+
+    arrived(pl2, ru.at[1])
+    for ten in range(2):
+        for j in range(4):
+            add_into(pl2.at[ten, j], pl1.at[ten, par, j], pl2.shape[2])
+    moves = []
+    for ten in range(2):
+        for i in range(4):
+            cc = (c + i) % 4
+            src, dst = pl2.at[ten, cc], rows_out.at[ten, c]
+            away = jnp.logical_not(stays) if i == 0 else None
+            send(src, dst, s_o.at[ten, i], r_o.at[ten, c], (to_f, cc, to_t), away)
+        moves.append(pltpu.make_async_copy(pl2.at[ten, c], rows_out.at[ten, c], sem_l.at[4 + ten]))
+        pl.when(stays)(moves[ten].start)
+
+    def half_add(dst, src, off, n):
+        def go(i, _):
+            r = pl.ds(pl.multiple_of(off + i * 16, 16), 16)
+            dst[r, :] = dst[r, :] + src[r, :]
+            return 0
+        lax.fori_loop(0, n // 16, go, 0)
+
+    for tt in turn:
+        arrived(got1.at[tt, 0, h0], r1.at[0, 0, tt])
+        half_add(own.at[tt, c], got1.at[tt, 0], 0, cut)
+        arrived(got1.at[tt, 1, h0], r1.at[0, 1, tt])
+        half_add(own.at[tt, cx], got1.at[tt, 1], 0, cut)
+        arrived(got1.at[tt, 0, h1], r1.at[1, 0, tt])
+        half_add(own.at[tt, c], got1.at[tt, 0], cut, rows - cut)
+        arrived(got1.at[tt, 1, h1], r1.at[1, 1, tt])
+        half_add(own.at[tt, cy], got1.at[tt, 1], cut, rows - cut)
+        send(own.at[tt, cx, h0], got2.at[tt, h0], s2.at[0, tt], r2.at[0, tt], x_nb)
+        send(own.at[tt, cy, h1], got2.at[tt, h1], s2.at[1, tt], r2.at[1, tt], y_nb)
+
+    for i, tt in enumerate(turn):
+        arrived(got2.at[tt, h0], r2.at[0, tt])
+        arrived(got2.at[tt, h1], r2.at[1, tt])
+        add_into(own.at[tt, c], got2.at[tt], rows)
+        if i < 3:
+            send(own.at[tt, c], got3.at[t], s3.at[tt], r3.at[t], (f, c, tt))
+    keep = pltpu.make_async_copy(own.at[t, c], got3.at[t], sem_l.at[6])
+    keep.start()
+    keep.wait()
+    for tt in turn[:3]:
+        arrived(got3.at[tt], r3.at[tt])
+
+    def go(i, _):
+        r = pl.ds(pl.multiple_of(i * 16, 16), 16)
+        a, b, e, g = (got3[k, r, :].astype(F32) for k in range(4))
+        total[r, :] = ((a + b) + e) + g
+        return 0
+    lax.fori_loop(0, rows // 16, go, 0)
+
+    for ten in range(2):
+        for i in range(4):
+            cc = (c + i) % 4
+            if i == 0:
+                @pl.when(jnp.logical_not(stays))
+                def _(ten=ten, cc=cc):
+                    arrived(rows_out.at[ten, cc], r_o.at[ten, cc])
+                pl.when(stays)(moves[ten].wait)
+            else:
+                arrived(rows_out.at[ten, cc], r_o.at[ten, cc])
+    for pred, d in pending:
+        if pred is None:
+            d.wait_send()
+        else:
+            pl.when(pred)(d.wait_send)
+
+
+def comm_out(gg, place, cut):
+    dma = pltpu.SemaphoreType.DMA
+    n_t, n_fc, rows, width = gg.shape
+    n_n = place.shape[1]
+    block = n_n // 16
+    place = place.reshape(2, 4, 4, block, width)
+    v = pltpu.VMEM
+    vm = pl.BlockSpec(memory_space=pltpu.VMEM)
+    any_ = pl.BlockSpec(memory_space=pl.ANY)
+    return pl.pallas_call(
+        functools.partial(comm_out_kernel, cut),
+        out_shape=(jax.ShapeDtypeStruct((rows, width), F32), jax.ShapeDtypeStruct((2, 4, block, width), BF)),
+        in_specs=[any_, vm],
+        out_specs=(vm, vm),
+        scratch_shapes=[v((4, 4, rows, width), BF), v((4, 4, rows, width), BF), v((4, 2, rows, width), BF),
+                        v((4, rows, width), BF), v((4, rows, width), BF), v((2, 2, 4, block, width), BF),
+                        v((2, 4, block, width), BF), v((8, 128), F32),
+                        dma((7,)), dma((4, 4)), dma((4, 4)), dma((2, 2, 4)), dma((2, 2, 4)), dma((2, 4)), dma((2, 4)),
+                        dma((4,)), dma((4,)), dma((2,)), dma((2,)), dma((2, 4)), dma((2, 4))],
+        compiler_params=pltpu.CompilerParams(collective_id=2, has_side_effects=True, vmem_limit_bytes=62 * 1024 * 1024),
+        name="comm_out",
+    )(gg, place)
+
+
+def quad_body(tokens_in, cotangent, seq_lengths, row_order, w_query, b_query, w_key, w_value, b_value,
+              w_out, b_out, mid_gain, mid_shift, w_up, b_up, w_down, b_down, end_gain, end_shift):
+    f, c = lax.axis_index("fsdp"), lax.axis_index("ctx")
+    fc = f * 4 + c
+    own, width = tokens_in.shape[1:]
+    wl = w_query.shape[0]
+    heads_l, head_l = b_query.shape
+    head = head_l * 8
+    up_l = b_up.shape[1]
+    hw = width // 4
+    mat_a = jnp.concatenate([w_out, w_query, w_key, w_value], axis=1)
+
+    vecs = jnp.stack([b_out, mid_gain, mid_shift, b_down, end_gain, end_shift])
+    col = lax.broadcasted_iota(jnp.int32, (1, width), 1)
+    row_v = jnp.where(col // wl == fc, jnp.tile(vecs, (1, 8)), 0)
+    part = (col % head) // head_l == fc
+    three = jnp.stack([jnp.zeros_like(b_query), b_query, jnp.zeros_like(b_query), b_value])
+    row_a = jnp.where(part, jnp.tile(three, (1, 1, 8)).reshape(1, width), 0)
+    row_u = jnp.where((col % (8 * up_l)) // up_l == fc, jnp.tile(b_up, (1, 8)).reshape(1, width), 0)
+    small = jnp.concatenate([row_v, row_a, row_u, jnp.zeros((8, width), BF)], axis=0)
+    pack = jnp.concatenate([mat_a, w_up, w_down, small], axis=0)
+
+    order = row_order[:, 0]
+    n_n = order.shape[1]
+    moved = order.reshape(4, 4, 4, own).transpose(0, 2, 1, 3).reshape(4, n_n)
+    lens = jnp.pad(seq_lengths[:, 0].reshape(1, -1), ((0, 3), (0, n_n - 12)))
+    meta_own = jnp.concatenate([order, lens, moved, jnp.zeros((4, n_n), jnp.int32)], axis=0)
+
+    cut = (pack.shape[0] // 32) * 16
+    gath, group, meta = comm_in(tokens_in, cotangent, pack, meta_own, cut)
+    group = group.reshape(2, n_n, width)
+    gg, dq, dkv, xm, da, op, dr1, y, vec = k1(gath, meta, group, head)
+    dkv_in = swap(dkv)
+    gg, place = k2(gath, meta, dq, dkv, dkv_in, xm, da, op, dr1, y, vec, gg)
+    total, rows = comm_out(gg, place, cut)
+
+    g_a, g_up, g_down = total[:wl], total[wl:2 * wl], total[2 * wl:3 * wl]
+    sv = lax.dynamic_slice(total[3 * wl:3 * wl + 6], (0, fc * wl), (6, wl))
+    ba = total[3 * wl + 6].reshape(4, heads_l, head)
+    gb = lax.dynamic_slice(ba, (0, 0, fc * head_l), (4, heads_l, head_l))
+    gu = lax.dynamic_slice(total[3 * wl + 7].reshape(heads_l, -1), (0, fc * up_l), (heads_l, up_l))
+    return (rows[0], rows[1], g_a[:, hw:2 * hw], gb[1], g_a[:, 2 * hw:3 * hw], g_a[:, 3 * hw:], gb[3], g_a[:, :hw],
+            sv[0], sv[1], sv[2], g_up, gu, g_down, sv[3], sv[4], sv[5])
+
+
 def solution(mesh):
     ins, outs = specs()
-    return jax.shard_map(body, mesh=mesh, in_specs=ins, out_specs=outs, check_vma=False)
+    small_mesh = (mesh.shape["fsdp"], mesh.shape["ctx"], mesh.shape["tp"]) == (2, 4, 4)
+    fn = quad_body if small_mesh else body
+    return jax.shard_map(fn, mesh=mesh, in_specs=ins, out_specs=outs, check_vma=False)

time: 722 us -> 298 us (0.41); the launches traced: 709 us -> 294 us
  waiting for transfers between devices: 299 us -> 0 us
  Pallas kernels: 0 us -> 272 us
  local copies, waits for them, and re-layouts: 189 us -> 18 us
  blocking collectives: 103 us -> 0 us
  matrix products: 73.7 us -> 0 us
  between operations: 16.2 us -> 0.76 us
  other arithmetic: 15.8 us -> 3.21 us
  starting transfers between devices: 11.3 us -> 0 us
    pallas_call x0 -> x5, Pallas kernels: none -> 272 us  [the longest x1 104 us: comm_out(): pl.pallas_call(functools.partial(comm_out_kernel, cut), out_shape=(jax.Sh...]
    reduce_scatter x4 -> x0, waiting for transfers between devices: 214 us -> none  [the longest x1 158 us: body(): lax.psum_scatter(packed_g, ALL, scatter_dimension=0, tiled=True)[0]]
    all_gather x2 -> x0, blocking collectives: 89.9 us -> none  [the longest x1 68.8 us: body(): lax.all_gather(jnp.concatenate(bias, axis=1), ALL, axis=0, tiled=False)]
    dot_general x25 -> x0, matrix products: 67.5 us -> none  [the longest x8 25.9 us: mm(): return jnp.dot(a, b, preferred_element_type=F32)]
    reshape x19 -> x1, local copies, waits for them, and re-layouts: 54.9 us -> 0.09 us  [quad_body(): moved = order.reshape(4, 4, 4, own).transpose(0, 2, 1, 3).reshape(4, n_n)]
    concatenate x4 -> x2, local copies, waits for them, and re-layouts: 54.7 us -> 5.1 us  [the longest x1 5.02 us: quad_body(): pack = jnp.concatenate([mat_a, w_up, w_down, small], axis=0)]
    unnamed x9 -> x0, waiting for transfers between devices: 41 us -> none
    all_gather x3 -> x0, waiting for transfers between devices: 33.2 us -> none  [the longest x1 33.1 us: body(): lax.all_gather(jnp.concatenate(mats, axis=1), ALL, axis=0, tiled=False)]
  transfers between devices with their start and end apart: 11 -> 0, of which waited for: 7 -> 0; matrix products, arithmetic and copies ran while one was open for 34% -> 0% of each run, Pallas kernels for 0% -> 0%
where the time goes in v2:
time: 298 us; the launch traced here: 294 us
  Pallas kernels  272 us (91%)
  local copies, waits for them, and re-layouts  18 us (6%)
  other arithmetic  3.21 us (1%)
    pallas_call x1, Pallas kernels, comm_out(): pl.pallas_call(functools.partial(comm_out_kernel, cut), out_shape=(jax.Sh...  104 us
    pallas_call x1, Pallas kernels, comm_in(): pl.pallas_call(functools.partial(comm_in_kernel, cut), out_shape=(jax.Sha...  85.9 us
    pallas_call x1, Pallas kernels, k1(): pl.pallas_call(functools.partial(k1_kernel, head), out_shape=(sds(gath.sh...  63.5 us
    pallas_call x1, Pallas kernels, k2(): pl.pallas_call(k2_kernel, out_shape=(jax.ShapeDtypeStruct(gg.shape, BF),...  13.9 us

profile of v2, /device:TPU:0, one launch (start us, length us, event | category | flops | bytes accessed | tf_op | source)
XLA Modules:
  0.0 294.1 jit_solution(9814152293031347508)
XLA Ops:
  0.7 0.7 pad_maximum_fusion.1
  1.4 0.1 tile.28
  1.5 0.7 tile.29
  2.2 0.1 tile.30
  2.3 0.8 stack.36
  3.1 0.1 tile.26
  3.2 1.0 pad_maximum_fusion
  4.2 5.0 %concatenate.10.pack = bf16[304,768]{1,0:T(8,128)(2,1)} concatenate(bf16[96,768]{1,0:T(8,128)(2,1)S(1)} %pad_maximum_fusion, bf16[96,768]{1,0:T(8,128)(2,1)} %param.32, bf16[96,768]{1,0:T(8,128)(2,1)} %param.34, bf16[6,768]{1,0:T(8,128)(2,1)S(1)} %broadcast_select_fusion, bf16[1,768]{1,0:T(2,128)(2,1)S(1)} %get-tuple-element.68, bf16[1,768]{1,0:T(2,128)(2,1)S(1)} %get-tuple-element.67, ...), dimensions={0} | concatenate | bytes 933888 | tf_op jit(solution)/shard_map/concatenate | solution.py:935
  9.2 0.8 reduce
  10.0 0.1 reshape_squeeze.13
  10.1 0.1 reshape.298
  10.2 0.7 copy.45
  10.9 0.8 copy.39
  11.7 0.1 reshape_squeeze.12
  11.8 0.1 pad.8.clone
  11.8 0.7 fusion.1.meta
  12.5 85.9 %comm_in.1 = (bf16[4,8,304,768]{3,2,1,0:T(8,128)(2,1)}, bf16[2,4,4,64,768]{4,3,2,1,0:T(8,128)(2,1)}, s32[2,16,1024]{2,1,0:T(8,128)}) custom-call(bf16[4,64,768]{2,1,0:T(8,128)(2,1)} %tok.1, bf16[4,64,768]{2,1,0:T(8,128)(2,1)} %cot.1, bf16[304,768]{1,0:T(8,128)(2,1)} %concatenate.10.pack, s32[16,1024]{1,0:T(8,128)} %fusion.1.meta), custom_call_target="tpu_custom_call" | custom-call | tf_op jit(solution)/shard_map/comm_in/pallas_call | solution.py:702
  98.5 63.5 %layer_main.1 = (bf16[4,8,304,768]{3,2,1,0:T(8,128)(2,1)}, bf16[4,256,192]{2,1,0:T(8,128)(2,1)}, bf16[4,512,384]{2,1,0:T(8,128)(2,1)}, bf16[256,768]{1,0:T(8,128...) custom-call(bf16[4,8,304,768]{3,2,1,0:T(8,128)(2,1)} %get-tuple-elem, ...), custom_call_target="tpu_custom_call" | custom-call | tf_op jit(solution)/shard_map/layer_main/pallas_call | solution.py:450
  161.9 4.8 %core_swap.1.dkv_in = bf16[4,256,384]{2,1,0:T(8,128)(2,1)} custom-call(bf16[4,512,384]{2,1,0:T(8,128)(2,1)} %get-tuple-element.37.dkv), custom_call_target="tpu_custom_call" | custom-call | tf_op jit(solution)/shard_map/core_swap/pallas_call | solution.py:730
  166.8 13.9 %layer_tail.1 = (bf16[4,8,304,768]{3,2,1,0:T(8,128)(2,1)}, bf16[2,1024,768]{2,1,0:T(8,128)(2,1)}) custom-call(bf16[4,8,304,768]{3,2,1,0:T(8,128)(2,1)} %get-tuple-element.33.gath, s32[2,16,1024]{2,1,0:T(8,128)} %get-tuple-element.34.meta_ref, bf16[4,256,192]{2,1,0:T(8,128)(2,1)} %get-tuple-element.36.dq, ...), custom_call_target="tpu_custom_call", output_to_operand_aliasing={{0}: (11, {})} | custom-call | tf_op jit(solution)/shard_map/layer_tail/pallas_call | solution.py:523
  180.7 104.0 %comm_out.1 = (f32[304,768]{1,0:T(8,128)}, bf16[2,4,64,768]{3,2,1,0:T(8,128)(2,1)}) custom-call(bf16[4,8,304,768]{3,2,1,0:T(8,128)(2,1)} %get-tuple-element.45.gg, bf16[2,4,4,64,768]{4,3,2,1,0:T(8,128)(2,1)} %bitcast.42), custom_call_target="tpu_custom_call" | custom-call | tf_op jit(solution)/shard_map/comm_out/pallas_call | solution.py:900
  284.7 2.0 slice_bitcast_fusion
  286.8 1.9 fusion.6
  288.7 1.9 fusion.7
  290.5 0.7 slice.71
  291.3 0.1 constant_dynamic-slice_fusion.1
  291.3 0.5 slice_bitcast_fusion.2
  291.9 0.8 slice_reduce_fusion
  292.7 0.1 reshape_squeeze.14
  292.8 0.7 dynamic-slice_bitcast_fusion
  293.5 0.6 constant_dynamic-slice_fusion
  (10 shorter events, 0.1 us)

commit v3 on v2

--- a/solution.py
+++ b/solution.py
@@ -300,6 +300,8 @@
 
     nat_row = wrap(start + lax.broadcasted_iota(jnp.int32, (1, s_n), 1), n_n)
     seg_row = (nat_row >= e0).astype(jnp.int32) + (nat_row >= e1).astype(jnp.int32)
+    nat_q = wrap(start + f * r_n + lax.broadcasted_iota(jnp.int32, (r_n, 1), 0), n_n)
+    same = ((nat_q >= e0).astype(jnp.int32) + (nat_q >= e1).astype(jnp.int32)) == seg_row
 
     def forward_t(t):
         row6 = bias[t][6:7, :]
@@ -312,15 +314,11 @@
             sbuf[...] = mm_rt(q3[:, lo:lo + head], kv[:, lo + hw:lo + hw + head])
             at = t * per_t + h
 
-            def soft(rows):
-                nat = wrap(start + f * r_n + rows.start + lax.broadcasted_iota(jnp.int32, (rows.size, 1), 0), n_n)
-                seg = (nat >= e0).astype(jnp.int32) + (nat >= e1).astype(jnp.int32)
-                s = jnp.where(seg == seg_row, sbuf[rows, :] * 0.125, MASKED)
-                p = jnp.exp(s - jnp.max(s, axis=1, keepdims=True))
-                p = p / jnp.sum(p, axis=1, keepdims=True)
-                probs[at, rows, :] = p
-                pb[rows, :] = p.astype(BF)
-            chunks(r_n, soft)
+            s = jnp.where(same, sbuf[...] * 0.125, MASKED)
+            p = jnp.exp(s - jnp.max(s, axis=1, keepdims=True))
+            p = p * (1.0 / jnp.sum(p, axis=1, keepdims=True))
+            probs[at] = p
+            pb[...] = p.astype(BF)
             outs.append(mm(pb[...], kv[:, lo + 2 * hw:lo + 2 * hw + head]).astype(BF))
         outs.append(jnp.zeros((r_n, width - hw), BF))
         op_out[t] = jnp.concatenate(outs, axis=1)
@@ -800,24 +798,64 @@
             return 0
         lax.fori_loop(0, total_rows // step, go, 0, unroll=2 if (total_rows // step) % 2 == 0 else 1)
 
-    blocks = pl1.shape[2]
+    def half_add(dst, src, off, n):
+        def go(i, _):
+            r = pl.ds(pl.multiple_of(off + i * 16, 16), 16)
+            dst[r, :] = dst[r, :] + src[r, :]
+            return 0
+        lax.fori_loop(0, n // 16, go, 0)
+
+    def roles(i):
+        return (cy, cx, y_nb, x_nb) if i % 2 == 0 else (cx, cy, x_nb, y_nb)
+
+    def stage1(i):
+        tt = turn[i]
+        ca, cb, a_nb, b_nb = roles(i)
+        loads[i].wait()
+        for k in (1, 2, 3, 0):
+            cc = (c + k) % 4
+            arrived(got0.at[tt, cc], r0.at[tt, cc])
+            add_into(own.at[tt, cc], got0.at[tt, cc], rows)
+        for k, cc in enumerate((ca, cd)):
+            send(own.at[tt, cc, h0], got1.at[tt, k, h0], s1.at[0, k, tt], r1.at[0, k, tt], a_nb)
+        for k, cc in enumerate((cb, cd)):
+            send(own.at[tt, cc, h1], got1.at[tt, k, h1], s1.at[1, k, tt], r1.at[1, k, tt], b_nb)
+
+    def stage2(i):
+        tt = turn[i]
+        ca, cb, a_nb, b_nb = roles(i)
+        arrived(got1.at[tt, 1, h0], r1.at[0, 1, tt])
+        half_add(own.at[tt, cb], got1.at[tt, 1], 0, cut)
+        arrived(got1.at[tt, 1, h1], r1.at[1, 1, tt])
+        half_add(own.at[tt, ca], got1.at[tt, 1], cut, rows - cut)
+        send(own.at[tt, cb, h0], got2.at[tt, h0], s2.at[0, tt], r2.at[0, tt], b_nb)
+        send(own.at[tt, ca, h1], got2.at[tt, h1], s2.at[1, tt], r2.at[1, tt], a_nb)
+        arrived(got1.at[tt, 0, h0], r1.at[0, 0, tt])
+        half_add(own.at[tt, c], got1.at[tt, 0], 0, cut)
+        arrived(got1.at[tt, 0, h1], r1.at[1, 0, tt])
+        half_add(own.at[tt, c], got1.at[tt, 0], cut, rows - cut)
+
+    def stage3(i):
+        tt = turn[i]
+        arrived(got2.at[tt, h0], r2.at[0, tt])
+        arrived(got2.at[tt, h1], r2.at[1, tt])
+        add_into(own.at[tt, c], got2.at[tt], rows)
+        if i < 3:
+            send(own.at[tt, c], got3.at[t], s3.at[tt], r3.at[t], (f, c, tt))
+
+    stage1(0)
+    stage1(1)
     arrived(pl1, ru.at[0])
     for ten in range(2):
         for k in (0, 1):
             for j in range(4):
                 add_into(pl1.at[ten, k, j], place.at[ten, lo + k, j], pl1.shape[3])
     send(pl1.at[:, 1 - par], pl2, su.at[1], ru.at[1], z_nb)
-
-    for i, tt in enumerate(turn):
-        loads[i].wait()
-        for k in (1, 2, 3, 0):
-            cc = (c + k) % 4
-            arrived(got0.at[tt, cc], r0.at[tt, cc])
-            add_into(own.at[tt, cc], got0.at[tt, cc], rows)
-        for k, cc in enumerate((cy, cd)):
-            send(own.at[tt, cc, h0], got1.at[tt, k, h0], s1.at[0, k, tt], r1.at[0, k, tt], y_nb)
-        for k, cc in enumerate((cx, cd)):
-            send(own.at[tt, cc, h1], got1.at[tt, k, h1], s1.at[1, k, tt], r1.at[1, k, tt], x_nb)
+    stage2(0)
+    stage1(2)
+    stage2(1)
+    stage3(0)
+    stage1(3)
 
     arrived(pl2, ru.at[1])
     for ten in range(2):
@@ -833,31 +871,11 @@
         moves.append(pltpu.make_async_copy(pl2.at[ten, c], rows_out.at[ten, c], sem_l.at[4 + ten]))
         pl.when(stays)(moves[ten].start)
 
-    def half_add(dst, src, off, n):
-        def go(i, _):
-            r = pl.ds(pl.multiple_of(off + i * 16, 16), 16)
-            dst[r, :] = dst[r, :] + src[r, :]
-            return 0
-        lax.fori_loop(0, n // 16, go, 0)
-
-    for tt in turn:
-        arrived(got1.at[tt, 0, h0], r1.at[0, 0, tt])
-        half_add(own.at[tt, c], got1.at[tt, 0], 0, cut)
-        arrived(got1.at[tt, 1, h0], r1.at[0, 1, tt])
-        half_add(own.at[tt, cx], got1.at[tt, 1], 0, cut)
-        arrived(got1.at[tt, 0, h1], r1.at[1, 0, tt])
-        half_add(own.at[tt, c], got1.at[tt, 0], cut, rows - cut)
-        arrived(got1.at[tt, 1, h1], r1.at[1, 1, tt])
-        half_add(own.at[tt, cy], got1.at[tt, 1], cut, rows - cut)
-        send(own.at[tt, cx, h0], got2.at[tt, h0], s2.at[0, tt], r2.at[0, tt], x_nb)
-        send(own.at[tt, cy, h1], got2.at[tt, h1], s2.at[1, tt], r2.at[1, tt], y_nb)
-
-    for i, tt in enumerate(turn):
-        arrived(got2.at[tt, h0], r2.at[0, tt])
-        arrived(got2.at[tt, h1], r2.at[1, tt])
-        add_into(own.at[tt, c], got2.at[tt], rows)
-        if i < 3:
-            send(own.at[tt, c], got3.at[t], s3.at[tt], r3.at[t], (f, c, tt))
+    stage2(2)
+    stage3(1)
+    stage2(3)
+    stage3(2)
+    stage3(3)
     keep = pltpu.make_async_copy(own.at[t, c], got3.at[t], sem_l.at[6])
     keep.start()
     keep.wait()

time: 298 us -> 274 us (0.919); the launches traced: 294 us -> 274 us
  Pallas kernels: 272 us -> 252 us
    pallas_call x1, Pallas kernels: 63.5 us -> 46.4 us  [k1(): pl.pallas_call(functools.partial(k1_kernel, head), out_shape=(sds(gath.sh...]
    pallas_call x1, Pallas kernels: 104 us -> 101 us  [comm_out(): pl.pallas_call(functools.partial(comm_out_kernel, cut), out_shape=(jax.Sh...]
where the time goes in v3:
time: 274 us
  Pallas kernels  252 us (92%)
  local copies, waits for them, and re-layouts  18 us (7%)
  other arithmetic  3.21 us (1%)
    pallas_call x1, Pallas kernels, comm_out(): pl.pallas_call(functools.partial(comm_out_kernel, cut), out_shape=(jax.Sh...  101 us
    pallas_call x1, Pallas kernels, comm_in(): pl.pallas_call(functools.partial(comm_in_kernel, cut), out_shape=(jax.Sha...  85.9 us
    pallas_call x1, Pallas kernels, k1(): pl.pallas_call(functools.partial(k1_kernel, head), out_shape=(sds(gath.sh...  46.4 us
    pallas_call x1, Pallas kernels, k2(): pl.pallas_call(k2_kernel, out_shape=(jax.ShapeDtypeStruct(gg.shape, BF),...  13.9 us

profile of v3, /device:TPU:0, one launch (start us, length us, event | category | flops | bytes accessed | tf_op | source)
XLA Modules:
  0.0 273.7 jit_solution(506525908211315300)
XLA Ops:
  0.7 0.7 pad_maximum_fusion.1
  1.4 0.1 tile.28
  1.5 0.7 tile.29
  2.2 0.1 tile.30
  2.3 0.8 stack.36
  3.1 0.1 tile.26
  3.2 1.0 pad_maximum_fusion
  4.2 5.0 %concatenate.10.pack = bf16[304,768]{1,0:T(8,128)(2,1)} concatenate(bf16[96,768]{1,0:T(8,128)(2,1)S(1)} %pad_maximum_fusion, bf16[96,768]{1,0:T(8,128)(2,1)} %param.32, bf16[96,768]{1,0:T(8,128)(2,1)} %param.34, bf16[6,768]{1,0:T(8,128)(2,1)S(1)} %broadcast_select_fusion, bf16[1,768]{1,0:T(2,128)(2,1)S(1)} %get-tuple-element.68, bf16[1,768]{1,0:T(2,128)(2,1)S(1)} %get-tuple-element.67, ...), dimensions={0} | concatenate | bytes 933888 | tf_op jit(solution)/shard_map/concatenate | solution.py:953
  9.2 0.8 reduce
  10.0 0.1 reshape_squeeze.13
  10.1 0.1 reshape.298
  10.2 0.7 copy.45
  10.9 0.8 copy.39
  11.7 0.1 reshape_squeeze.12
  11.8 0.1 pad.8.clone
  11.8 0.7 fusion.1.meta
  12.5 85.9 %comm_in.1 = (bf16[4,8,304,768]{3,2,1,0:T(8,128)(2,1)}, bf16[2,4,4,64,768]{4,3,2,1,0:T(8,128)(2,1)}, s32[2,16,1024]{2,1,0:T(8,128)}) custom-call(bf16[4,64,768]{2,1,0:T(8,128)(2,1)} %tok.1, bf16[4,64,768]{2,1,0:T(8,128)(2,1)} %cot.1, bf16[304,768]{1,0:T(8,128)(2,1)} %concatenate.10.pack, s32[16,1024]{1,0:T(8,128)} %fusion.1.meta), custom_call_target="tpu_custom_call" | custom-call | tf_op jit(solution)/shard_map/comm_in/pallas_call | solution.py:700
  98.5 46.4 %layer_main.1 = (bf16[4,8,304,768]{3,2,1,0:T(8,128)(2,1)}, bf16[4,256,192]{2,1,0:T(8,128)(2,1)}, bf16[4,512,384]{2,1,0:T(8,128)(2,1)}, bf16[256,768]{1,0:T(8,128...) custom-call(bf16[4,8,304,768]{3,2,1,0:T(8,128)(2,1)} %get-tuple-elem, ...), custom_call_target="tpu_custom_call" | custom-call | tf_op jit(solution)/shard_map/layer_main/pallas_call | solution.py:448
  144.9 4.8 %core_swap.1.dkv_in = bf16[4,256,384]{2,1,0:T(8,128)(2,1)} custom-call(bf16[4,512,384]{2,1,0:T(8,128)(2,1)} %get-tuple-element.37.dkv), custom_call_target="tpu_custom_call" | custom-call | tf_op jit(solution)/shard_map/core_swap/pallas_call | solution.py:728
  149.7 13.9 %layer_tail.1 = (bf16[4,8,304,768]{3,2,1,0:T(8,128)(2,1)}, bf16[2,1024,768]{2,1,0:T(8,128)(2,1)}) custom-call(bf16[4,8,304,768]{3,2,1,0:T(8,128)(2,1)} %get-tuple-element.33.gath, s32[2,16,1024]{2,1,0:T(8,128)} %get-tuple-element.34.meta_ref, bf16[4,256,192]{2,1,0:T(8,128)(2,1)} %get-tuple-element.36.dq, ...), custom_call_target="tpu_custom_call", output_to_operand_aliasing={{0}: (11, {})} | custom-call | tf_op jit(solution)/shard_map/layer_tail/pallas_call | solution.py:521
  163.6 100.6 %comm_out.1 = (f32[304,768]{1,0:T(8,128)}, bf16[2,4,64,768]{3,2,1,0:T(8,128)(2,1)}) custom-call(bf16[4,8,304,768]{3,2,1,0:T(8,128)(2,1)} %get-tuple-element.45.gg, bf16[2,4,4,64,768]{4,3,2,1,0:T(8,128)(2,1)} %bitcast.42), custom_call_target="tpu_custom_call" | custom-call | tf_op jit(solution)/shard_map/comm_out/pallas_call | solution.py:918
  264.3 2.0 slice_bitcast_fusion
  266.3 1.9 fusion.6
  268.2 1.9 fusion.7
  270.1 0.7 slice.71
  270.8 0.1 constant_dynamic-slice_fusion.1
  270.9 0.5 slice_bitcast_fusion.2
  271.5 0.8 slice_reduce_fusion
  272.3 0.1 reshape_squeeze.14
  272.4 0.7 dynamic-slice_bitcast_fusion
  273.0 0.6 constant_dynamic-slice_fusion
  (10 shorter events, 0.1 us)

commit v4 on v3

--- a/solution.py
+++ b/solution.py
@@ -393,8 +393,8 @@
         g_d[t] = mm_lt(df[...], act[t]).astype(BF).reshape(g_d.shape[1:])
         g_u[t] = mm_lt(midb[...], n2[...]).astype(BF).reshape(g_u.shape[1:])
     each_t(ffn_back_t)
-    stores = [pltpu.make_async_copy(g_u, gg.at[:, :, pl.ds(wl, wl)], sem.at[4]),
-              pltpu.make_async_copy(g_d, gg.at[:, :, pl.ds(2 * wl, wl)], sem.at[5])]
+    stores = [pltpu.make_async_copy(g_u, gg.at[:, :, pl.ds(0, wl)], sem.at[4]),
+              pltpu.make_async_copy(g_d, gg.at[:, :, pl.ds(wl, wl)], sem.at[5])]
     for d in stores:
         d.start()
 
@@ -447,7 +447,7 @@
     wshape = (n_t, n_fc, wl, width)
     return pl.pallas_call(
         functools.partial(k1_kernel, head),
-        out_shape=(sds(gath.shape, BF), sds((n_t, r_n, hw), BF), sds((n_t, s_n, 2 * hw), BF), sds((r_n, width), BF),
+        out_shape=(sds((n_t, n_fc, 2 * wl, width), BF), sds((n_t, r_n, hw), BF), sds((n_t, s_n, 2 * hw), BF), sds((r_n, width), BF),
                    sds((r_n, width), BF), sds((n_t, r_n, width), BF), sds((r_n, width), F32), sds((r_n, width), BF),
                    sds((16, 8, width), F32)),
         in_specs=[any_, vm, vm],
@@ -462,73 +462,6 @@
         compiler_params=pltpu.CompilerParams(vmem_limit_bytes=VMEM_MAX),
         name="layer_main",
     )(gath, meta, group)
-
-
-def k2_kernel(gath, meta_ref, dq, dkv, dkv_in, xm, da, op, dr1, y, vec, gg_in, gg, place,
-              w_a, g_a, g_s, acc, dqkv, sem):
-    f, c, t_me = lax.axis_index("fsdp"), lax.axis_index("ctx"), lax.axis_index("tp")
-    r_n, width = xm.shape
-    n_n = place.shape[1]
-    wl = w_a.shape[2]
-    hw = width // 4
-    load = pltpu.make_async_copy(gath.at[:, :, pl.ds(0, wl)], w_a, sem.at[0])
-    load.start()
-    meta = meta_ref[t_me // 2]
-    start, _, _ = row_facts(meta, n_n)
-    order = pick_row(meta[8:12, :], c)
-    nat = wrap(start + f * r_n + lax.broadcasted_iota(jnp.int32, (r_n, 1), 0), n_n)
-    mine = pl.ds(pl.multiple_of(f * r_n, r_n), r_n)
-    acc[...] = dr1[...]
-    load.wait()
-    lane16 = lax.broadcasted_iota(jnp.int32, (16, width), 0)
-    sums = jnp.sum(vec[...], axis=1)
-
-    def grads_t(t):
-        both = (dkv[t, mine, :].astype(F32) + dkv_in[t].astype(F32)).astype(BF)
-        dqkv[...] = jnp.concatenate([jnp.zeros((r_n, hw), BF), dq[t], both], axis=1)
-        d = dqkv[...]
-        acc[...] += mm_rt(d, block_mat(w_a, t))
-        g_a[t] = (mm_lt(xm[...], d) + mm_lt(da[...], op[t])).astype(BF).reshape(g_a.shape[1:])
-        base = jnp.where(lane16 < 6, sums, 0.0)
-        base = base + jnp.where(lane16 == 6, jnp.sum(d.astype(F32), axis=0, keepdims=True), 0.0)
-        base = base + jnp.where(lane16 == 7, jnp.sum(vec[8 + t], axis=0, keepdims=True), 0.0)
-        g_s[t] = jnp.broadcast_to(base.astype(BF)[None], g_s.shape[1:])
-    each_t(grads_t)
-    stores = [pltpu.make_async_copy(g_a, gg.at[:, :, pl.ds(0, wl)], sem.at[1]),
-              pltpu.make_async_copy(g_s, gg.at[:, :, pl.ds(3 * wl, 16)], sem.at[2])]
-    for d in stores:
-        d.start()
-    pick = (order == nat).astype(F32).astype(BF)
-    place[0] = mm_lt(pick, y[...]).astype(BF)
-    lane = lax.broadcasted_iota(jnp.int32, (1, n_n), 1)
-    block = n_n // 16
-    at = ((lane // block) % 4) * (4 * block) + (lane // (4 * block)) * block + lane % block
-    pick2 = (at == nat).astype(F32).astype(BF)
-    place[1] = mm_lt(pick2, acc[...].astype(BF)).astype(BF)
-    for d in stores:
-        d.wait()
-
-
-def k2(gath, meta, dq, dkv, dkv_in, xm, da, op, dr1, y, vec, gg):
-    n_t, n_fc, rows, width = gath.shape
-    wl = (rows - 16) // 3
-    r_n = xm.shape[0]
-    n_n = 4 * r_n
-    v = pltpu.VMEM
-    vm = pl.BlockSpec(memory_space=pltpu.VMEM)
-    any_ = pl.BlockSpec(memory_space=pl.ANY)
-    wshape = (n_t, n_fc, wl, width)
-    return pl.pallas_call(
-        k2_kernel,
-        out_shape=(jax.ShapeDtypeStruct(gg.shape, BF), jax.ShapeDtypeStruct((2, n_n, width), BF)),
-        in_specs=[any_] + [vm] * 10 + [any_],
-        out_specs=(any_, vm),
-        input_output_aliases={11: 0},
-        scratch_shapes=[v(wshape, BF), v(wshape, BF), v((n_t, n_fc, 16, width), BF), v((r_n, width), F32),
-                        v((r_n, width), BF), pltpu.SemaphoreType.DMA((3,))],
-        compiler_params=pltpu.CompilerParams(vmem_limit_bytes=VMEM_MAX),
-        name="layer_tail",
-    )(gath, meta, dq, dkv, dkv_in, xm, da, op, dr1, y, vec, gg)
 
 
 def comm_in_kernel(cut, tok, cot, pack, meta, gath, group, meta_all, held, *sems):
@@ -709,33 +642,15 @@
     )(tok, cot, pack, meta)
 
 
-def swap_kernel(dkv, got, ssem, rsem):
+def tail_out_kernel(gath, meta_ref, dq, dkv, xm, da, op, dr1, y, vec, gg, tot_a, tot_w, rows_out,
+                    w_a, g_a, acc, dqkv, dkv_in, place, pl1, pl2, own, w0, w1, w2, w3, a0, a1, a2, a3,
+                    sem_l, s_d, r_d, s_u, r_u, s_o, r_o,
+                    ws0, wr0, ws1, wr1, ws2, wr2, ws3, wr3, as0, ar0, as1, ar1, as2, ar2, as3, ar3):
     f, c, t = lax.axis_index("fsdp"), lax.axis_index("ctx"), lax.axis_index("tp")
-    partner = (1 - f, c, t)
-    barrier = pltpu.get_barrier_semaphore()
-    pl.semaphore_signal(barrier, inc=1, device_id=partner, device_id_type=MESH)
-    pl.semaphore_wait(barrier, 1)
-    n = got.shape[1]
-    d = pltpu.make_async_remote_copy(src_ref=dkv.at[:, pl.ds(pl.multiple_of((1 - f) * n, n), n)], dst_ref=got, send_sem=ssem, recv_sem=rsem,
-                                     device_id=partner, device_id_type=MESH)
-    d.start()
-    d.wait()
-
-
-def swap(dkv):
-    n_t, s_n, w = dkv.shape
-    vm = pl.BlockSpec(memory_space=pltpu.VMEM)
-    return pl.pallas_call(
-        swap_kernel, out_shape=jax.ShapeDtypeStruct((n_t, s_n // 2, w), BF), in_specs=[vm], out_specs=vm,
-        scratch_shapes=[pltpu.SemaphoreType.DMA, pltpu.SemaphoreType.DMA],
-        compiler_params=pltpu.CompilerParams(collective_id=1, has_side_effects=True), name="core_swap")(dkv)
-
-
-def comm_out_kernel(cut, gg, place, total, rows_out, own, got0, got1, got2, got3, pl1, pl2, final, *sems):
-    (sem_l, s0, r0, s1, r1, s2, r2, s3, r3, su, ru, s_o, r_o) = sems
-    f, c, t = lax.axis_index("fsdp"), lax.axis_index("ctx"), lax.axis_index("tp")
-    rows = got0.shape[2]
-    h0, h1 = pl.ds(0, cut), pl.ds(cut, rows - cut)
+    r_n, width = xm.shape
+    n_n = 4 * r_n
+    hw = width // 4
+    wl = w_a.shape[2]
     partner = (1 - f, c, t)
     cx = c + 1 - 2 * (c % 2)
     cy = (c + 2) % 4
@@ -746,6 +661,15 @@
     to_f, to_t = t // 2, 2 * f + par
     stays = to_f == f
 
+    load_a = pltpu.make_async_copy(gath.at[:, :, pl.ds(0, wl)], w_a, sem_l.at[0])
+    load_a.start()
+    turn = [(t + 2) % 4, (t + 1) % 4, (t + 3) % 4, t]
+    loads = []
+    for i, tt in enumerate(turn):
+        d = pltpu.make_async_copy(gg.at[tt, pl.ds(pl.multiple_of(f * 4, 4), 4)], own.at[tt], sem_l.at[1 + i])
+        d.start()
+        loads.append(d)
+
     barrier = pltpu.get_barrier_semaphore()
     peers = [partner] + [(f, (c + i) % 4, t) for i in (1, 2, 3)] + [(f, c, (t + i) % 4) for i in (1, 2, 3)]
     for p in peers:
@@ -773,121 +697,190 @@
         pending.append((pred, d))
 
     def arrived(dst, rsem):
-        pltpu.make_async_remote_copy(src_ref=dst, dst_ref=dst, send_sem=su.at[0], recv_sem=rsem,
+        pltpu.make_async_remote_copy(src_ref=dst, dst_ref=dst, send_sem=s_d, recv_sem=rsem,
                                      device_id=partner, device_id_type=MESH).wait_recv()
 
-    turn = [(t + 2) % 4, (t + 1) % 4, (t + 3) % 4, t]
-    own_base = pl.ds(pl.multiple_of(f * 4, 4), 4)
-    loads = []
-    for i, tt in enumerate(turn):
-        d = pltpu.make_async_copy(gg.at[tt, own_base], own.at[tt], sem_l.at[i])
-        d.start()
-        loads.append(d)
-    lo = pl.multiple_of(2 * f, 2)
-    hi = pl.multiple_of(2 - 2 * f, 2)
-    send(place.at[:, pl.ds(hi, 2)], pl1, su.at[0], ru.at[0], partner)
-    for tt in turn:
-        for i in (1, 2, 3, 0):
-            cc = (c + i) % 4
-            send(gg.at[tt, 4 * (1 - f) + cc], got0.at[tt, cc], s0.at[tt, cc], r0.at[tt, cc], partner)
-
-    def add_into(dst, src, total_rows, step=16):
-        def go(i, _):
-            r = pl.ds(pl.multiple_of(i * step, step), step)
-            dst[r, :] = dst[r, :] + src[r, :]
-            return 0
-        lax.fori_loop(0, total_rows // step, go, 0, unroll=2 if (total_rows // step) % 2 == 0 else 1)
-
-    def half_add(dst, src, off, n):
+    def add_into(dst, src, off, n):
         def go(i, _):
             r = pl.ds(pl.multiple_of(off + i * 16, 16), 16)
             dst[r, :] = dst[r, :] + src[r, :]
             return 0
         lax.fori_loop(0, n // 16, go, 0)
 
-    def roles(i):
-        return (cy, cx, y_nb, x_nb) if i % 2 == 0 else (cx, cy, x_nb, y_nb)
-
-    def stage1(i):
-        tt = turn[i]
-        ca, cb, a_nb, b_nb = roles(i)
-        loads[i].wait()
-        for k in (1, 2, 3, 0):
-            cc = (c + k) % 4
-            arrived(got0.at[tt, cc], r0.at[tt, cc])
-            add_into(own.at[tt, cc], got0.at[tt, cc], rows)
-        for k, cc in enumerate((ca, cd)):
-            send(own.at[tt, cc, h0], got1.at[tt, k, h0], s1.at[0, k, tt], r1.at[0, k, tt], a_nb)
-        for k, cc in enumerate((cb, cd)):
-            send(own.at[tt, cc, h1], got1.at[tt, k, h1], s1.at[1, k, tt], r1.at[1, k, tt], b_nb)
-
-    def stage2(i):
-        tt = turn[i]
-        ca, cb, a_nb, b_nb = roles(i)
-        arrived(got1.at[tt, 1, h0], r1.at[0, 1, tt])
-        half_add(own.at[tt, cb], got1.at[tt, 1], 0, cut)
-        arrived(got1.at[tt, 1, h1], r1.at[1, 1, tt])
-        half_add(own.at[tt, ca], got1.at[tt, 1], cut, rows - cut)
-        send(own.at[tt, cb, h0], got2.at[tt, h0], s2.at[0, tt], r2.at[0, tt], b_nb)
-        send(own.at[tt, ca, h1], got2.at[tt, h1], s2.at[1, tt], r2.at[1, tt], a_nb)
-        arrived(got1.at[tt, 0, h0], r1.at[0, 0, tt])
-        half_add(own.at[tt, c], got1.at[tt, 0], 0, cut)
-        arrived(got1.at[tt, 0, h1], r1.at[1, 0, tt])
-        half_add(own.at[tt, c], got1.at[tt, 0], cut, rows - cut)
-
-    def stage3(i):
-        tt = turn[i]
-        arrived(got2.at[tt, h0], r2.at[0, tt])
-        arrived(got2.at[tt, h1], r2.at[1, tt])
-        add_into(own.at[tt, c], got2.at[tt], rows)
-        if i < 3:
-            send(own.at[tt, c], got3.at[t], s3.at[tt], r3.at[t], (f, c, tt))
-
-    stage1(0)
-    stage1(1)
-    arrived(pl1, ru.at[0])
-    for ten in range(2):
+    def make_pass(mine, theirs, g0, g1, g2, g3, cut, sems):
+        q0, p0, q1, p1, q2, p2, q3, p3 = sems
+        rows = g0.shape[2]
+        h0, h1 = pl.ds(0, cut), pl.ds(cut, rows - cut)
+
+        def roles(i):
+            return (cy, cx, y_nb, x_nb) if i % 2 == 0 else (cx, cy, x_nb, y_nb)
+
+        def stage0(i):
+            tt = turn[i]
+            for k in (1, 2, 3, 0):
+                cc = (c + k) % 4
+                send(theirs(tt, cc), g0.at[tt, cc], q0.at[tt, cc], p0.at[tt, cc], partner)
+
+        def stage1(i):
+            tt = turn[i]
+            ca, cb, a_nb, b_nb = roles(i)
+            for k in (1, 2, 3, 0):
+                cc = (c + k) % 4
+                arrived(g0.at[tt, cc], p0.at[tt, cc])
+                add_into(mine(tt, cc), g0.at[tt, cc], 0, rows)
+            for k, cc in enumerate((ca, cd)):
+                send(mine(tt, cc).at[h0], g1.at[tt, k, h0], q1.at[0, k, tt], p1.at[0, k, tt], a_nb)
+            for k, cc in enumerate((cb, cd)):
+                send(mine(tt, cc).at[h1], g1.at[tt, k, h1], q1.at[1, k, tt], p1.at[1, k, tt], b_nb)
+
+        def stage2(i):
+            tt = turn[i]
+            ca, cb, a_nb, b_nb = roles(i)
+            arrived(g1.at[tt, 1, h0], p1.at[0, 1, tt])
+            add_into(mine(tt, cb), g1.at[tt, 1], 0, cut)
+            arrived(g1.at[tt, 1, h1], p1.at[1, 1, tt])
+            add_into(mine(tt, ca), g1.at[tt, 1], cut, rows - cut)
+            send(mine(tt, cb).at[h0], g2.at[tt, h0], q2.at[0, tt], p2.at[0, tt], b_nb)
+            send(mine(tt, ca).at[h1], g2.at[tt, h1], q2.at[1, tt], p2.at[1, tt], a_nb)
+            arrived(g1.at[tt, 0, h0], p1.at[0, 0, tt])
+            add_into(mine(tt, c), g1.at[tt, 0], 0, cut)
+            arrived(g1.at[tt, 0, h1], p1.at[1, 0, tt])
+            add_into(mine(tt, c), g1.at[tt, 0], cut, rows - cut)
+
+        def stage3(i):
+            tt = turn[i]
+            arrived(g2.at[tt, h0], p2.at[0, tt])
+            arrived(g2.at[tt, h1], p2.at[1, tt])
+            add_into(mine(tt, c), g2.at[tt], 0, rows)
+            if i < 3:
+                send(mine(tt, c), g3.at[t], q3.at[tt], p3.at[t], (f, c, tt))
+
+        def finish(total, ls):
+            keep = pltpu.make_async_copy(mine(t, c), g3.at[t], ls)
+            keep.start()
+            keep.wait()
+            for tt in turn[:3]:
+                arrived(g3.at[tt], p3.at[tt])
+
+            def go(i, _):
+                r = pl.ds(pl.multiple_of(i * 16, 16), 16)
+                a, b, e, g = (g3[k, r, :].astype(F32) for k in range(4))
+                total[r, :] = ((a + b) + e) + g
+                return 0
+            lax.fori_loop(0, rows // 16, go, 0)
+        return stage0, stage1, stage2, stage3, finish
+
+    wp = make_pass(lambda tt, cc: own.at[tt, cc], lambda tt, cc: gg.at[tt, 4 * (1 - f) + cc],
+                   w0, w1, w2, w3, own.shape[2] // 2, (ws0, wr0, ws1, wr1, ws2, wr2, ws3, wr3))
+    a_rows = g_a.shape[2]
+    ap = make_pass(lambda tt, cc: g_a.at[tt, 4 * f + cc], lambda tt, cc: g_a.at[tt, 4 * (1 - f) + cc],
+                   a0, a1, a2, a3, (a_rows // 32) * 16, (as0, ar0, as1, ar1, as2, ar2, as3, ar3))
+
+    lo = pl.multiple_of(2 * f, 2)
+    hi = pl.multiple_of(2 - 2 * f, 2)
+    block = place.shape[3]
+    moves = [pltpu.make_async_copy(pl2.at[ten, c], rows_out.at[ten, c], sem_l.at[5 + ten]) for ten in range(2)]
+
+    def rows1(ten):
+        send(place.at[ten, pl.ds(hi, 2)], pl1.at[ten], s_u.at[0, ten], r_u.at[0, ten], partner)
+
+    def rows2(ten):
+        arrived(pl1.at[ten], r_u.at[0, ten])
         for k in (0, 1):
             for j in range(4):
-                add_into(pl1.at[ten, k, j], place.at[ten, lo + k, j], pl1.shape[3])
-    send(pl1.at[:, 1 - par], pl2, su.at[1], ru.at[1], z_nb)
-    stage2(0)
-    stage1(2)
-    stage2(1)
-    stage3(0)
-    stage1(3)
-
-    arrived(pl2, ru.at[1])
-    for ten in range(2):
+                add_into(pl1.at[ten, k, j], place.at[ten, lo + k, j], 0, block)
+        send(pl1.at[ten, 1 - par], pl2.at[ten], s_u.at[1, ten], r_u.at[1, ten], z_nb)
+
+    def rows3(ten):
+        arrived(pl2.at[ten], r_u.at[1, ten])
         for j in range(4):
-            add_into(pl2.at[ten, j], pl1.at[ten, par, j], pl2.shape[2])
-    moves = []
-    for ten in range(2):
+            add_into(pl2.at[ten, j], pl1.at[ten, par, j], 0, block)
         for i in range(4):
             cc = (c + i) % 4
-            src, dst = pl2.at[ten, cc], rows_out.at[ten, c]
             away = jnp.logical_not(stays) if i == 0 else None
-            send(src, dst, s_o.at[ten, i], r_o.at[ten, c], (to_f, cc, to_t), away)
-        moves.append(pltpu.make_async_copy(pl2.at[ten, c], rows_out.at[ten, c], sem_l.at[4 + ten]))
+            send(pl2.at[ten, cc], rows_out.at[ten, c], s_o.at[ten, i], r_o.at[ten, c], (to_f, cc, to_t), away)
         pl.when(stays)(moves[ten].start)
 
-    stage2(2)
-    stage3(1)
-    stage2(3)
-    stage3(2)
-    stage3(3)
-    keep = pltpu.make_async_copy(own.at[t, c], got3.at[t], sem_l.at[6])
-    keep.start()
-    keep.wait()
-    for tt in turn[:3]:
-        arrived(got3.at[tt], r3.at[tt])
-
-    def go(i, _):
-        r = pl.ds(pl.multiple_of(i * 16, 16), 16)
-        a, b, e, g = (got3[k, r, :].astype(F32) for k in range(4))
-        total[r, :] = ((a + b) + e) + g
-        return 0
-    lax.fori_loop(0, rows // 16, go, 0)
+    meta = meta_ref[t // 2]
+    start, _, _ = row_facts(meta, n_n)
+    nat = wrap(start + f * r_n + lax.broadcasted_iota(jnp.int32, (r_n, 1), 0), n_n)
+    mine_rows = pl.ds(pl.multiple_of(f * r_n, r_n), r_n)
+    lane16 = lax.broadcasted_iota(jnp.int32, (16, width), 0)
+
+    def grads_t(k):
+        both = (dkv[k, mine_rows, :].astype(F32) + dkv_in[k].astype(F32)).astype(BF)
+        dqkv[...] = jnp.concatenate([jnp.zeros((r_n, hw), BF), dq[k], both], axis=1)
+        d = dqkv[...]
+        acc[...] += mm_rt(d, block_mat(w_a, k))
+        g_a[k, :, 0:wl, :] = (mm_lt(xm[...], d) + mm_lt(da[...], op[k])).astype(BF).reshape(g_a.shape[1], wl, width)
+        sums = jnp.sum(vec[...], axis=1)
+        base = jnp.where(lane16 < 6, sums, 0.0)
+        base = base + jnp.where(lane16 == 6, jnp.sum(d.astype(F32), axis=0, keepdims=True), 0.0)
+        base = base + jnp.where(lane16 == 7, jnp.sum(vec[8 + k], axis=0, keepdims=True), 0.0)
+        g_a[k, :, wl:wl + 16, :] = jnp.broadcast_to(base.astype(BF)[None], (g_a.shape[1], 16, width))
+
+    def two(first):
+        def step(k, _):
+            grads_t(k)
+            return 0
+        lax.fori_loop(first, first + 2, step, 0)
+
+    n_d = dkv_in.shape[1]
+    send(dkv.at[:, pl.ds(pl.multiple_of((1 - f) * n_d, n_d), n_d)], dkv_in, s_d, r_d, partner)
+    wp[0](0)
+    wp[0](1)
+    order = pick_row(meta[8:12, :], c)
+    pick = (order == nat).astype(F32).astype(BF)
+    place[0] = mm_lt(pick, y[...]).astype(BF).reshape(place.shape[1:])
+    acc[...] = dr1[...]
+    wp[0](2)
+    rows1(0)
+    wp[0](3)
+    loads[0].wait()
+    wp[1](0)
+    loads[1].wait()
+    wp[1](1)
+    arrived(dkv_in, r_d)
+    load_a.wait()
+    two(0)
+    rows2(0)
+    wp[2](0)
+    loads[2].wait()
+    wp[1](2)
+    two(2)
+    wp[2](1)
+    wp[3](0)
+    loads[3].wait()
+    wp[1](3)
+    rows3(0)
+    for i in range(4):
+        ap[0](i)
+    lane = lax.broadcasted_iota(jnp.int32, (1, n_n), 1)
+    at = ((lane // block) % 4) * (4 * block) + (lane // (4 * block)) * block + lane % block
+    pick2 = (at == nat).astype(F32).astype(BF)
+    place[1] = mm_lt(pick2, acc[...].astype(BF)).astype(BF).reshape(place.shape[1:])
+    wp[2](2)
+    wp[3](1)
+    rows1(1)
+    ap[1](0)
+    wp[2](3)
+    wp[3](2)
+    rows2(1)
+    ap[1](1)
+    ap[2](0)
+    wp[3](3)
+    rows3(1)
+    ap[1](2)
+    ap[2](1)
+    ap[3](0)
+    ap[1](3)
+    wp[4](tot_w, sem_l.at[7])
+    ap[2](2)
+    ap[3](1)
+    ap[2](3)
+    ap[3](2)
+    ap[3](3)
+    ap[4](tot_a, sem_l.at[8])
 
     for ten in range(2):
         for i in range(4):
@@ -906,28 +899,33 @@
             pl.when(pred)(d.wait_send)
 
 
-def comm_out(gg, place, cut):
+def tail_out(gath, meta, dq, dkv, xm, da, op, dr1, y, vec, gg):
+    n_t, n_fc, rows, width = gath.shape
+    wl = (rows - 16) // 3
+    r_n = xm.shape[0]
+    block = r_n // 4
+    v = pltpu.VMEM
     dma = pltpu.SemaphoreType.DMA
-    n_t, n_fc, rows, width = gg.shape
-    n_n = place.shape[1]
-    block = n_n // 16
-    place = place.reshape(2, 4, 4, block, width)
-    v = pltpu.VMEM
     vm = pl.BlockSpec(memory_space=pltpu.VMEM)
     any_ = pl.BlockSpec(memory_space=pl.ANY)
+    ra, rw = wl + 16, 2 * wl
+    def bufs(n):
+        return [v((4, 4, n, width), BF), v((4, 2, n, width), BF), v((4, n, width), BF), v((4, n, width), BF)]
+    pass_sems = [dma((4, 4)), dma((4, 4)), dma((2, 2, 4)), dma((2, 2, 4)), dma((2, 4)), dma((2, 4)), dma((4,)), dma((4,))]
     return pl.pallas_call(
-        functools.partial(comm_out_kernel, cut),
-        out_shape=(jax.ShapeDtypeStruct((rows, width), F32), jax.ShapeDtypeStruct((2, 4, block, width), BF)),
-        in_specs=[any_, vm],
-        out_specs=(vm, vm),
-        scratch_shapes=[v((4, 4, rows, width), BF), v((4, 4, rows, width), BF), v((4, 2, rows, width), BF),
-                        v((4, rows, width), BF), v((4, rows, width), BF), v((2, 2, 4, block, width), BF),
-                        v((2, 4, block, width), BF), v((8, 128), F32),
-                        dma((7,)), dma((4, 4)), dma((4, 4)), dma((2, 2, 4)), dma((2, 2, 4)), dma((2, 4)), dma((2, 4)),
-                        dma((4,)), dma((4,)), dma((2,)), dma((2,)), dma((2, 4)), dma((2, 4))],
-        compiler_params=pltpu.CompilerParams(collective_id=2, has_side_effects=True, vmem_limit_bytes=62 * 1024 * 1024),
-        name="comm_out",
-    )(gg, place)
+        tail_out_kernel,
+        out_shape=(jax.ShapeDtypeStruct((ra, width), F32), jax.ShapeDtypeStruct((rw, width), F32),
+                   jax.ShapeDtypeStruct((2, 4, block, width), BF)),
+        in_specs=[any_] + [vm] * 9 + [any_],
+        out_specs=(vm, vm, vm),
+        scratch_shapes=[v((n_t, n_fc, wl, width), BF), v((n_t, n_fc, ra, width), BF), v((r_n, width), F32),
+                        v((r_n, width), BF), v((n_t, r_n, dkv.shape[2]), BF), v((2, 4, 4, block, width), BF),
+                        v((2, 2, 4, block, width), BF), v((2, 4, block, width), BF), v((4, 4, rw, width), BF)]
+        + bufs(rw) + bufs(ra)
+        + [dma((9,)), dma, dma, dma((2, 2)), dma((2, 2)), dma((2, 4)), dma((2, 4))] + pass_sems + pass_sems,
+        compiler_params=pltpu.CompilerParams(collective_id=2, has_side_effects=True, vmem_limit_bytes=VMEM_MAX),
+        name="tail_out",
+    )(gath, meta, dq, dkv, xm, da, op, dr1, y, vec, gg)
 
 
 def quad_body(tokens_in, cotangent, seq_lengths, row_order, w_query, b_query, w_key, w_value, b_value,
@@ -962,15 +960,13 @@
     gath, group, meta = comm_in(tokens_in, cotangent, pack, meta_own, cut)
     group = group.reshape(2, n_n, width)
     gg, dq, dkv, xm, da, op, dr1, y, vec = k1(gath, meta, group, head)
-    dkv_in = swap(dkv)
-    gg, place = k2(gath, meta, dq, dkv, dkv_in, xm, da, op, dr1, y, vec, gg)
-    total, rows = comm_out(gg, place, cut)
-
-    g_a, g_up, g_down = total[:wl], total[wl:2 * wl], total[2 * wl:3 * wl]
-    sv = lax.dynamic_slice(total[3 * wl:3 * wl + 6], (0, fc * wl), (6, wl))
-    ba = total[3 * wl + 6].reshape(4, heads_l, head)
+    tot_a, tot_w, rows = tail_out(gath, meta, dq, dkv, xm, da, op, dr1, y, vec, gg)
+
+    g_a, g_up, g_down = tot_a[:wl], tot_w[:wl], tot_w[wl:]
+    sv = lax.dynamic_slice(tot_a[wl:wl + 6], (0, fc * wl), (6, wl))
+    ba = tot_a[wl + 6].reshape(4, heads_l, head)
     gb = lax.dynamic_slice(ba, (0, 0, fc * head_l), (4, heads_l, head_l))
-    gu = lax.dynamic_slice(total[3 * wl + 7].reshape(heads_l, -1), (0, fc * up_l), (heads_l, up_l))
+    gu = lax.dynamic_slice(tot_a[wl + 7].reshape(heads_l, -1), (0, fc * up_l), (heads_l, up_l))
     return (rows[0], rows[1], g_a[:, hw:2 * hw], gb[1], g_a[:, 2 * hw:3 * hw], g_a[:, 3 * hw:], gb[3], g_a[:, :hw],
             sv[0], sv[1], sv[2], g_up, gu, g_down, sv[3], sv[4], sv[5])
 

time: 274 us -> 258 us (0.942)
  Pallas kernels: 252 us -> 235 us
    pallas_call x4 -> x2, Pallas kernels: 166 us -> 149 us  [the longest x1 103 us: tail_out(): pl.pallas_call(tail_out_kernel, out_shape=(jax.ShapeDtypeStruct((ra, widt...]
where the time goes in v4:
time: 258 us; the launch traced here: 257 us
  Pallas kernels  235 us (91%)
  local copies, waits for them, and re-layouts  18 us (7%)
  other arithmetic  3.21 us (1%)
    pallas_call x1, Pallas kernels, tail_out(): pl.pallas_call(tail_out_kernel, out_shape=(jax.ShapeDtypeStruct((ra, widt...  103 us
    pallas_call x1, Pallas kernels, comm_in(): pl.pallas_call(functools.partial(comm_in_kernel, cut), out_shape=(jax.Sha...  85.9 us
    pallas_call x1, Pallas kernels, k1(): pl.pallas_call(functools.partial(k1_kernel, head), out_shape=(sds((n_t, n...  46.5 us

profile of v4, /device:TPU:0, one launch (start us, length us, event | category | flops | bytes accessed | tf_op | source)
XLA Modules:
  0.0 257.4 jit_solution(5103585993763752393)
XLA Ops:
  0.7 0.7 pad_maximum_fusion.1
  1.4 0.1 tile.28
  1.5 0.7 tile.29
  2.2 0.1 tile.30
  2.3 0.8 stack.36
  3.1 0.1 tile.26
  3.2 1.0 pad_maximum_fusion
  4.2 5.0 %concatenate.10.pack = bf16[304,768]{1,0:T(8,128)(2,1)} concatenate(bf16[96,768]{1,0:T(8,128)(2,1)S(1)} %pad_maximum_fusion, bf16[96,768]{1,0:T(8,128)(2,1)} %param.32, bf16[96,768]{1,0:T(8,128)(2,1)} %param.34, bf16[6,768]{1,0:T(8,128)(2,1)S(1)} %broadcast_select_fusion, bf16[1,768]{1,0:T(2,128)(2,1)S(1)} %get-tuple-element.66, bf16[1,768]{1,0:T(2,128)(2,1)S(1)} %get-tuple-element.65, ...), dimensions={0} | concatenate | bytes 933888 | tf_op jit(solution)/shard_map/concatenate | solution.py:951
  9.2 0.8 reduce
  10.0 0.1 reshape_squeeze.13
  10.1 0.1 reshape.295
  10.2 0.7 copy.44
  10.9 0.8 copy.38
  11.7 0.1 reshape_squeeze.12
  11.8 0.1 pad.8.clone
  11.9 0.7 fusion.1.meta
  12.6 85.9 %comm_in.1 = (bf16[4,8,304,768]{3,2,1,0:T(8,128)(2,1)}, bf16[2,4,4,64,768]{4,3,2,1,0:T(8,128)(2,1)}, s32[2,16,1024]{2,1,0:T(8,128)}) custom-call(bf16[4,64,768]{2,1,0:T(8,128)(2,1)} %tok.1, bf16[4,64,768]{2,1,0:T(8,128)(2,1)} %cot.1, bf16[304,768]{1,0:T(8,128)(2,1)} %concatenate.10.pack, s32[16,1024]{1,0:T(8,128)} %fusion.1.meta), custom_call_target="tpu_custom_call" | custom-call | tf_op jit(solution)/shard_map/comm_in/pallas_call | solution.py:633
  98.5 46.5 %layer_main.1 = (bf16[4,8,192,768]{3,2,1,0:T(8,128)(2,1)}, bf16[4,256,192]{2,1,0:T(8,128)(2,1)}, bf16[4,512,384]{2,1,0:T(8,128)(2,1)}, bf16[256,768]{1,0:T(8,128...) custom-call(bf16[4,8,304,768]{3,2,1,0:T(8,128)(2,1)} %get-tuple-elem, ...), custom_call_target="tpu_custom_call" | custom-call | tf_op jit(solution)/shard_map/layer_main/pallas_call | solution.py:448
  145.0 103.0 %tail_out.1 = (f32[112,768]{1,0:T(8,128)}, f32[192,768]{1,0:T(8,128)}, bf16[2,4,64,768]{3,2,1,0:T(8,128)(2,1)}) custom-call(bf16[4,8,304,768]{3,2,1,0:T(8,128)(2,1)} %get-tuple-element.32.gath, s32[2,16,1024]{2,1,0:T(8,128)} %get-tuple-element.33.meta_ref, bf16[4,256,192]{2,1,0:T(8,128)(2,1)} %get-tuple-element.35.dq, ...), custom_call_target="tpu_custom_call" | custom-call | tf_op jit(solution)/shard_map/tail_out/pallas_call | solution.py:915
  248.0 2.0 slice_bitcast_fusion
  250.0 1.9 fusion.6
  251.9 1.9 fusion.7
  253.8 0.7 slice.71
  254.5 0.1 constant_dynamic-slice_fusion.1
  254.6 0.5 slice_bitcast_fusion.2
  255.1 0.8 slice_reduce_fusion
  256.0 0.1 reshape_squeeze.14
  256.0 0.7 dynamic-slice_bitcast_fusion
  256.7 0.6 constant_dynamic-slice_fusion
  (10 shorter events, 0.1 us)

commit v5 on v4

--- a/solution.py
+++ b/solution.py
@@ -216,11 +216,6 @@
 VMEM_MAX = 62 * 1024 * 1024
 
 
-def block_mat(ref, t):
-    n, rows, width = ref.shape[1:]
-    return ref[t].reshape(n * rows, width)
-
-
 def row_facts(meta, group_n):
     c, t = lax.axis_index("ctx"), lax.axis_index("tp")
     lens = meta[4:5, :].astype(F32)
@@ -258,46 +253,203 @@
     lax.fori_loop(0, 4, step, 0)
 
 
-def k1_kernel(head, gath, meta_ref, group, gg, dq_out, dkv_out, xm_out, da_out, op_out, dr1_out, y_out, vec_out,
-              w_a, w_u, w_d, small, xh, dy, qkv, probs, sbuf, pb, pb2, acc, mid, midb, n1, inv1, gelu_d, act, n2, df, big, bias,
-              g_u, g_d, sem):
+def main_in_kernel(head, tok, cot, pack, meta, ga, gg, meta_all, dq_out, dkv_out, xm_out, da_out, op_out, dr1_out, y_out, vec_out,
+                   gu, group, held, xh, dy, qkv, probs, sbuf, pb, pb2, acc, midb, n1, inv1, gelu_d, act, n2, df, big, bias,
+                   g_u, g_d, sem_l, s_e, r_e, s_xg, r_xg, s_xf, s_m, r_m, *pass_sems):
     f, c, t_me = lax.axis_index("fsdp"), lax.axis_index("ctx"), lax.axis_index("tp")
     width = xh.shape[1]
-    s_n, r_n, n_n = xh.shape[0], dy.shape[0], group.shape[1]
-    wl = w_a.shape[2]
+    s_n, r_n = xh.shape[0], dy.shape[0]
+    n_n = 2 * s_n
+    wl = (gu.shape[2]) // 2
     hw = width // 4
     per_t = hw // head
-
-    loads = [pltpu.make_async_copy(gath.at[:, :, pl.ds(wl * i, wl)], ref, sem.at[i])
-             for i, ref in enumerate((w_a, w_u, w_d))]
-    loads.append(pltpu.make_async_copy(gath.at[:, :, pl.ds(3 * wl, 16)], small, sem.at[3]))
-    for d in (loads[3], loads[0], loads[1], loads[2]):
+    partner = (1 - f, c, t_me)
+    slot = f * 4 + c
+    cx = c + 1 - 2 * (c % 2)
+    cy = (c + 2) % 4
+    cd = (cx + 2) % 4
+    x_nb, y_nb = (f, cx, t_me), (f, cy, t_me)
+    near, far = 1 + f, 3 * f
+    is_near = t_me == near
+    receiver = (t_me // 2) == f
+
+    barrier = pltpu.get_barrier_semaphore()
+    peers = [partner] + [(f, (c + i) % 4, t_me) for i in (1, 2, 3)] + [(f, c, (t_me + i) % 4) for i in (1, 2, 3)]
+    for p in peers:
+        pl.semaphore_signal(barrier, inc=1, device_id=p, device_id_type=MESH)
+    pl.semaphore_wait(barrier, len(peers))
+
+    pending = []
+
+    def send(src, dst, ssem, rsem, dev, pred=None):
+        d = pltpu.make_async_remote_copy(src_ref=src, dst_ref=dst, send_sem=ssem, recv_sem=rsem,
+                                         device_id=dev, device_id_type=MESH)
+        if pred is None:
+            d.start()
+        else:
+            pl.when(pred)(d.start)
+        pending.append((pred, d))
+
+    def arrived(dst, rsem, pred=None):
+        d = pltpu.make_async_remote_copy(src_ref=dst, dst_ref=dst, send_sem=s_e.at[0, 0], recv_sem=rsem,
+                                         device_id=partner, device_id_type=MESH)
+        if pred is None:
+            d.wait_recv()
+        else:
+            pl.when(pred)(d.wait_recv)
+
+    def first_sends(ten, ref):
+        for i in (1, 2, 3):
+            to = (c + i) % 4
+            send(ref.at[to], held.at[ten, c], s_e.at[ten, i], r_e.at[ten, c], (f, to, t_me))
+
+    a_rows = ga.shape[2]
+    w_rows = gu.shape[2]
+    own_a, own_w = pack.at[pl.ds(0, a_rows)], pack.at[pl.ds(a_rows, w_rows)]
+    first_sends(0, tok)
+    local = [pltpu.make_async_copy(tok.at[c], held.at[0, c], sem_l.at[0]),
+             pltpu.make_async_copy(cot.at[c], held.at[1, c], sem_l.at[1]),
+             pltpu.make_async_copy(own_a, ga.at[t_me, slot], sem_l.at[2]),
+             pltpu.make_async_copy(own_w, gu.at[t_me, slot], sem_l.at[3]),
+             pltpu.make_async_copy(meta, meta_all.at[f], sem_l.at[8])]
+    for d in local:
         d.start()
-
-    meta = meta_ref[t_me // 2]
+    send(meta, meta_all.at[f], s_m.at[0], r_m.at[0], partner)
+
+    columns = [(t_me, None)]
+    for d in (1, 2, 3):
+        columns.append(((t_me - d + 4) % 4, t_me - d >= 0))
+        columns.append(((t_me + d) % 4, t_me + d <= 3))
+
+    def make_gather(gath, own, cut, sems):
+        (s_z, r_z, s_x0, r_x0, s_y0, r_y0, s_y1, r_y1, s_x1, r_x1, s_c, r_c, s_c0, r_c0, s_c1, r_c1) = sems
+        rows = gath.shape[2]
+        h0, h1 = pl.ds(0, cut), pl.ds(cut, rows - cut)
+
+        def have_column(src, tt, pred=None):
+            send(src.at[h0], gath.at[tt, slot, h0], s_x0.at[tt], r_x0.at[tt], x_nb, pred)
+            send(src.at[h1], gath.at[tt, slot, h1], s_y1.at[tt], r_y1.at[tt], y_nb, pred)
+            send(src.at[h0], gath.at[tt, slot, h0], s_y0.at[0, tt], r_y0.at[0, tt], y_nb, pred)
+            send(src.at[h1], gath.at[tt, slot, h1], s_x1.at[0, tt], r_x1.at[0, tt], x_nb, pred)
+            send(src, gath.at[tt, slot], s_c.at[tt], r_c.at[tt], partner, pred)
+
+        def begin():
+            send(own, gath.at[t_me, slot], s_z.at[0, t_me], r_z.at[t_me], (f, c, (t_me + 1) % 4), t_me < 3)
+            send(own, gath.at[t_me, slot], s_z.at[1, t_me], r_z.at[t_me], (f, c, (t_me + 3) % 4), t_me > 0)
+            have_column(own, t_me)
+
+        def z_step(d):
+            for sign in (-1, 1):
+                tt = t_me + sign * d
+                there = tt >= 0 if sign < 0 else tt <= 3
+                tt = (tt + 4) % 4
+                arrived(gath.at[tt, slot], r_z.at[tt], there)
+                on = t_me < 3 if sign < 0 else t_me > 0
+                nxt = (t_me + 1) % 4 if sign < 0 else (t_me + 3) % 4
+                if d < 3:
+                    send(gath.at[tt, slot], gath.at[tt, slot], s_z.at[0 if sign < 0 else 1, tt], r_z.at[tt],
+                         (f, c, nxt), jnp.logical_and(there, on))
+                have_column(gath.at[tt, slot], tt, there)
+
+        def mid_step(i):
+            tt, pred = columns[i]
+            a = gath.at[tt, f * 4 + cx, h0]
+            arrived(a, r_x0.at[tt], pred)
+            send(a, a, s_y0.at[1, tt], r_y0.at[1, tt], y_nb, pred)
+            send(a, a, s_c0.at[0, tt], r_c0.at[0, tt], partner, pred)
+            b = gath.at[tt, f * 4 + cy, h1]
+            arrived(b, r_y1.at[tt], pred)
+            send(b, b, s_x1.at[1, tt], r_x1.at[1, tt], x_nb, pred)
+            send(b, b, s_c1.at[0, tt], r_c1.at[0, tt], partner, pred)
+
+        def late_step(step, i):
+            tt, pred = columns[i]
+            a = gath.at[tt, f * 4 + (cy if step == 0 else cd), h0]
+            arrived(a, r_y0.at[step, tt], pred)
+            send(a, a, s_c0.at[1 + step, tt], r_c0.at[1 + step, tt], partner, pred)
+            b = gath.at[tt, f * 4 + (cx if step == 0 else cd), h1]
+            arrived(b, r_x1.at[step, tt], pred)
+            send(b, b, s_c1.at[1 + step, tt], r_c1.at[1 + step, tt], partner, pred)
+
+        def finish():
+            other = (1 - f) * 4
+            for tt in range(4):
+                arrived(gath.at[tt, other + c], r_c.at[tt])
+                for j, cc in enumerate((cx, cy, cd)):
+                    arrived(gath.at[tt, other + cc, h0], r_c0.at[j, tt])
+                for j, cc in enumerate((cy, cx, cd)):
+                    arrived(gath.at[tt, other + cc, h1], r_c1.at[j, tt])
+        return begin, z_step, mid_step, late_step, finish
+
+    half_sems = len(pass_sems) // 2
+    a_begin, a_z, a_mid, a_late, a_finish = make_gather(ga, own_a, (a_rows // 32) * 16, pass_sems[:half_sems])
+    w_begin, w_z, w_mid, w_late, w_finish = make_gather(gu, own_w, w_rows // 2, pass_sems[half_sems:])
+
+    def second_sends(ten):
+        local[ten].wait()
+        for i in (1, 2, 3):
+            frm = (c + i) % 4
+            arrived(held.at[ten, frm], r_e.at[ten, frm])
+        blk = held.at[ten]
+        dst = group.at[ten, :, t_me]
+        to = jnp.where(is_near, far, near)
+        send(blk, dst, s_xg.at[ten, t_me], r_xg.at[ten, t_me], (f, c, to))
+        send(blk, dst, s_xf.at[ten, t_me], r_xg.at[ten, t_me], partner, receiver)
+        keep = pltpu.make_async_copy(blk, dst, sem_l.at[4 + ten])
+        pl.when(receiver)(keep.start)
+        return keep
+
+    def relay(ten):
+        for i in (1, 2, 3):
+            tt = (t_me + i) % 4
+            arrived(group.at[ten, :, tt], r_xg.at[ten, tt], receiver)
+            send(group.at[ten, :, tt], group.at[ten, :, tt], s_xg.at[ten, tt], r_xg.at[ten, tt], (f, c, far),
+                 jnp.logical_and(is_near, tt != far))
+            send(group.at[ten, :, tt], group.at[ten, :, tt], s_xf.at[ten, tt], r_xg.at[ten, tt], partner, receiver)
+
+    def rows_here(ten, keep):
+        for tt in range(4):
+            arrived(group.at[ten, :, tt], r_xg.at[ten, tt], jnp.logical_not(receiver))
+        pl.when(receiver)(keep.wait)
+
+    def mat_of(ref, t, at):
+        return ref[t, :, at:at + wl, :].reshape(ref.shape[1] * wl, width)
+
+    a_begin()
+    keep0 = second_sends(0)
+    a_z(1)
+    relay(0)
+    a_z(2)
+    a_z(3)
+    for i in range(7):
+        a_mid(i)
+    first_sends(1, cot)
+    w_begin()
+    for step in (0, 1):
+        for i in range(7):
+            a_late(step, i)
+    w_z(1)
+    keep1 = second_sends(1)
+    rows_here(0, keep0)
+    arrived(meta_all.at[1 - f], r_m.at[0])
+    local[4].wait()
+
+    meta = meta_all[t_me // 2]
     start, e0, e1 = row_facts(meta, n_n)
     order = pick_row(meta[0:4, :], c)
+    mine = pl.ds(pl.multiple_of(f * r_n, r_n), r_n)
 
     def half_rows(rows):
         nat = wrap(start + rows.start + lax.broadcasted_iota(jnp.int32, (rows.size, 1), 0), n_n)
         sel = (lax.broadcasted_iota(jnp.int32, (rows.size, n_n), 1) == nat).astype(F32).astype(BF)
-        xh[rows, :] = mm(sel, group[0]).astype(BF)
+        xh[rows, :] = mm(sel, group[0].reshape(n_n, width)).astype(BF)
     chunks(s_n, half_rows, 128)
-
-    def quarter_rows(rows):
-        nat = wrap(start + f * r_n + rows.start + lax.broadcasted_iota(jnp.int32, (rows.size, 1), 0), n_n)
-        sel = (order == nat).astype(F32).astype(BF)
-        dy[rows, :] = mm(sel, group[1])
-    chunks(r_n, quarter_rows, 128)
-
-    mine = pl.ds(pl.multiple_of(f * r_n, r_n), r_n)
-    loads[3].wait()
+    a_finish()
+    local[2].wait()
     for t in range(4):
-        bias[t] = jnp.sum(small[t].astype(F32), axis=0)
+        bias[t] = jnp.sum(ga[t, :, wl:wl + 16, :].astype(F32), axis=0)
     vec = bias[0]
     bo, mg, ms, bd, eg, es = (vec[i:i + 1, :] for i in range(6))
-    loads[0].wait()
-
     nat_row = wrap(start + lax.broadcasted_iota(jnp.int32, (1, s_n), 1), n_n)
     seg_row = (nat_row >= e0).astype(jnp.int32) + (nat_row >= e1).astype(jnp.int32)
     nat_q = wrap(start + f * r_n + lax.broadcasted_iota(jnp.int32, (r_n, 1), 0), n_n)
@@ -305,7 +457,7 @@
 
     def forward_t(t):
         row6 = bias[t][6:7, :]
-        qkv[t] = (mm(xh[...], block_mat(w_a, t)) + row6).astype(BF)
+        qkv[t] = (mm(xh[...], mat_of(ga, t, 0)) + row6).astype(BF)
         q3 = qkv[t, mine, :]
         kv = qkv[t]
         outs = []
@@ -322,14 +474,32 @@
             outs.append(mm(pb[...], kv[:, lo + 2 * hw:lo + 2 * hw + head]).astype(BF))
         outs.append(jnp.zeros((r_n, width - hw), BF))
         op_out[t] = jnp.concatenate(outs, axis=1)
-    each_t(forward_t)
-
+
+    def two(first, fn):
+        def step(t, _):
+            fn(t)
+            return 0
+        lax.fori_loop(first, first + 2, step, 0)
+
+    w_z(2)
+    relay(1)
+    two(0, forward_t)
+    w_z(3)
+    w_mid(0)
+    w_mid(1)
+    w_mid(2)
+    two(2, forward_t)
+    for i in range(3, 7):
+        w_mid(i)
     xm_out[...] = xh[mine, :]
     acc[...] = xm_out[...].astype(F32) + bo
 
     def out_t(t):
-        acc[...] += mm_rt(op_out[t], block_mat(w_a, t))
+        acc[...] += mm_rt(op_out[t], mat_of(ga, t, 0))
     each_t(out_t)
+    w_late(0, 0)
+    w_late(0, 1)
+    w_late(0, 2)
 
     def norm_rows(u):
         centre = u - jnp.mean(u, axis=-1, keepdims=True)
@@ -341,17 +511,26 @@
         n1[rows, :] = n
         inv1[rows, :] = jnp.broadcast_to(inv, (rows.size, 128))
         m = n * mg + ms
-        mid[rows, :] = m
         midb[rows, :] = m.astype(BF)
         acc[rows, :] = m + bd
     chunks(r_n, first_norm)
-
-    loads[1].wait()
-    loads[2].wait()
+    rows_here(1, keep1)
+
+    def quarter_rows(rows):
+        nat = wrap(start + f * r_n + rows.start + lax.broadcasted_iota(jnp.int32, (rows.size, 1), 0), n_n)
+        sel = (order == nat).astype(F32).astype(BF)
+        dy[rows, :] = mm(sel, group[1].reshape(n_n, width))
+    chunks(r_n, quarter_rows, 128)
+    for i in range(3, 7):
+        w_late(0, i)
+    for i in range(7):
+        w_late(1, i)
+    w_finish()
+    local[3].wait()
 
     def ffn_t(t):
         row7 = bias[t][7:8, :]
-        big[...] = mm(midb[...], block_mat(w_u, t))
+        big[...] = mm(midb[...], mat_of(gu, t, 0))
 
         def gelu(rows):
             u = big[rows, :] + row7
@@ -360,7 +539,7 @@
             act[t, rows, :] = (u * cdf).astype(BF)
             gelu_d[t, rows, :] = cdf + u * pdf
         chunks(r_n, gelu, 16)
-        acc[...] += mm_rt(act[t], block_mat(w_d, t))
+        acc[...] += mm_rt(act[t], mat_of(gu, t, wl))
     each_t(ffn_t)
 
     vec_out[...] = jnp.zeros_like(vec_out)
@@ -382,19 +561,19 @@
     chunks(r_n, second_norm)
 
     def ffn_back_t(t):
-        big[...] = mm(df[...], block_mat(w_d, t))
+        big[...] = mm(df[...], mat_of(gu, t, wl))
 
         def times(rows):
             d = (big[rows, :] * gelu_d[t, rows, :]).astype(BF)
             n2[rows, :] = d
             add_vec(8 + t, d.astype(F32))
         chunks(r_n, times)
-        acc[...] += mm_rt(n2[...], block_mat(w_u, t))
+        acc[...] += mm_rt(n2[...], mat_of(gu, t, 0))
         g_d[t] = mm_lt(df[...], act[t]).astype(BF).reshape(g_d.shape[1:])
         g_u[t] = mm_lt(midb[...], n2[...]).astype(BF).reshape(g_u.shape[1:])
     each_t(ffn_back_t)
-    stores = [pltpu.make_async_copy(g_u, gg.at[:, :, pl.ds(0, wl)], sem.at[4]),
-              pltpu.make_async_copy(g_d, gg.at[:, :, pl.ds(wl, wl)], sem.at[5])]
+    stores = [pltpu.make_async_copy(g_u, gg.at[:, :, pl.ds(0, wl)], sem_l.at[6]),
+              pltpu.make_async_copy(g_d, gg.at[:, :, pl.ds(wl, wl)], sem_l.at[7])]
     for d in stores:
         d.start()
 
@@ -410,7 +589,7 @@
     chunks(r_n, first_norm_back)
 
     def attn_back_t(t):
-        do = mm(da_out[...], block_mat(w_a, t)).astype(BF)
+        do = mm(da_out[...], mat_of(ga, t, 0)).astype(BF)
         q3 = qkv[t, mine, :]
         kv = qkv[t]
         dqs, dks, dvs = [], [], []
@@ -433,188 +612,6 @@
         d.wait()
 
 
-def k1(gath, meta, group, head):
-    n_t, n_fc, rows, width = gath.shape
-    wl = (rows - 16) // 3
-    n_n = group.shape[1]
-    s_n, r_n = n_n // 2, n_n // 4
-    hw = width // 4
-    heads = width // head
-    v = pltpu.VMEM
-    sds = jax.ShapeDtypeStruct
-    vm = pl.BlockSpec(memory_space=pltpu.VMEM)
-    any_ = pl.BlockSpec(memory_space=pl.ANY)
-    wshape = (n_t, n_fc, wl, width)
-    return pl.pallas_call(
-        functools.partial(k1_kernel, head),
-        out_shape=(sds((n_t, n_fc, 2 * wl, width), BF), sds((n_t, r_n, hw), BF), sds((n_t, s_n, 2 * hw), BF), sds((r_n, width), BF),
-                   sds((r_n, width), BF), sds((n_t, r_n, width), BF), sds((r_n, width), F32), sds((r_n, width), BF),
-                   sds((16, 8, width), F32)),
-        in_specs=[any_, vm, vm],
-        out_specs=(any_,) + (vm,) * 8,
-        scratch_shapes=[
-            v(wshape, BF), v(wshape, BF), v(wshape, BF), v((n_t, n_fc, 16, width), BF),
-            v((s_n, width), BF), v((r_n, width), F32), v((n_t, s_n, width), BF), v((heads, r_n, s_n), F32),
-            v((r_n, s_n), F32), v((r_n, s_n), BF), v((r_n, s_n), BF), v((r_n, width), F32), v((r_n, width), F32), v((r_n, width), BF),
-            v((r_n, width), F32), v((r_n, 128), F32), v((n_t, r_n, width), F32), v((n_t, r_n, width), BF),
-            v((r_n, width), BF), v((r_n, width), BF), v((r_n, width), F32), v((n_t, 16, width), F32),
-            v(wshape, BF), v(wshape, BF), pltpu.SemaphoreType.DMA((6,))],
-        compiler_params=pltpu.CompilerParams(vmem_limit_bytes=VMEM_MAX),
-        name="layer_main",
-    )(gath, meta, group)
-
-
-def comm_in_kernel(cut, tok, cot, pack, meta, gath, group, meta_all, held, *sems):
-    (sem_l, s_e, r_e, s_xg, r_xg, s_xf, s_z, r_z, s_x0, r_x0, s_y0, r_y0, s_y1, r_y1, s_x1, r_x1,
-     s_c, r_c, s_c0, r_c0, s_c1, r_c1, s_m, r_m) = sems
-    f, c, t = lax.axis_index("fsdp"), lax.axis_index("ctx"), lax.axis_index("tp")
-    rows = pack.shape[0]
-    h0, h1 = pl.ds(0, cut), pl.ds(cut, rows - cut)
-    slot = f * 4 + c
-    partner = (1 - f, c, t)
-    cx = c + 1 - 2 * (c % 2)
-    cy = (c + 2) % 4
-    cd = (cx + 2) % 4
-    x_nb, y_nb = (f, cx, t), (f, cy, t)
-    near, far = 1 + f, 3 * f
-    is_near, is_far = t == near, t == far
-    receiver = (t // 2) == f
-
-    barrier = pltpu.get_barrier_semaphore()
-    peers = [partner] + [(f, (c + i) % 4, t) for i in (1, 2, 3)] + [(f, c, (t + i) % 4) for i in (1, 2, 3)]
-    for p in peers:
-        pl.semaphore_signal(barrier, inc=1, device_id=p, device_id_type=MESH)
-    pl.semaphore_wait(barrier, len(peers))
-
-    pending = []
-
-    def send(src, dst, ssem, rsem, dev, pred=None):
-        d = pltpu.make_async_remote_copy(src_ref=src, dst_ref=dst, send_sem=ssem, recv_sem=rsem,
-                                         device_id=dev, device_id_type=MESH)
-        if pred is None:
-            d.start()
-        else:
-            pl.when(pred)(d.start)
-        pending.append((pred, d))
-
-    def arrived(dst, rsem, pred=None):
-        d = pltpu.make_async_remote_copy(src_ref=dst, dst_ref=dst, send_sem=s_e.at[0, 0], recv_sem=rsem,
-                                         device_id=partner, device_id_type=MESH)
-        if pred is None:
-            d.wait_recv()
-        else:
-            pl.when(pred)(d.wait_recv)
-
-    def both(a, b):
-        return b if a is None else jnp.logical_and(a, b)
-
-    def first_sends(ten, ref):
-        for i in (1, 2, 3):
-            to = (c + i) % 4
-            send(ref.at[to], held.at[ten, c], s_e.at[ten, i], r_e.at[ten, c], (f, to, t))
-
-    first_sends(0, tok)
-    local = [pltpu.make_async_copy(tok.at[c], held.at[0, c], sem_l.at[0]),
-             pltpu.make_async_copy(cot.at[c], held.at[1, c], sem_l.at[1]),
-             pltpu.make_async_copy(pack, gath.at[t, slot], sem_l.at[2])]
-    for d in local:
-        d.start()
-    send(meta, meta_all.at[f], s_m.at[0], r_m.at[0], partner)
-    own_meta = pltpu.make_async_copy(meta, meta_all.at[f], sem_l.at[5])
-    own_meta.start()
-
-    def have_column(src, tt, pred=None):
-        send(src.at[h0], gath.at[tt, slot, h0], s_x0.at[tt], r_x0.at[tt], x_nb, pred)
-        send(src.at[h1], gath.at[tt, slot, h1], s_y1.at[tt], r_y1.at[tt], y_nb, pred)
-        send(src.at[h0], gath.at[tt, slot, h0], s_y0.at[0, tt], r_y0.at[0, tt], y_nb, pred)
-        send(src.at[h1], gath.at[tt, slot, h1], s_x1.at[0, tt], r_x1.at[0, tt], x_nb, pred)
-        send(src, gath.at[tt, slot], s_c.at[tt], r_c.at[tt], partner, pred)
-
-    send(pack, gath.at[t, slot], s_z.at[0, t], r_z.at[t], (f, c, (t + 1) % 4), t < 3)
-    send(pack, gath.at[t, slot], s_z.at[1, t], r_z.at[t], (f, c, (t + 3) % 4), t > 0)
-    have_column(pack, t)
-    first_sends(1, cot)
-
-    def second_sends(ten):
-        local[ten].wait()
-        for i in (1, 2, 3):
-            frm = (c + i) % 4
-            arrived(held.at[ten, frm], r_e.at[ten, frm])
-        blk = held.at[ten]
-        dst = group.at[ten, :, t]
-        to = jnp.where(is_near, far, near)
-        send(blk, dst, s_xg.at[ten, t], r_xg.at[ten, t], (f, c, to))
-        send(blk, dst, s_xf.at[ten, 0, t], r_xg.at[ten, t], partner, receiver)
-        keep = pltpu.make_async_copy(blk, dst, sem_l.at[3 + ten])
-        pl.when(receiver)(keep.start)
-        return keep
-
-    keeps = [second_sends(0)]
-
-    def z_step(d):
-        for sign in (-1, 1):
-            tt = t + sign * d
-            there = tt >= 0 if sign < 0 else tt <= 3
-            tt = (tt + 4) % 4
-            arrived(gath.at[tt, slot], r_z.at[tt], there)
-            on = t < 3 if sign < 0 else t > 0
-            nxt = (t + 1) % 4 if sign < 0 else (t + 3) % 4
-            if d < 3:
-                send(gath.at[tt, slot], gath.at[tt, slot], s_z.at[(1 - sign) // 2 * 0 + (0 if sign < 0 else 1), tt],
-                     r_z.at[tt], (f, c, nxt), both(there, on))
-            have_column(gath.at[tt, slot], tt, there)
-
-    def relay(ten):
-        for i in (1, 2, 3):
-            tt = (t + i) % 4
-            arrived(group.at[ten, :, tt], r_xg.at[ten, tt], receiver)
-            send(group.at[ten, :, tt], group.at[ten, :, tt], s_xg.at[ten, tt], r_xg.at[ten, tt], (f, c, far),
-                 jnp.logical_and(is_near, tt != far))
-            send(group.at[ten, :, tt], group.at[ten, :, tt], s_xf.at[ten, 0, tt], r_xg.at[ten, tt], partner, receiver)
-
-    z_step(1)
-    relay(0)
-    keeps.append(second_sends(1))
-    z_step(2)
-    z_step(3)
-    relay(1)
-
-    columns = [(t, None)]
-    for d in (1, 2, 3):
-        columns.append(((t - d + 4) % 4, t - d >= 0))
-        columns.append(((t + d) % 4, t + d <= 3))
-    for tt, pred in columns:
-        a = gath.at[tt, f * 4 + cx, h0]
-        arrived(a, r_x0.at[tt], pred)
-        send(a, a, s_y0.at[1, tt], r_y0.at[1, tt], y_nb, pred)
-        send(a, a, s_c0.at[0, tt], r_c0.at[0, tt], partner, pred)
-        b = gath.at[tt, f * 4 + cy, h1]
-        arrived(b, r_y1.at[tt], pred)
-        send(b, b, s_x1.at[1, tt], r_x1.at[1, tt], x_nb, pred)
-        send(b, b, s_c1.at[0, tt], r_c1.at[0, tt], partner, pred)
-    for step in (0, 1):
-        for tt, pred in columns:
-            a = gath.at[tt, f * 4 + (cy if step == 0 else cd), h0]
-            arrived(a, r_y0.at[step, tt], pred)
-            send(a, a, s_c0.at[1 + step, tt], r_c0.at[1 + step, tt], partner, pred)
-            b = gath.at[tt, f * 4 + (cx if step == 0 else cd), h1]
-            arrived(b, r_x1.at[step, tt], pred)
-            send(b, b, s_c1.at[1 + step, tt], r_c1.at[1 + step, tt], partner, pred)
-
-    other = (1 - f) * 4
-    for tt in range(4):
-        arrived(gath.at[tt, other + c], r_c.at[tt])
-        for j, cc in enumerate((cx, cy, cd)):
-            arrived(gath.at[tt, other + cc, h0], r_c0.at[j, tt])
-        for j, cc in enumerate((cy, cx, cd)):
-            arrived(gath.at[tt, other + cc, h1], r_c1.at[j, tt])
-    for ten in (0, 1):
-        for tt in range(4):
-            arrived(group.at[ten, :, tt], r_xg.at[ten, tt], jnp.logical_not(receiver))
-        pl.when(receiver)(keeps[ten].wait)
-    arrived(meta_all.at[1 - f], r_m.at[0])
-    own_meta.wait()
-    local[2].wait()
     for pred, d in pending:
         if pred is None:
             d.wait_send()
@@ -622,35 +619,51 @@
             pl.when(pred)(d.wait_send)
 
 
-def comm_in(tok, cot, pack, meta, cut):
+def main_in(tok, cot, pack, meta, head):
+    own, width = tok.shape[1:]
+    wl = (pack.shape[0] - 16) // 3
+    n_n = own * 16
+    s_n, r_n = n_n // 2, n_n // 4
+    hw = width // 4
+    heads = width // head
+    v = pltpu.VMEM
     dma = pltpu.SemaphoreType.DMA
-    rows, width = pack.shape
-    own = tok.shape[1]
-    sems = [dma((6,)), dma((2, 4)), dma((2, 4)), dma((2, 4)), dma((2, 4)), dma((2, 1, 4)), dma((2, 4)), dma((4,)),
-            dma((4,)), dma((4,)), dma((2, 4)), dma((2, 4)), dma((4,)), dma((4,)), dma((2, 4)), dma((2, 4)),
-            dma((4,)), dma((4,)), dma((3, 4)), dma((3, 4)), dma((3, 4)), dma((3, 4)), dma((1,)), dma((1,))]
+    sds = jax.ShapeDtypeStruct
+    vm = pl.BlockSpec(memory_space=pltpu.VMEM)
     any_ = pl.BlockSpec(memory_space=pl.ANY)
+    wshape = (4, 8, wl, width)
+    pass_sems = [dma((2, 4)), dma((4,)), dma((4,)), dma((4,)), dma((2, 4)), dma((2, 4)), dma((4,)), dma((4,)),
+                 dma((2, 4)), dma((2, 4)), dma((4,)), dma((4,)), dma((3, 4)), dma((3, 4)), dma((3, 4)), dma((3, 4))]
     return pl.pallas_call(
-        functools.partial(comm_in_kernel, cut),
-        out_shape=(jax.ShapeDtypeStruct((4, 8, rows, width), BF),
-                   jax.ShapeDtypeStruct((2, 4, 4, own, width), BF), jax.ShapeDtypeStruct((2,) + meta.shape, jnp.int32)),
-        in_specs=[any_, any_, pl.BlockSpec(memory_space=pltpu.VMEM), pl.BlockSpec(memory_space=pltpu.VMEM)],
-        out_specs=(any_, any_, any_),
-        scratch_shapes=[pltpu.VMEM((2, 4, own, width), BF)] + sems,
-        compiler_params=pltpu.CompilerParams(collective_id=0, has_side_effects=True),
-        name="comm_in",
+        functools.partial(main_in_kernel, head),
+        out_shape=(sds((4, 8, wl + 16, width), BF), sds((4, 8, 2 * wl, width), BF), sds((2,) + meta.shape, jnp.int32),
+                   sds((4, r_n, hw), BF), sds((4, s_n, 2 * hw), BF), sds((r_n, width), BF), sds((r_n, width), BF),
+                   sds((4, r_n, width), BF), sds((r_n, width), F32), sds((r_n, width), BF), sds((16, 8, width), F32)),
+        in_specs=[any_, any_, vm, vm],
+        out_specs=(vm, any_) + (vm,) * 9,
+        scratch_shapes=[
+            v((4, 8, 2 * wl, width), BF), v((2, 4, 4, own, width), BF), v((2, 4, own, width), BF),
+            v((s_n, width), BF), v((r_n, width), F32), v((4, s_n, width), BF), v((heads, r_n, s_n), F32),
+            v((r_n, s_n), F32), v((r_n, s_n), BF), v((r_n, s_n), BF), v((r_n, width), F32), v((r_n, width), BF),
+            v((r_n, width), F32), v((r_n, 128), F32), v((4, r_n, width), F32), v((4, r_n, width), BF),
+            v((r_n, width), BF), v((r_n, width), BF), v((r_n, width), F32), v((4, 16, width), F32),
+            v(wshape, BF), v(wshape, BF),
+            dma((9,)), dma((2, 4)), dma((2, 4)), dma((2, 4)), dma((2, 4)), dma((2, 4)), dma((1,)), dma((1,))]
+        + pass_sems + pass_sems,
+        compiler_params=pltpu.CompilerParams(collective_id=0, has_side_effects=True, vmem_limit_bytes=VMEM_MAX),
+        name="main_in",
     )(tok, cot, pack, meta)
 
 
-def tail_out_kernel(gath, meta_ref, dq, dkv, xm, da, op, dr1, y, vec, gg, tot_a, tot_w, rows_out,
-                    w_a, g_a, acc, dqkv, dkv_in, place, pl1, pl2, own, w0, w1, w2, w3, a0, a1, a2, a3,
+def tail_out_kernel(w_a, meta_ref, dq, dkv, xm, da, op, dr1, y, vec, gg, tot_a, tot_w, rows_out,
+                    g_a, acc, dqkv, dkv_in, place, pl1, pl2, own, w0, w1, w2, w3, a0, a1, a2, a3,
                     sem_l, s_d, r_d, s_u, r_u, s_o, r_o,
                     ws0, wr0, ws1, wr1, ws2, wr2, ws3, wr3, as0, ar0, as1, ar1, as2, ar2, as3, ar3):
     f, c, t = lax.axis_index("fsdp"), lax.axis_index("ctx"), lax.axis_index("tp")
     r_n, width = xm.shape
     n_n = 4 * r_n
     hw = width // 4
-    wl = w_a.shape[2]
+    wl = w_a.shape[2] - 16
     partner = (1 - f, c, t)
     cx = c + 1 - 2 * (c % 2)
     cy = (c + 2) % 4
@@ -661,8 +674,6 @@
     to_f, to_t = t // 2, 2 * f + par
     stays = to_f == f
 
-    load_a = pltpu.make_async_copy(gath.at[:, :, pl.ds(0, wl)], w_a, sem_l.at[0])
-    load_a.start()
     turn = [(t + 2) % 4, (t + 1) % 4, (t + 3) % 4, t]
     loads = []
     for i, tt in enumerate(turn):
@@ -811,7 +822,7 @@
         both = (dkv[k, mine_rows, :].astype(F32) + dkv_in[k].astype(F32)).astype(BF)
         dqkv[...] = jnp.concatenate([jnp.zeros((r_n, hw), BF), dq[k], both], axis=1)
         d = dqkv[...]
-        acc[...] += mm_rt(d, block_mat(w_a, k))
+        acc[...] += mm_rt(d, w_a[k, :, 0:wl, :].reshape(w_a.shape[1] * wl, width))
         g_a[k, :, 0:wl, :] = (mm_lt(xm[...], d) + mm_lt(da[...], op[k])).astype(BF).reshape(g_a.shape[1], wl, width)
         sums = jnp.sum(vec[...], axis=1)
         base = jnp.where(lane16 < 6, sums, 0.0)
@@ -841,7 +852,6 @@
     loads[1].wait()
     wp[1](1)
     arrived(dkv_in, r_d)
-    load_a.wait()
     two(0)
     rows2(0)
     wp[2](0)
@@ -901,7 +911,7 @@
 
 def tail_out(gath, meta, dq, dkv, xm, da, op, dr1, y, vec, gg):
     n_t, n_fc, rows, width = gath.shape
-    wl = (rows - 16) // 3
+    wl = rows - 16
     r_n = xm.shape[0]
     block = r_n // 4
     v = pltpu.VMEM
@@ -916,9 +926,9 @@
         tail_out_kernel,
         out_shape=(jax.ShapeDtypeStruct((ra, width), F32), jax.ShapeDtypeStruct((rw, width), F32),
                    jax.ShapeDtypeStruct((2, 4, block, width), BF)),
-        in_specs=[any_] + [vm] * 9 + [any_],
+        in_specs=[vm] * 10 + [any_],
         out_specs=(vm, vm, vm),
-        scratch_shapes=[v((n_t, n_fc, wl, width), BF), v((n_t, n_fc, ra, width), BF), v((r_n, width), F32),
+        scratch_shapes=[v((n_t, n_fc, ra, width), BF), v((r_n, width), F32),
                         v((r_n, width), BF), v((n_t, r_n, dkv.shape[2]), BF), v((2, 4, 4, block, width), BF),
                         v((2, 2, 4, block, width), BF), v((2, 4, block, width), BF), v((4, 4, rw, width), BF)]
         + bufs(rw) + bufs(ra)
@@ -948,7 +958,7 @@
     row_a = jnp.where(part, jnp.tile(three, (1, 1, 8)).reshape(1, width), 0)
     row_u = jnp.where((col % (8 * up_l)) // up_l == fc, jnp.tile(b_up, (1, 8)).reshape(1, width), 0)
     small = jnp.concatenate([row_v, row_a, row_u, jnp.zeros((8, width), BF)], axis=0)
-    pack = jnp.concatenate([mat_a, w_up, w_down, small], axis=0)
+    pack = jnp.concatenate([mat_a, small, w_up, w_down], axis=0)
 
     order = row_order[:, 0]
     n_n = order.shape[1]
@@ -956,11 +966,8 @@
     lens = jnp.pad(seq_lengths[:, 0].reshape(1, -1), ((0, 3), (0, n_n - 12)))
     meta_own = jnp.concatenate([order, lens, moved, jnp.zeros((4, n_n), jnp.int32)], axis=0)
 
-    cut = (pack.shape[0] // 32) * 16
-    gath, group, meta = comm_in(tokens_in, cotangent, pack, meta_own, cut)
-    group = group.reshape(2, n_n, width)
-    gg, dq, dkv, xm, da, op, dr1, y, vec = k1(gath, meta, group, head)
-    tot_a, tot_w, rows = tail_out(gath, meta, dq, dkv, xm, da, op, dr1, y, vec, gg)
+    ga, gg, meta, dq, dkv, xm, da, op, dr1, y, vec = main_in(tokens_in, cotangent, pack, meta_own, head)
+    tot_a, tot_w, rows = tail_out(ga, meta, dq, dkv, xm, da, op, dr1, y, vec, gg)
 
     g_a, g_up, g_down = tot_a[:wl], tot_w[:wl], tot_w[wl:]
     sv = lax.dynamic_slice(tot_a[wl:wl + 6], (0, fc * wl), (6, wl))

time: 258 us -> 252 us (0.977)
  Pallas kernels: 235 us -> 229 us
    pallas_call x2 -> x1, Pallas kernels: 132 us -> 126 us  [main_in(): pl.pallas_call(functools.partial(main_in_kernel, head), out_shape=(sds((4...]
where the time goes in v5:
time: 252 us; the launch traced here: 251 us
  Pallas kernels  229 us (91%)
  local copies, waits for them, and re-layouts  18 us (7%)
  other arithmetic  3.21 us (1%)
    pallas_call x1, Pallas kernels, main_in(): pl.pallas_call(functools.partial(main_in_kernel, head), out_shape=(sds((4...  126 us
    pallas_call x1, Pallas kernels, tail_out(): pl.pallas_call(tail_out_kernel, out_shape=(jax.ShapeDtypeStruct((ra, widt...  103 us

profile of v5, /device:TPU:0, one launch (start us, length us, event | category | flops | bytes accessed | tf_op | source)
XLA Modules:
  0.0 251.3 jit_solution(13272483354795475300)
XLA Ops:
  0.7 0.7 pad_maximum_fusion.1
  1.4 0.1 tile.28
  1.5 0.7 tile.29
  2.2 0.1 tile.30
  2.3 0.8 stack.36
  3.1 0.1 tile.26
  3.2 1.0 pad_maximum_fusion
  4.2 5.0 %concatenate.10.pack = bf16[304,768]{1,0:T(8,128)(2,1)} concatenate(bf16[96,768]{1,0:T(8,128)(2,1)S(1)} %pad_maximum_fusion, bf16[6,768]{1,0:T(8,128)(2,1)S(1)} %broadcast_select_fusion, bf16[1,768]{1,0:T(2,128)(2,1)S(1)} %get-tuple-element.64, bf16[1,768]{1,0:T(2,128)(2,1)S(1)} %get-tuple-element.63, bf16[8,768]{1,0:T(8,128)(2,1)S(1)} %broadcast_in_dim.26, ...), dimensions={0} | concatenate | bytes 933888 | tf_op jit(solution)/shard_map/concatenate | solution.py:961
  9.2 0.8 reduce
  10.0 0.1 reshape_squeeze.13
  10.1 0.1 reshape.292
  10.2 0.7 copy.44
  10.9 0.8 copy.38
  11.7 0.1 reshape_squeeze.12
  11.8 0.1 pad.8.clone
  11.8 0.7 fusion.1.meta
  12.5 125.9 %main_in.1 = (bf16[4,8,112,768]{3,2,1,0:T(8,128)(2,1)}, bf16[4,8,192,768]{3,2,1,0:T(8,128)(2,1)}, s32[2,16,1024]{2,1,0:T(8,128)}, bf16[4,256,192]{2,1,0:T(8,128)...) custom-call(bf16[4,64,768]{2,1,0:T(8,128)(2,1)} %tok.1, ...), custom_call_target="tpu_custom_call" | custom-call | tf_op jit(solution)/shard_map/main_in/pallas_call | solution.py:637
  138.5 103.5 %tail_out.1 = (f32[112,768]{1,0:T(8,128)}, f32[192,768]{1,0:T(8,128)}, bf16[2,4,64,768]{3,2,1,0:T(8,128)(2,1)}) custom-call(bf16[4,8,112,768]{3,2,1,0:T(8,128)(2,1)} %get-tuple-element.31.w_a, s32[2,16,1024]{2,1,0:T(8,128)} %get-tuple-element.32.meta_ref, bf16[4,256,192]{2,1,0:T(8,128)(2,1)} %get-tuple-element.33.dq, ...), custom_call_target="tpu_custom_call" | custom-call | tf_op jit(solution)/shard_map/tail_out/pallas_call | solution.py:925
  241.9 2.0 slice_bitcast_fusion
  244.0 1.9 fusion.6
  245.9 1.9 fusion.7
  247.8 0.7 slice.71
  248.5 0.1 constant_dynamic-slice_fusion.1
  248.6 0.5 slice_bitcast_fusion.2
  249.1 0.8 slice_reduce_fusion
  249.9 0.1 reshape_squeeze.14
  250.0 0.7 dynamic-slice_bitcast_fusion
  250.7 0.6 constant_dynamic-slice_fusion
  (10 shorter events, 0.1 us)

commit v6 on v5

--- a/solution.py
+++ b/solution.py
@@ -253,7 +253,7 @@
     lax.fori_loop(0, 4, step, 0)
 
 
-def main_in_kernel(head, tok, cot, pack, meta, ga, gg, meta_all, dq_out, dkv_out, xm_out, da_out, op_out, dr1_out, y_out, vec_out,
+def main_in_kernel(head, tok, cot, pack, meta, up, down, ga, gg, meta_all, dq_out, dkv_out, xm_out, da_out, op_out, dr1_out, y_out, vec_out,
                    gu, group, held, xh, dy, qkv, probs, sbuf, pb, pb2, acc, midb, n1, inv1, gelu_d, act, n2, df, big, bias,
                    g_u, g_d, sem_l, s_e, r_e, s_xg, r_xg, s_xf, s_m, r_m, *pass_sems):
     f, c, t_me = lax.axis_index("fsdp"), lax.axis_index("ctx"), lax.axis_index("tp")
@@ -305,14 +305,15 @@
 
     a_rows = ga.shape[2]
     w_rows = gu.shape[2]
-    own_a, own_w = pack.at[pl.ds(0, a_rows)], pack.at[pl.ds(a_rows, w_rows)]
+    own_a, own_w = pack, gu.at[t_me, slot]
+    shards = [pltpu.make_async_copy(up, gu.at[t_me, slot, pl.ds(0, wl)], sem_l.at[3]),
+              pltpu.make_async_copy(down, gu.at[t_me, slot, pl.ds(wl, wl)], sem_l.at[9])]
     first_sends(0, tok)
     local = [pltpu.make_async_copy(tok.at[c], held.at[0, c], sem_l.at[0]),
              pltpu.make_async_copy(cot.at[c], held.at[1, c], sem_l.at[1]),
              pltpu.make_async_copy(own_a, ga.at[t_me, slot], sem_l.at[2]),
-             pltpu.make_async_copy(own_w, gu.at[t_me, slot], sem_l.at[3]),
              pltpu.make_async_copy(meta, meta_all.at[f], sem_l.at[8])]
-    for d in local:
+    for d in local + shards:
         d.start()
     send(meta, meta_all.at[f], s_m.at[0], r_m.at[0], partner)
 
@@ -418,21 +419,27 @@
     a_begin()
     keep0 = second_sends(0)
     a_z(1)
+    for d in shards:
+        d.wait()
+    w_begin()
     relay(0)
     a_z(2)
+    first_sends(1, cot)
     a_z(3)
+    for i in range(5):
+        a_mid(i)
+    w_z(1)
+    for i in range(5, 7):
+        a_mid(i)
     for i in range(7):
-        a_mid(i)
-    first_sends(1, cot)
-    w_begin()
-    for step in (0, 1):
-        for i in range(7):
-            a_late(step, i)
-    w_z(1)
+        a_late(0, i)
+    w_z(2)
+    for i in range(7):
+        a_late(1, i)
     keep1 = second_sends(1)
     rows_here(0, keep0)
     arrived(meta_all.at[1 - f], r_m.at[0])
-    local[4].wait()
+    local[3].wait()
 
     meta = meta_all[t_me // 2]
     start, e0, e1 = row_facts(meta, n_n)
@@ -481,7 +488,6 @@
             return 0
         lax.fori_loop(first, first + 2, step, 0)
 
-    w_z(2)
     relay(1)
     two(0, forward_t)
     w_z(3)
@@ -526,7 +532,6 @@
     for i in range(7):
         w_late(1, i)
     w_finish()
-    local[3].wait()
 
     def ffn_t(t):
         row7 = bias[t][7:8, :]
@@ -619,9 +624,9 @@
             pl.when(pred)(d.wait_send)
 
 
-def main_in(tok, cot, pack, meta, head):
+def main_in(tok, cot, pack, meta, up, down, head):
     own, width = tok.shape[1:]
-    wl = (pack.shape[0] - 16) // 3
+    wl = up.shape[0]
     n_n = own * 16
     s_n, r_n = n_n // 2, n_n // 4
     hw = width // 4
@@ -639,7 +644,7 @@
         out_shape=(sds((4, 8, wl + 16, width), BF), sds((4, 8, 2 * wl, width), BF), sds((2,) + meta.shape, jnp.int32),
                    sds((4, r_n, hw), BF), sds((4, s_n, 2 * hw), BF), sds((r_n, width), BF), sds((r_n, width), BF),
                    sds((4, r_n, width), BF), sds((r_n, width), F32), sds((r_n, width), BF), sds((16, 8, width), F32)),
-        in_specs=[any_, any_, vm, vm],
+        in_specs=[any_, any_, vm, vm, any_, any_],
         out_specs=(vm, any_) + (vm,) * 9,
         scratch_shapes=[
             v((4, 8, 2 * wl, width), BF), v((2, 4, 4, own, width), BF), v((2, 4, own, width), BF),
@@ -648,11 +653,11 @@
             v((r_n, width), F32), v((r_n, 128), F32), v((4, r_n, width), F32), v((4, r_n, width), BF),
             v((r_n, width), BF), v((r_n, width), BF), v((r_n, width), F32), v((4, 16, width), F32),
             v(wshape, BF), v(wshape, BF),
-            dma((9,)), dma((2, 4)), dma((2, 4)), dma((2, 4)), dma((2, 4)), dma((2, 4)), dma((1,)), dma((1,))]
+            dma((10,)), dma((2, 4)), dma((2, 4)), dma((2, 4)), dma((2, 4)), dma((2, 4)), dma((1,)), dma((1,))]
         + pass_sems + pass_sems,
         compiler_params=pltpu.CompilerParams(collective_id=0, has_side_effects=True, vmem_limit_bytes=VMEM_MAX),
         name="main_in",
-    )(tok, cot, pack, meta)
+    )(tok, cot, pack, meta, up, down)
 
 
 def tail_out_kernel(w_a, meta_ref, dq, dkv, xm, da, op, dr1, y, vec, gg, tot_a, tot_w, rows_out,
@@ -958,7 +963,7 @@
     row_a = jnp.where(part, jnp.tile(three, (1, 1, 8)).reshape(1, width), 0)
     row_u = jnp.where((col % (8 * up_l)) // up_l == fc, jnp.tile(b_up, (1, 8)).reshape(1, width), 0)
     small = jnp.concatenate([row_v, row_a, row_u, jnp.zeros((8, width), BF)], axis=0)
-    pack = jnp.concatenate([mat_a, small, w_up, w_down], axis=0)
+    pack = jnp.concatenate([mat_a, small], axis=0)
 
     order = row_order[:, 0]
     n_n = order.shape[1]
@@ -966,7 +971,7 @@
     lens = jnp.pad(seq_lengths[:, 0].reshape(1, -1), ((0, 3), (0, n_n - 12)))
     meta_own = jnp.concatenate([order, lens, moved, jnp.zeros((4, n_n), jnp.int32)], axis=0)
 
-    ga, gg, meta, dq, dkv, xm, da, op, dr1, y, vec = main_in(tokens_in, cotangent, pack, meta_own, head)
+    ga, gg, meta, dq, dkv, xm, da, op, dr1, y, vec = main_in(tokens_in, cotangent, pack, meta_own, w_up, w_down, head)
     tot_a, tot_w, rows = tail_out(ga, meta, dq, dkv, xm, da, op, dr1, y, vec, gg)
 
     g_a, g_up, g_down = tot_a[:wl], tot_w[:wl], tot_w[wl:]

time: 252 us -> 243 us (0.964)
  Pallas kernels: 229 us -> 223 us
  local copies, waits for them, and re-layouts: 18 us -> 14.9 us
    pallas_call x1, Pallas kernels: 126 us -> 117 us  [main_in(): pl.pallas_call(functools.partial(main_in_kernel, head), out_shape=(sds((4...]
    concatenate x1, local copies, waits for them, and re-layouts: 5.02 us -> 1.92 us  [quad_body(): pack = jnp.concatenate([mat_a, small], axis=0)]
    pallas_call x1, Pallas kernels: 103 us -> 106 us  [tail_out(): pl.pallas_call(tail_out_kernel, out_shape=(jax.ShapeDtypeStruct((ra, widt...]
where the time goes in v6:
time: 243 us; the launch traced here: 242 us
  Pallas kernels  223 us (92%)
  local copies, waits for them, and re-layouts  14.9 us (6%)
  other arithmetic  3.21 us (1%)
    pallas_call x1, Pallas kernels, main_in(): pl.pallas_call(functools.partial(main_in_kernel, head), out_shape=(sds((4...  117 us
    pallas_call x1, Pallas kernels, tail_out(): pl.pallas_call(tail_out_kernel, out_shape=(jax.ShapeDtypeStruct((ra, widt...  106 us

profile of v6, /device:TPU:0, one launch (start us, length us, event | category | flops | bytes accessed | tf_op | source)
XLA Modules:
  0.0 242.2 jit_solution(11244571904252167745)
XLA Ops:
  0.7 0.7 pad_maximum_fusion.1
  1.4 0.1 tile.28
  1.5 0.7 tile.29
  2.2 0.1 tile.30
  2.3 0.8 stack.36
  3.1 0.1 tile.26
  3.2 1.0 pad_maximum_fusion
  4.2 1.9 concatenate.10.pack
  6.1 0.8 reduce
  6.9 0.1 reshape_squeeze.13
  7.0 0.1 reshape.292
  7.1 0.7 copy.44
  7.8 0.8 copy.38
  8.6 0.1 reshape_squeeze.12
  8.7 0.1 pad.8.clone
  8.7 0.7 fusion.1.meta
  9.4 116.9 %main_in.1 = (bf16[4,8,112,768]{3,2,1,0:T(8,128)(2,1)}, bf16[4,8,192,768]{3,2,1,0:T(8,128)(2,1)}, s32[2,16,1024]{2,1,0:T(8,128)}, bf16[4,256,192]{2,1,0:T(8,128)...) custom-call(bf16[4,64,768]{2,1,0:T(8,128)(2,1)} %tok.1, ...), custom_call_target="tpu_custom_call" | custom-call | tf_op jit(solution)/shard_map/main_in/pallas_call | solution.py:642
  126.4 106.4 %tail_out.1 = (f32[112,768]{1,0:T(8,128)}, f32[192,768]{1,0:T(8,128)}, bf16[2,4,64,768]{3,2,1,0:T(8,128)(2,1)}) custom-call(bf16[4,8,112,768]{3,2,1,0:T(8,128)(2,1)} %get-tuple-element.31.w_a, s32[2,16,1024]{2,1,0:T(8,128)} %get-tuple-element.32.meta_ref, bf16[4,256,192]{2,1,0:T(8,128)(2,1)} %get-tuple-element.33.dq, ...), custom_call_target="tpu_custom_call" | custom-call | tf_op jit(solution)/shard_map/tail_out/pallas_call | solution.py:930
  232.8 2.0 slice_bitcast_fusion
  234.8 1.9 fusion.6
  236.7 1.9 fusion.7
  238.6 0.7 slice.71
  239.3 0.1 constant_dynamic-slice_fusion.1
  239.4 0.5 slice_bitcast_fusion.2
  240.0 0.8 slice_reduce_fusion
  240.8 0.1 reshape_squeeze.14
  240.9 0.7 dynamic-slice_bitcast_fusion
  241.5 0.6 constant_dynamic-slice_fusion
  (10 shorter events, 0.1 us)

commit v7 on v6

--- a/solution.py
+++ b/solution.py
@@ -845,56 +845,56 @@
     send(dkv.at[:, pl.ds(pl.multiple_of((1 - f) * n_d, n_d), n_d)], dkv_in, s_d, r_d, partner)
     wp[0](0)
     wp[0](1)
-    order = pick_row(meta[8:12, :], c)
-    pick = (order == nat).astype(F32).astype(BF)
-    place[0] = mm_lt(pick, y[...]).astype(BF).reshape(place.shape[1:])
-    acc[...] = dr1[...]
     wp[0](2)
-    rows1(0)
     wp[0](3)
     loads[0].wait()
     wp[1](0)
     loads[1].wait()
     wp[1](1)
+    order = pick_row(meta[8:12, :], c)
+    pick = (order == nat).astype(F32).astype(BF)
+    place[0] = mm_lt(pick, y[...]).astype(BF).reshape(place.shape[1:])
+    acc[...] = dr1[...]
+    rows1(0)
     arrived(dkv_in, r_d)
     two(0)
-    rows2(0)
     wp[2](0)
     loads[2].wait()
     wp[1](2)
     two(2)
+    for i in range(4):
+        ap[0](i)
+    rows2(0)
     wp[2](1)
     wp[3](0)
     loads[3].wait()
     wp[1](3)
-    rows3(0)
-    for i in range(4):
-        ap[0](i)
     lane = lax.broadcasted_iota(jnp.int32, (1, n_n), 1)
     at = ((lane // block) % 4) * (4 * block) + (lane // (4 * block)) * block + lane % block
     pick2 = (at == nat).astype(F32).astype(BF)
     place[1] = mm_lt(pick2, acc[...].astype(BF)).astype(BF).reshape(place.shape[1:])
+    rows1(1)
+    rows3(0)
     wp[2](2)
+    ap[1](0)
     wp[3](1)
-    rows1(1)
-    ap[1](0)
     wp[2](3)
+    ap[1](1)
     wp[3](2)
     rows2(1)
-    ap[1](1)
+    ap[1](2)
     ap[2](0)
+    ap[1](3)
     wp[3](3)
     rows3(1)
-    ap[1](2)
     ap[2](1)
     ap[3](0)
-    ap[1](3)
-    wp[4](tot_w, sem_l.at[7])
     ap[2](2)
     ap[3](1)
     ap[2](3)
     ap[3](2)
     ap[3](3)
+    wp[4](tot_w, sem_l.at[7])
     ap[4](tot_a, sem_l.at[8])
 
     for ten in range(2):

time: 243 us -> 237 us (0.975)
  Pallas kernels: 223 us -> 218 us
    pallas_call x1, Pallas kernels: 106 us -> 101 us  [tail_out(): pl.pallas_call(tail_out_kernel, out_shape=(jax.ShapeDtypeStruct((ra, widt...]
where the time goes in v7:
time: 237 us; the launch traced here: 236 us
  Pallas kernels  218 us (92%)
  local copies, waits for them, and re-layouts  14.9 us (6%)
  other arithmetic  3.21 us (1%)
    pallas_call x1, Pallas kernels, main_in(): pl.pallas_call(functools.partial(main_in_kernel, head), out_shape=(sds((4...  117 us
    pallas_call x1, Pallas kernels, tail_out(): pl.pallas_call(tail_out_kernel, out_shape=(jax.ShapeDtypeStruct((ra, widt...  101 us

profile of v7, /device:TPU:0, one launch (start us, length us, event | category | flops | bytes accessed | tf_op | source)
XLA Modules:
  0.0 236.4 jit_solution(14674926798454677879)
XLA Ops:
  0.7 0.7 pad_maximum_fusion.1
  1.4 0.1 tile.28
  1.5 0.7 tile.29
  2.2 0.1 tile.30
  2.3 0.8 stack.36
  3.1 0.1 tile.26
  3.2 1.0 pad_maximum_fusion
  4.2 1.9 concatenate.10.pack
  6.1 0.8 reduce
  6.9 0.1 reshape_squeeze.13
  7.0 0.1 reshape.292
  7.1 0.7 copy.44
  7.8 0.8 copy.38
  8.6 0.1 reshape_squeeze.12
  8.7 0.1 pad.8.clone
  8.7 0.7 fusion.1.meta
  9.4 116.9 %main_in.1 = (bf16[4,8,112,768]{3,2,1,0:T(8,128)(2,1)}, bf16[4,8,192,768]{3,2,1,0:T(8,128)(2,1)}, s32[2,16,1024]{2,1,0:T(8,128)}, bf16[4,256,192]{2,1,0:T(8,128)...) custom-call(bf16[4,64,768]{2,1,0:T(8,128)(2,1)} %tok.1, ...), custom_call_target="tpu_custom_call" | custom-call | tf_op jit(solution)/shard_map/main_in/pallas_call | solution.py:642
  126.4 100.6 %tail_out.1 = (f32[112,768]{1,0:T(8,128)}, f32[192,768]{1,0:T(8,128)}, bf16[2,4,64,768]{3,2,1,0:T(8,128)(2,1)}) custom-call(bf16[4,8,112,768]{3,2,1,0:T(8,128)(2,1)} %get-tuple-element.31.w_a, s32[2,16,1024]{2,1,0:T(8,128)} %get-tuple-element.32.meta_ref, bf16[4,256,192]{2,1,0:T(8,128)(2,1)} %get-tuple-element.33.dq, ...), custom_call_target="tpu_custom_call" | custom-call | tf_op jit(solution)/shard_map/tail_out/pallas_call | solution.py:930
  227.0 2.0 slice_bitcast_fusion
  229.0 1.9 fusion.6
  230.9 1.9 fusion.7
  232.8 0.7 slice.71
  233.5 0.1 constant_dynamic-slice_fusion.1
  233.6 0.5 slice_bitcast_fusion.2
  234.2 0.8 slice_reduce_fusion
  235.0 0.1 reshape_squeeze.14
  235.1 0.7 dynamic-slice_bitcast_fusion
  235.7 0.6 constant_dynamic-slice_fusion
  (10 shorter events, 0.1 us)
